TPU v7x, 32 devices: a whole 2x2x4 slice. The times are simulated.
32 devices in a mesh: dp: 16 (over z, x, core), tensor: 2 (over y).
Axes of the slice: x: 2, y: 2, z: 4, core: 2. Of those that a mesh axis runs over, the one named last changes fastest.
Arguments:
- inputs: bfloat16 [2, 16, 1024, 768], P(None, 'dp', 'tensor'), may hold values from -6 to 6
- seg_ids: int32 [2, 16, 1024], P(None, 'dp'), may hold values from 0 to 7, never falling along the last dimension, each value on 1 to 512 neighbouring positions
- keep_mask: int32 [2, 16, 1024], P(None, 'dp'), may hold values 0 or 1
- w_qkv: bfloat16 [3, 768, 768], P(None, 'dp', 'tensor'), may hold values from -0.21875 to 0.21875
- b_qv: float32 [2, 768], replicated, may hold values from -3 to 3
- w_o: bfloat16 [768, 768], P('tensor', 'dp'), may hold values from -1.75 to 1.75
- b_o: float32 [768], replicated, may hold values from -3 to 3
- gain_one: float32 [768], replicated, may hold values from 0.5 to 1.5
- shift_one: float32 [768], replicated, may hold values from -3 to 3
- w_up: bfloat16 [768, 3072], P('dp', 'tensor'), may hold values from -0.21875 to 0.21875
- b_up: float32 [3072], replicated, may hold values from -3 to 3
- w_down: bfloat16 [3072, 768], P('tensor', 'dp'), may hold values from -0.109375 to 0.109375
- b_down: float32 [768], replicated, may hold values from -3 to 3
- gain_two: float32 [768], replicated, may hold values from 0.5 to 1.5
- shift_two: float32 [768], replicated, may hold values from -3 to 3
- out_grad: bfloat16 [2, 16, 1024, 768], P(None, 'dp', 'tensor'), may hold values from -6 to 6
Outputs:
- out: bfloat16 [2, 16, 1024, 768], P(None, 'dp', 'tensor')
- x_grad: float32 [2, 16, 1024, 768], P(None, 'dp', 'tensor')
- w_qkv_grad: float32 [3, 768, 768], P(None, 'dp', 'tensor')
- b_qv_grad: float32 [2, 768], P(None, 'tensor')
- w_o_grad: float32 [768, 768], P('tensor', 'dp')
- b_o_grad: float32 [768], replicated
- gain_one_grad: float32 [768], replicated
- shift_one_grad: float32 [768], replicated
- w_up_grad: float32 [768, 3072], P('dp', 'tensor')
- b_up_grad: float32 [3072], P('tensor')
- w_down_grad: float32 [3072, 768], P('tensor', 'dp')
- b_down_grad: float32 [768], replicated
- gain_two_grad: float32 [768], replicated
- shift_two_grad: float32 [768], replicated
Inputs may be any that keep to these rules, and one draw needn't show every extreme that they name: `seg_ids`: within each sequence of 1024 positions the document numbers never fall; each document holds 1 to 512 positions and one holds exactly 512.
All inputs are finite; a program needn't handle non-finite values. No bound on the sum of `keep_mask` on one device may be relied on, other than what follows from the above.
Results may differ from a plain program's by a relative error of at most 0.015.
Values may be sent and summed in bfloat16 or wider, within the bound.
A program may use at most 192 MiB of HBM per device.

v0:
```python
import math

import jax
import jax.numpy as jnp
from jax import lax
from jax.sharding import PartitionSpec as P

HEAD_DIM = 64


EPS = 1e-06


def gelu_exact(v):
    return 0.5 * v * (1.0 + lax.erf(v * 0.7071067811865476))


def gelu_slope(v):
    return (
        0.5 * (1.0 + lax.erf(v * 0.7071067811865476))
        + v * jnp.exp(-0.5 * v * v) * 0.3989422804014327
    )


def norm_rows(v, gain, shift):
    row_mean = jnp.mean(v, axis=-1, keepdims=True)
    centered = v - row_mean
    factor = lax.rsqrt(jnp.mean(centered * centered, axis=-1, keepdims=True) + EPS)
    normed = centered * factor
    return (normed * gain + shift, normed, factor)


def norm_back(grad_rows, normed, factor, gain):
    inner = grad_rows * gain
    return factor * (
        inner
        - jnp.mean(inner, axis=-1, keepdims=True)
        - normed * jnp.mean(inner * normed, axis=-1, keepdims=True)
    )


def allowed_keys(seg_block, seg_full, keep_full, row_start):
    shape_pair = (seg_block.shape[0], seg_full.shape[0])
    own_pos = row_start + lax.broadcasted_iota(jnp.int32, shape_pair, 0)
    key_pos = lax.broadcasted_iota(jnp.int32, shape_pair, 1)
    return (seg_block[:, None] == seg_full[None, :]) & (
        (keep_full[None, :] == 1) | (own_pos == key_pos)
    )


def block_scores(q_rows, key_rows, allowed, score_scale):
    raw = (
        jnp.einsum("qhd,khd->hqk", q_rows, key_rows, preferred_element_type=jnp.float32)
        * score_scale
    )
    return jnp.where(allowed[None], raw, -1e30)


def attend(queries, key_rows, values, seg_full, keep_full, score_scale, block_rows):
    length, head_count, head_width = queries.shape
    block_count = length // block_rows
    starts = jnp.arange(block_count, dtype=jnp.int32) * block_rows

    def per_block(block_item):
        q_rows, seg_block, row_start = block_item
        scores = block_scores(
            q_rows, key_rows, allowed_keys(seg_block, seg_full, keep_full, row_start), score_scale
        )
        row_max = jnp.max(scores, axis=-1, keepdims=True)
        exps_rows = jnp.exp(scores - row_max)
        denom = jnp.sum(exps_rows, axis=-1, keepdims=True)
        low_probs = (exps_rows / denom).astype(jnp.bfloat16)
        context = jnp.einsum("hqk,khd->qhd", low_probs, values, preferred_element_type=jnp.float32)
        return (context.astype(jnp.bfloat16), (row_max + jnp.log(denom))[..., 0])

    context, logsum = lax.map(
        per_block,
        (
            queries.reshape(block_count, block_rows, head_count, head_width),
            seg_full.reshape(block_count, block_rows),
            starts,
        ),
    )
    return (context.reshape(length, head_count * head_width), logsum)


def attend_back(
    queries, key_rows, values, grad_context, logsum, seg_full, keep_full, score_scale, block_rows
):
    length, head_count, head_width = queries.shape
    block_count = length // block_rows
    starts = jnp.arange(block_count, dtype=jnp.int32) * block_rows

    def per_block(carried, block_item):
        key_acc, value_acc = carried
        q_rows, g_rows, lse_rows, seg_block, row_start = block_item
        scores = block_scores(
            q_rows, key_rows, allowed_keys(seg_block, seg_full, keep_full, row_start), score_scale
        )
        probs = jnp.exp(scores - lse_rows[..., None])
        low_probs = probs.astype(jnp.bfloat16)
        grad_probs = jnp.einsum("qhd,khd->hqk", g_rows, values, preferred_element_type=jnp.float32)
        inner = jnp.sum(probs * grad_probs, axis=-1, keepdims=True)
        grad_scores = (probs * (grad_probs - inner)).astype(jnp.bfloat16)
        grad_q = (
            jnp.einsum("hqk,khd->qhd", grad_scores, key_rows, preferred_element_type=jnp.float32)
            * score_scale
        )
        key_acc = (
            key_acc
            + jnp.einsum("hqk,qhd->khd", grad_scores, q_rows, preferred_element_type=jnp.float32)
            * score_scale
        )
        value_acc = value_acc + jnp.einsum(
            "hqk,qhd->khd", low_probs, g_rows, preferred_element_type=jnp.float32
        )
        return ((key_acc, value_acc), grad_q.astype(jnp.bfloat16))

    zero_grad = jnp.zeros((length, head_count, head_width), jnp.float32)
    grad_ctx4 = grad_context.reshape(block_count, block_rows, head_count, head_width)
    (key_acc, value_acc), grad_q = lax.scan(
        per_block,
        (zero_grad, zero_grad),
        (
            queries.reshape(block_count, block_rows, head_count, head_width),
            grad_ctx4,
            logsum,
            seg_full.reshape(block_count, block_rows),
            starts,
        ),
    )
    flat = head_count * head_width
    return (
        grad_q.reshape(length, flat),
        key_acc.reshape(length, flat).astype(jnp.bfloat16),
        value_acc.reshape(length, flat).astype(jnp.bfloat16),
    )


def add_all(left, right):
    return tuple((a + b for a, b in zip(left, right)))


def shards(
    inputs,
    seg_ids,
    keep_mask,
    w_qkv,
    b_qv,
    w_o,
    b_o,
    gain_one,
    shift_one,
    w_up,
    b_up,
    w_down,
    b_down,
    gain_two,
    shift_two,
    out_grad,
):
    micro_count = inputs.shape[0]
    own_count = inputs.shape[2]
    half_width = w_qkv.shape[2]
    half_units = w_up.shape[1]
    score_scale = 1.0 / math.sqrt(HEAD_DIM)
    tensor_count = lax.axis_size("tensor")
    tensor_rank = lax.axis_index("tensor")
    length = own_count * tensor_count
    block_rows = min(512, length)
    bias_qv = lax.dynamic_slice_in_dim(b_qv, tensor_rank * half_width, half_width, 1)
    bias_up = lax.dynamic_slice_in_dim(b_up, tensor_rank * half_units, half_units, 0)
    shard_grads = None
    local_totals = None
    small_totals = None
    out_list = []
    grad_list = []
    for micro_index in range(micro_count):
        own_rows = inputs[micro_index, 0]
        seg_full = seg_ids[micro_index, 0]
        keep_full = keep_mask[micro_index, 0]
        full_qkv = lax.all_gather(w_qkv, "dp", axis=1, tiled=True)
        full_o = lax.all_gather(w_o, "dp", axis=1, tiled=True)
        full_up = lax.all_gather(w_up, "dp", axis=0, tiled=True)
        full_down = lax.all_gather(w_down, "dp", axis=1, tiled=True)
        head_count = full_qkv.shape[2] // HEAD_DIM
        gathered = lax.all_gather(own_rows, "tensor", axis=0, tiled=True)
        projected = jnp.einsum(
            "ld,cde->cle", gathered, full_qkv, preferred_element_type=jnp.float32
        )
        bias_rows = jnp.stack([bias_qv[0], jnp.zeros_like(bias_qv[0]), bias_qv[1]])
        projected = (projected + bias_rows[:, None, :]).astype(jnp.bfloat16)
        queries = projected[0].reshape(length, head_count, HEAD_DIM)
        key_rows = projected[1].reshape(length, head_count, HEAD_DIM)
        values = projected[2].reshape(length, head_count, HEAD_DIM)
        context, logsum = attend(
            queries, key_rows, values, seg_full, keep_full, score_scale, block_rows
        )
        attn_rows = lax.psum_scatter(
            jnp.dot(context, full_o, preferred_element_type=jnp.float32),
            "tensor",
            scatter_dimension=0,
            tiled=True,
        )
        first_sum = own_rows.astype(jnp.float32) + attn_rows + b_o
        hidden, normed_one, factor_one = norm_rows(first_sum, gain_one, shift_one)
        hidden_low = hidden.astype(jnp.bfloat16)
        spread = lax.all_gather(hidden_low, "tensor", axis=0, tiled=True)
        upward = jnp.dot(spread, full_up, preferred_element_type=jnp.float32) + bias_up
        active = gelu_exact(upward).astype(jnp.bfloat16)
        ffn_rows = lax.psum_scatter(
            jnp.dot(active, full_down, preferred_element_type=jnp.float32),
            "tensor",
            scatter_dimension=0,
            tiled=True,
        )
        second_sum = hidden + ffn_rows + b_down
        result, normed_two, factor_two = norm_rows(second_sum, gain_two, shift_two)
        grad_out = out_grad[micro_index, 0].astype(jnp.float32)
        sum_g2 = jnp.sum(grad_out * normed_two, axis=0)
        sum_e2 = jnp.sum(grad_out, axis=0)
        grad_second = norm_back(grad_out, normed_two, factor_two, gain_two)
        sum_down = jnp.sum(grad_second, axis=0)
        second_low = grad_second.astype(jnp.bfloat16)
        grad_ffn = lax.all_gather(second_low, "tensor", axis=0, tiled=True)
        local_down = lax.dot_general(
            active, grad_ffn, (((0,), (0,)), ((), ())), preferred_element_type=jnp.float32
        )
        grad_active = lax.dot_general(
            grad_ffn, full_down, (((1,), (1,)), ((), ())), preferred_element_type=jnp.float32
        )
        grad_up = (grad_active * gelu_slope(upward)).astype(jnp.bfloat16)
        sum_up = jnp.sum(grad_up.astype(jnp.float32), axis=0)
        local_up = lax.dot_general(
            spread, grad_up, (((0,), (0,)), ((), ())), preferred_element_type=jnp.float32
        )
        grad_hidden = grad_second + lax.psum_scatter(
            lax.dot_general(
                grad_up, full_up, (((1,), (1,)), ((), ())), preferred_element_type=jnp.float32
            ),
            "tensor",
            scatter_dimension=0,
            tiled=True,
        )
        sum_g1 = jnp.sum(grad_hidden * normed_one, axis=0)
        sum_e1 = jnp.sum(grad_hidden, axis=0)
        grad_first = norm_back(grad_hidden, normed_one, factor_one, gain_one)
        sum_o = jnp.sum(grad_first, axis=0)
        first_low = grad_first.astype(jnp.bfloat16)
        grad_attn = lax.all_gather(first_low, "tensor", axis=0, tiled=True)
        local_o = lax.dot_general(
            context, grad_attn, (((0,), (0,)), ((), ())), preferred_element_type=jnp.float32
        )
        grad_context = lax.dot_general(
            grad_attn, full_o, (((1,), (1,)), ((), ())), preferred_element_type=jnp.float32
        ).astype(jnp.bfloat16)
        grad_q, grad_k, grad_v = attend_back(
            queries,
            key_rows,
            values,
            grad_context,
            logsum,
            seg_full,
            keep_full,
            score_scale,
            block_rows,
        )
        grad_proj = jnp.stack([grad_q, grad_k, grad_v])
        sum_qv = jnp.stack(
            [
                jnp.sum(grad_q.astype(jnp.float32), axis=0),
                jnp.sum(grad_v.astype(jnp.float32), axis=0),
            ]
        )
        local_qkv = jnp.einsum(
            "ld,cle->cde", gathered, grad_proj, preferred_element_type=jnp.float32
        )
        x_rows = grad_first + lax.psum_scatter(
            jnp.einsum(
                "cle,cde->ld", grad_proj, full_qkv, preferred_element_type=jnp.float32
            ).astype(jnp.bfloat16),
            "tensor",
            scatter_dimension=0,
            tiled=True,
        ).astype(jnp.float32)
        smalls = (sum_qv, sum_o, sum_g1, sum_e1, sum_up, sum_down, sum_g2, sum_e2)
        result, x_rows, local_grads, smalls = (
            result.astype(jnp.bfloat16),
            x_rows,
            (local_qkv, local_o, local_up, local_down),
            smalls,
        )
        out_list.append(result)
        grad_list.append(x_rows)
        small_totals = smalls if small_totals is None else add_all(small_totals, smalls)
        take_shard_grads = shard_grads
        settled = (
            lax.psum_scatter(local_grads[0], "dp", scatter_dimension=1, tiled=True),
            lax.psum_scatter(local_grads[1], "dp", scatter_dimension=1, tiled=True),
            lax.psum_scatter(local_grads[2], "dp", scatter_dimension=0, tiled=True),
            lax.psum_scatter(local_grads[3], "dp", scatter_dimension=1, tiled=True),
        )
        take_shard_grads = (
            settled if take_shard_grads is None else add_all(take_shard_grads, settled)
        )
        shard_grads, local_totals = (take_shard_grads, local_totals)
    out_rows = jnp.stack(out_list)[:, None]
    grad_rows = jnp.stack(grad_list)[:, None]
    qv_full = lax.dynamic_update_slice(
        jnp.zeros((2, half_width * tensor_count), jnp.float32),
        small_totals[0],
        (jnp.int32(0), tensor_rank * half_width),
    )
    up_full = lax.dynamic_update_slice(
        jnp.zeros((half_units * tensor_count,), jnp.float32),
        small_totals[4],
        (tensor_rank * half_units,),
    )
    summed = lax.psum(
        (
            qv_full,
            small_totals[1],
            small_totals[2],
            small_totals[3],
            up_full,
            small_totals[5],
            small_totals[6],
            small_totals[7],
        ),
        ("dp", "tensor"),
    )
    grad_qv = lax.dynamic_slice_in_dim(summed[0], tensor_rank * half_width, half_width, 1)
    grad_up_bias = lax.dynamic_slice_in_dim(summed[4], tensor_rank * half_units, half_units, 0)
    return (
        out_rows,
        grad_rows,
        shard_grads[0],
        grad_qv,
        shard_grads[1],
        summed[1],
        summed[2],
        summed[3],
        shard_grads[2],
        grad_up_bias,
        shard_grads[3],
        summed[5],
        summed[6],
        summed[7],
    )


def solution(mesh):
    placed = (
        P(None, "dp", "tensor", None),
        P(None, "dp", None),
        P(None, "dp", None),
        P(None, "dp", "tensor"),
        P(),
        P("tensor", "dp"),
        P(),
        P(),
        P(),
        P("dp", "tensor"),
        P(),
        P("tensor", "dp"),
        P(),
        P(),
        P(),
        P(None, "dp", "tensor", None),
    )
    return jax.shard_map(
        shards,
        mesh=mesh,
        in_specs=placed,
        out_specs=(
            P(None, "dp", "tensor", None),
            P(None, "dp", "tensor", None),
            P(None, "dp", "tensor"),
            P(None, "tensor"),
            P("tensor", "dp"),
            P(),
            P(),
            P(),
            P("dp", "tensor"),
            P("tensor"),
            P("tensor", "dp"),
            P(),
            P(),
            P(),
        ),
        check_vma=False,
    )
```

profile of v0, /device:TPU:0, one launch (start us, length us, event | category | flops | bytes accessed | tf_op | source)
XLA Modules:
  0.0 1215.2 jit_solution(6514101610812780588)
XLA Ops:
  11.5 24.9 %all_gather.42 = bf16[384,768]{0,1:T(8,128)(2,1)S(1)} all-gather(bf16[384,48]{0,1:T(8,128)(2,1)S(1)} %copy-done.58), channel_id=1, replica_groups=mesh['dp'=16,'tensor'=2] {'dp'}, dimensions={1}, use_global_device_ids=true | all-gather | bytes 626688 | tf_op jit(solution)/shard_map/all_gather | solution.py:183
  40.1 42.8 %all-gather.14.cloned.1.call-done = bf16[3,768,384]{2,1,0:T(8,128)(2,1)} async-done(((bf16[3,48,384]{2,1,0:T(8,128)(2,1)}), bf16[3,768,384]{2,1,0:T(8,128)(2,1)}) %all-gather.14.cloned.1.call-update) | async-done | bytes 1769488 | tf_op jit(solution)/shard_map/all_gather | solution.py:182
  90.9 26.0 %while.55 = (s32[]{:T(128)}, bf16[2,512,6,64]{1,3,2,0:T(8,128)(2,1)}, f32[2,6,512]{2,1,0:T(8,128)S(1)}, s32[2,512]{1,0:T(2,128)S(1)}, s32[1,1,1024]{2,1,0:T(1,12...) while((s32[]{:T(128)}, ...), condition=%wide.region_13.14_spmd, body=%wide.region_10.13_spmd.sunk | while | flops 845347328 | bytes 42336904 | solution.py:76
  132.2 26.0 %while.54 = (s32[]{:T(128)}, bf16[2,512,6,64]{1,3,2,0:T(8,128)(2,1)}, f32[2,6,512]{2,1,0:T(8,128)S(1)}, s32[2,512]{1,0:T(2,128)S(1)}, s32[1,1,1024]{2,1,0:T(1,12...) while((s32[]{:T(128)}, ...), condition=%wide.region_3.4_spmd, body=%wide.region_0.3_spmd.sunk | while | flops 845347328 | bytes 42336904 | solution.py:76
  165.5 46.1 %reduce-scatter.12.cloned.1.call-done = f32[512,768]{1,0:T(8,128)} async-done(((f32[1024,768]{1,0:T(8,128)}), f32[512,768]{1,0:T(8,128)}) %reduce-scatter.12.cloned.1.call-update) | async-done | bytes 1572880 | tf_op jit(solution)/shard_map/reduce_scatter | solution.py:199
  218.6 37.5 %all-gather.18.cloned.1.call-done = bf16[768,1536]{1,0:T(8,128)(2,1)} async-done(((bf16[48,1536]{1,0:T(8,128)(2,1)}), bf16[768,1536]{1,0:T(8,128)(2,1)}) %all-gather.18.cloned.1.call-update) | async-done | bytes 2359312 | tf_op jit(solution)/shard_map/all_gather | solution.py:184
  256.1 27.5 %all-gather.22.cloned.1.call-done = bf16[1024,768]{1,0:T(8,128)(2,1)} async-done(((bf16[512,768]{1,0:T(8,128)(2,1)}), bf16[1024,768]{1,0:T(8,128)(2,1)}) %all-gather.22.cloned.1.call-update) | async-done | bytes 1572880 | tf_op jit(solution)/shard_map/all_gather | solution.py:208
  283.6 7.4 fusion.149
  291.0 21.9 %all-gather.16.cloned.1.call-done = bf16[1024,768]{1,0:T(8,128)(2,1)} async-done(((bf16[512,768]{1,0:T(8,128)(2,1)}), bf16[1024,768]{1,0:T(8,128)(2,1)}) %all-gather.16.cloned.1.call-update) | async-done | bytes 1572880 | tf_op jit(solution)/shard_map/all_gather | solution.py:208
  312.9 11.0 multiply_convert_fusion.3
  324.0 33.6 %all-gather.20.cloned.1.call-done = bf16[1536,768]{0,1:T(8,128)(2,1)} async-done(((bf16[1536,48]{0,1:T(8,128)(2,1)}), bf16[1536,768]{0,1:T(8,128)(2,1)}) %all-gather.20.cloned.1.call-update) | async-done | bytes 2359312 | tf_op jit(solution)/shard_map/all_gather | solution.py:185
  357.6 6.9 fusion.147
  364.5 6.9 fusion.150
  371.5 35.3 %reduce-scatter.14.cloned.1.call-done = f32[512,768]{1,0:T(8,128)} async-done(((f32[1024,768]{1,0:T(8,128)}), f32[512,768]{1,0:T(8,128)}) %reduce-scatter.14.cloned.1.call-update) | async-done | bytes 1572880 | tf_op jit(solution)/shard_map/reduce_scatter | solution.py:211
  406.8 45.7 %reduce-scatter.18.cloned.1.call-done = f32[512,768]{1,0:T(8,128)} async-done(((f32[1024,768]{1,0:T(8,128)}), f32[512,768]{1,0:T(8,128)}) %reduce-scatter.18.cloned.1.call-update) | async-done | bytes 1572880 | tf_op jit(solution)/shard_map/reduce_scatter | solution.py:211
  467.6 24.7 %all-gather.24.cloned.1.call-done = bf16[1024,768]{1,0:T(8,128)(2,1)} async-done(((bf16[512,768]{1,0:T(8,128)(2,1)}), bf16[1024,768]{1,0:T(8,128)(2,1)}) %all-gather.24.cloned.1.call-update) | async-done | bytes 1572880 | tf_op jit(solution)/shard_map/all_gather | solution.py:225
  492.2 7.7 convert_reduce_fusion.1
  505.9 15.0 %all-gather.28.cloned.1.call-done = bf16[1024,768]{1,0:T(8,128)(2,1)} async-done(((bf16[512,768]{1,0:T(8,128)(2,1)}), bf16[1024,768]{1,0:T(8,128)(2,1)}) %all-gather.28.cloned.1.call-update) | async-done | bytes 1572880 | tf_op jit(solution)/shard_map/all_gather | solution.py:225
  521.0 7.7 convert_reduce_fusion
  534.7 31.8 %reduce-scatter.20.cloned.1.call-done = f32[512,768]{1,0:T(8,128)} async-done(((f32[1024,768]{1,0:T(8,128)}), f32[512,768]{1,0:T(8,128)}) %reduce-scatter.20.cloned.1.call-update) | async-done | bytes 1572880 | tf_op jit(solution)/shard_map/reduce_scatter | solution.py:237
  571.3 40.8 %reduce-scatter.24.cloned.1.call-done = f32[512,768]{1,0:T(8,128)} async-done(((f32[1024,768]{1,0:T(8,128)}), f32[512,768]{1,0:T(8,128)}) %reduce-scatter.24.cloned.1.call-update) | async-done | bytes 1572880 | tf_op jit(solution)/shard_map/reduce_scatter | solution.py:237
  624.0 22.5 %all-gather.26.cloned.1.call-done = bf16[1024,768]{1,0:T(8,128)(2,1)} async-done(((bf16[512,768]{1,0:T(8,128)(2,1)}), bf16[1024,768]{1,0:T(8,128)(2,1)}) %all-gather.26.cloned.1.call-update) | async-done | bytes 1572880 | tf_op jit(solution)/shard_map/all_gather | solution.py:250
  651.7 65.0 %while.56 = (s32[]{:T(128)}, f32[1024,6,64]{0,2,1:T(8,128)}, f32[1024,6,64]{0,2,1:T(8,128)}, bf16[2,512,6,64]{1,3,2,0:T(8,128)(2,1)}, bf16[2,512,6,64]{1,3,2,0:T...) while((s32[]{:T(128)}, f32[1024,6,64]{0,2,1:T(8,128)}, ...), condition=%wide.region_27.28_spmd.clone, body=%wide.region_25.27_spmd.clone.sunk | while | flops 2064906752 | bytes 211006768 | solution.py:121
  655.8 6.3 multiply_reduce_fusion.14
  662.1 5.0 multiply_convert_fusion.6
  667.1 5.3 bitcast_add_fusion.8
  672.4 6.2 fusion.269
  687.4 6.3 multiply_reduce_fusion.14
  698.7 5.7 bitcast_add_fusion.8
  704.5 6.2 fusion.269
  710.7 6.0 bitcast_add_fusion.9
  725.1 65.3 %while.57 = (s32[]{:T(128)}, f32[1024,6,64]{0,2,1:T(8,128)}, f32[1024,6,64]{0,2,1:T(8,128)}, bf16[2,512,6,64]{1,3,2,0:T(8,128)(2,1)}, bf16[2,512,6,64]{1,3,2,0:T...) while((s32[]{:T(128)}, f32[1024,6,64]{0,2,1:T(8,128)}, ...), condition=%wide.region_36.37_spmd.clone, body=%wide.region_34.36_spmd.clone.sunk | while | flops 2064906752 | bytes 211006768 | solution.py:121
  729.4 6.3 multiply_reduce_fusion.15
  740.7 5.3 bitcast_add_fusion.10
  746.0 6.2 fusion.281
  761.0 6.3 multiply_reduce_fusion.15
  772.3 5.8 bitcast_add_fusion.10
  778.1 6.2 fusion.281
  784.2 6.0 bitcast_add_fusion.11
  814.9 5.2 bitcast_convert_fusion.1
  820.4 5.2 bitcast_convert_fusion
  857.5 41.0 %all-reduce.1 = (f32[2,768]{1,0:T(2,128)S(1)}, f32[768]{0:T(1024)}, f32[768]{0:T(1024)}, f32[768]{0:T(1024)}, f32[3072]{0:T(1024)S(1)}, /*index=5*/f32[768]{0:T(1024)}, f32[768]{0:T(1024)}, f32[768]{0:T(1024)}) all-reduce(f32[2,768]{1,0:T(2,128)S(1)} %fusion.125, ...), channel_id=1, replica_groups=mesh['dp'=16,'tensor'=2] {'dp','tensor'}, use_global_device_ids=true, to_apply=%region_44.45 | all-reduce | flops 9216 | bytes 73728 | tf_op jit(solution)/shard_map/psum | solution.py:319
  899.8 31.1 %all-reduce.4.cloned.1.call-done = f32[3,768,384]{2,0,1:T(4,128)} async-done(((f32[3,768,384]{2,0,1:T(4,128)}), f32[3,768,384]{2,0,1:T(4,128)}) %all-reduce.4.cloned.1.call-update) | async-done | bytes 3538960
  932.6 26.5 %reduce-scatter.22.cloned.1.call-done = bf16[512,768]{1,0:T(8,128)(2,1)} async-done(((bf16[1024,768]{1,0:T(8,128)(2,1)}), bf16[512,768]{1,0:T(8,128)(2,1)}) %reduce-scatter.22.cloned.1.call-update) | async-done | bytes 786448 | tf_op jit(solution)/shard_map/reduce_scatter | solution.py:278
  961.5 25.9 %reduce-scatter.26.cloned.1.call-done = bf16[512,768]{1,0:T(8,128)(2,1)} async-done(((bf16[1024,768]{1,0:T(8,128)(2,1)}), bf16[512,768]{1,0:T(8,128)(2,1)}) %reduce-scatter.26.cloned.1.call-update) | async-done | bytes 786448 | tf_op jit(solution)/shard_map/reduce_scatter | solution.py:278
  990.6 76.7 %reduce-scatter.32.cloned.1.call-done = f32[1536,48]{0,1:T(8,128)} async-done(((f32[1536,768]{0,1:T(8,128)}), f32[1536,48]{0,1:T(8,128)}) %reduce-scatter.32.cloned.1.call-update) | async-done | bytes 294928 | tf_op jit(solution)/shard_map/reduce_scatter | solution.py:301
  1067.4 79.2 %reduce-scatter.30.cloned.1.call-done = f32[48,1536]{1,0:T(8,128)} async-done(((f32[768,1536]{1,0:T(8,128)}), f32[48,1536]{1,0:T(8,128)}) %reduce-scatter.30.cloned.1.call-update) | async-done | bytes 294928 | tf_op jit(solution)/shard_map/reduce_scatter | solution.py:300
  1146.6 61.6 %reduce-scatter.28.cloned.1.call-done = f32[384,48]{0,1:T(8,128)} async-done(((f32[384,768]{0,1:T(8,128)}), f32[384,48]{0,1:T(8,128)}) %reduce-scatter.28.cloned.1.call-update) | async-done | bytes 73744 | tf_op jit(solution)/shard_map/reduce_scatter | solution.py:299
  (439 shorter events, 258.3 us)
Async XLA Ops:
  7.2 29.3 %copy-start.80 = (f32[2,768]{1,0:T(2,128)S(1)}, f32[2,768]{1,0:T(2,128)}, u32[]{:S(2)}) copy-start(f32[2,768]{1,0:T(2,128)} %param.28) | copy-start | bytes 18436
  7.2 32.9 %all-gather.34.cloned.1.call-start = ((), (), s32[]{:S(2)}) async-start(), calls=%async_computation.29 | async-start | bytes 2359296 | tf_op jit(solution)/shard_map/all_gather | solution.py:187
  9.9 73.0 %all-gather.14.cloned.1.call-start = ((), (), s32[]{:S(2)}) async-start(), calls=%async_computation.11 | async-start | bytes 1880064 | tf_op jit(solution)/shard_map/all_gather | solution.py:182
  10.7 112.9 %all-gather.32.cloned.1.call-start = ((), (), s32[]{:S(2)}) async-start(), calls=%async_computation.28 | async-start | bytes 2359296 | tf_op jit(solution)/shard_map/all_gather | solution.py:187
  11.4 154.1 %reduce-scatter.16.cloned.1.call-start = ((), (), s32[]{:S(2)}) async-start(), calls=%async_computation.17 | async-start | bytes 4718592 | tf_op jit(solution)/shard_map/reduce_scatter | solution.py:199
  36.4 83.3 %copy-start.29 = (bf16[384,768]{0,1:T(8,128)(2,1)}, bf16[384,768]{0,1:T(8,128)(2,1)S(1)}, u32[]{:S(2)}) copy-start(bf16[384,768]{0,1:T(8,128)(2,1)S(1)} %all_gather.42) | copy-start | bytes 1769476
  116.9 6.3 copy-start.4
  116.9 6.3 copy-start.8
  116.9 6.3 copy-start.11
  117.0 6.3 copy-start.49
  123.3 88.4 %reduce-scatter.12.cloned.1.call-start = ((), (), s32[]{:S(2)}) async-start(), calls=%async_computation.12 | async-start | bytes 4718592 | tf_op jit(solution)/shard_map/reduce_scatter | solution.py:199
  164.2 47.4 %copy-start.77 = (f32[768]{0:T(1024)S(1)}, f32[768]{0:T(1024)}, u32[]{:S(2)}) copy-start(f32[768]{0:T(1024)} %param.30) | copy-start | bytes 9220
  164.3 91.8 %all-gather.18.cloned.1.call-start = ((), (), s32[]{:S(2)}) async-start(), calls=%async_computation.14 | async-start | bytes 2506752 | tf_op jit(solution)/shard_map/all_gather | solution.py:184
  164.8 118.7 %all-gather.22.cloned.1.call-start = ((), (), s32[]{:S(2)}) async-start(), calls=%async_computation.18 | async-start | bytes 2359296 | tf_op jit(solution)/shard_map/all_gather | solution.py:208
  217.0 95.9 %all-gather.16.cloned.1.call-start = ((), (), s32[]{:S(2)}) async-start(), calls=%async_computation.13 | async-start | bytes 2359296 | tf_op jit(solution)/shard_map/all_gather | solution.py:208
  217.7 139.8 %all-gather.20.cloned.1.call-start = ((), (), s32[]{:S(2)}) async-start(), calls=%async_computation.15 | async-start | bytes 2506752 | tf_op jit(solution)/shard_map/all_gather | solution.py:185
  218.5 188.3 %reduce-scatter.14.cloned.1.call-start = ((), (), s32[]{:S(2)}) async-start(), calls=%async_computation.16 | async-start | bytes 4718592 | tf_op jit(solution)/shard_map/reduce_scatter | solution.py:211
  364.5 88.0 %reduce-scatter.18.cloned.1.call-start = ((), (), s32[]{:S(2)}) async-start(), calls=%async_computation.19 | async-start | bytes 4718592 | tf_op jit(solution)/shard_map/reduce_scatter | solution.py:211
  371.4 81.1 %copy-start.78 = (f32[768]{0:T(1024)S(1)}, f32[768]{0:T(1024)}, u32[]{:S(2)}) copy-start(f32[768]{0:T(1024)} %param.36) | copy-start | bytes 9220
  371.5 120.8 %all-gather.24.cloned.1.call-start = ((), (), s32[]{:S(2)}) async-start(), calls=%async_computation.20 | async-start | bytes 2359296 | tf_op jit(solution)/shard_map/all_gather | solution.py:225
  464.9 56.1 %all-gather.28.cloned.1.call-start = ((), (), s32[]{:S(2)}) async-start(), calls=%async_computation.24 | async-start | bytes 2359296 | tf_op jit(solution)/shard_map/all_gather | solution.py:225
  467.3 99.2 %reduce-scatter.20.cloned.1.call-start = ((), (), s32[]{:S(2)}) async-start(), calls=%async_computation.21 | async-start | bytes 4718592 | tf_op jit(solution)/shard_map/reduce_scatter | solution.py:237
  492.2 9.3 copy-start.81
  505.9 106.2 %reduce-scatter.24.cloned.1.call-start = ((), (), s32[]{:S(2)}) async-start(), calls=%async_computation.25 | async-start | bytes 4718592 | tf_op jit(solution)/shard_map/reduce_scatter | solution.py:237
  521.0 9.4 copy-start.82
  534.7 111.9 %all-gather.26.cloned.1.call-start = ((), (), s32[]{:S(2)}) async-start(), calls=%async_computation.22 | async-start | bytes 2359296 | tf_op jit(solution)/shard_map/all_gather | solution.py:250
  619.2 100.6 %all-gather.30.cloned.1.call-start = ((), (), s32[]{:S(2)}) async-start(), calls=%async_computation.26 | async-start | bytes 2359296 | tf_op jit(solution)/shard_map/all_gather | solution.py:250
  621.8 24.7 %copy-start.31 = (bf16[384,768]{0,1:T(8,128)(2,1)S(1)}, bf16[384,768]{0,1:T(8,128)(2,1)}, u32[]{:S(2)}) copy-start(bf16[384,768]{0,1:T(8,128)(2,1)} %copy-done.29) | copy-start | bytes 1769476
  624.0 306.9 %all-reduce.4.cloned.1.call-start = ((), (), s32[]{:S(2)}) async-start(), calls=%async_computation.33 | async-start | bytes 9437184
  655.8 6.3 copy-start
  667.1 11.5 copy-start.1
  687.4 6.3 copy-start
  698.7 12.0 copy-start.1
  704.5 6.3 copy-start.21
  729.3 6.3 copy-start.2
  740.7 11.5 copy-start.3
  760.9 6.3 copy-start.2
  772.3 12.0 copy-start.3
  813.5 6.8 copy-start.42
  813.6 6.8 copy-start.44
  813.6 145.5 %reduce-scatter.22.cloned.1.call-start = ((), (), s32[]{:S(2)}) async-start(), calls=%async_computation.23 | async-start | bytes 2359296 | tf_op jit(solution)/shard_map/reduce_scatter | solution.py:278
  820.1 167.3 %reduce-scatter.26.cloned.1.call-start = ((), (), s32[]{:S(2)}) async-start(), calls=%async_computation.27 | async-start | bytes 2359296 | tf_op jit(solution)/shard_map/reduce_scatter | solution.py:278
  825.7 241.7 %reduce-scatter.32.cloned.1.call-start = ((), (), s32[]{:S(2)}) async-start(), calls=%async_computation.32 | async-start | bytes 5013504 | tf_op jit(solution)/shard_map/reduce_scatter | solution.py:301
  834.9 311.7 %reduce-scatter.30.cloned.1.call-start = ((), (), s32[]{:S(2)}) async-start(), calls=%async_computation.31 | async-start | bytes 5013504 | tf_op jit(solution)/shard_map/reduce_scatter | solution.py:300
  845.8 362.4 %reduce-scatter.28.cloned.1.call-start = ((), (), s32[]{:S(2)}) async-start(), calls=%async_computation.30 | async-start | bytes 1253376 | tf_op jit(solution)/shard_map/reduce_scatter | solution.py:299
  856.3 102.8 %copy-start.19 = (f32[512,768]{1,0:T(8,128)S(1)}, f32[512,768]{1,0:T(8,128)}, u32[]{:S(2)}) copy-start(f32[512,768]{1,0:T(8,128)} %copy-done.18) | copy-start | bytes 4718596
  931.9 55.5 %copy-start.17 = (f32[512,768]{1,0:T(8,128)S(1)}, f32[512,768]{1,0:T(8,128)}, u32[]{:S(2)}) copy-start(f32[512,768]{1,0:T(8,128)} %copy-done.16) | copy-start | bytes 4718596
  961.5 27.2 %copy-start.28 = (f32[1,512,768]{2,1,0:T(8,128)S(1)}, f32[1,512,768]{2,1,0:T(8,128)}, u32[]{:S(2)}) copy-start(f32[1,512,768]{2,1,0:T(8,128)} %add_bitcast_fusion.2) | copy-start | bytes 4718596
  (73 other events, 202.6 us)
Sparse Core Ops, SparseCore 0:
  10.1 29.8 all-gather.33
  42.4 40.4 all-gather.13
  85.0 25.8 all-gather.31
  123.4 42.0 reduce-scatter.15
  168.2 43.4 reduce-scatter.11
  213.8 42.3 all-gather.17
  257.7 25.8 all-gather.21
  285.7 27.1 all-gather.15
  315.2 42.2 all-gather.19
  364.6 42.1 reduce-scatter.13
  409.0 43.4 reduce-scatter.17
  465.0 27.1 all-gather.23
  493.8 27.1 all-gather.27
  523.1 43.4 reduce-scatter.19
  568.6 43.4 reduce-scatter.23
  619.3 27.1 all-gather.25
  647.9 27.1 all-gather.29
  813.7 117.1 all-reduce.3
  933.1 25.9 reduce-scatter.21
  961.1 26.1 reduce-scatter.25
  991.8 75.5 reduce-scatter.31
  1071.8 74.7 reduce-scatter.29
  1150.8 57.3 reduce-scatter.27
where the time goes:
time: 1220 us
  waiting for transfers between devices  734 us (60%)
  matrix products  246 us (20%)
  other arithmetic  91.2 us (7%)
  blocking collectives  65.9 us (5%)
  local copies, waits for them, and re-layouts  59.4 us (5%)
  between operations  16.3 us (1%)
    reduce_scatter x2, waiting for transfers between devices, shards(): lax.psum_scatter(jnp.dot(active, full_down, preferred_element_type=jnp.fl...  81 us
    reduce_scatter x1, waiting for transfers between devices, shards(): lax.psum_scatter(local_grads[2], 'dp', scatter_dimension=0, tiled=True)  79.2 us
    reduce_scatter x1, waiting for transfers between devices, shards(): lax.psum_scatter(local_grads[3], 'dp', scatter_dimension=1, tiled=True)  76.7 us
    reduce_scatter x2, waiting for transfers between devices, shards(): lax.psum_scatter(lax.dot_general(grad_up, full_up, (((1,), (1,)), ((), ()...  72.6 us
    reduce_scatter x1, waiting for transfers between devices, shards(): lax.psum_scatter(local_grads[1], 'dp', scatter_dimension=1, tiled=True)  61.6 us
    reduce_scatter x2, waiting for transfers between devices, shards(): lax.psum_scatter(jnp.einsum('cle,cde->ld', grad_proj, full_qkv, preferred...  52.3 us
    all_gather x2, waiting for transfers between devices, shards(): spread = lax.all_gather(hidden_low, 'tensor', axis=0, tiled=True)  49.4 us
    reduce_scatter x2, waiting for transfers between devices, shards(): lax.psum_scatter(jnp.dot(context, full_o, preferred_element_type=jnp.floa...  46.3 us
  transfers between devices with their start and end apart: 23, of which 21 were waited for; matrix products, arithmetic and copies ran while one was open for 22% of the time, Pallas kernels for 0%

commit v1 on v0

v1 whole, which is shorter than its diff:
```python
import math
import functools
import jax
import jax.numpy as jnp
from jax import lax
from jax.sharding import PartitionSpec as P
from jax.experimental import pallas as pl
from jax.experimental.pallas import tpu as pltpu

HEAD_DIM = 64
EPS = 1e-06
F32 = jnp.float32
BF16 = jnp.bfloat16
VMEM_MOST = 60 * 1024 * 1024


def dot_nn(a, b):
    return lax.dot_general(a, b, (((1,), (0,)), ((), ())), preferred_element_type=F32)


def dot_nt(a, b):
    return lax.dot_general(a, b, (((1,), (1,)), ((), ())), preferred_element_type=F32)


def dot_tn(a, b):
    return lax.dot_general(a, b, (((0,), (0,)), ((), ())), preferred_element_type=F32)


def params(**more):
    return pltpu.CompilerParams(vmem_limit_bytes=VMEM_MOST, **more)


def qkv_kernel(x_ref, w_ref, bias_ref, out_ref):
    rows = x_ref.shape[0]
    step = min(256, rows)
    for start in range(0, rows, step):
        part = dot_nn(x_ref[start : start + step, :], w_ref[0, 0]) + bias_ref[0]
        out_ref[0, start : start + step, :] = part.astype(BF16)


def project(x, weights, bias):
    rows, width = x.shape
    parts, _, _, cols = weights.shape
    wide = bias.shape[-1]
    return pl.pallas_call(
        qkv_kernel,
        grid=(parts,),
        in_specs=[
            pl.BlockSpec((rows, width), lambda t: (0, 0)),
            pl.BlockSpec((1, 1, width, wide), lambda t: (t, 0, 0, 0)),
            pl.BlockSpec((1, 1, wide), lambda t: (t, 0, 0)),
        ],
        out_specs=pl.BlockSpec((1, rows, wide), lambda t: (t, 0, 0)),
        out_shape=jax.ShapeDtypeStruct((parts, rows, wide), BF16),
        compiler_params=params(),
        name="project",
    )(x, weights, bias)


TILE = 256


def allowed_tile(code_ref, seg_ref, key0, query0):
    codes = code_ref[pl.ds(key0, TILE), :]
    codes = jnp.concatenate([codes] * (TILE // codes.shape[1]), axis=1)
    same = codes == seg_ref[:, pl.ds(query0, TILE)]
    key_pos = key0 + lax.broadcasted_iota(jnp.int32, (TILE, TILE), 0)
    query_pos = query0 + lax.broadcasted_iota(jnp.int32, (TILE, TILE), 1)
    return same | (key_pos == query_pos)


def head_masks(lanes):
    lane = lax.broadcasted_iota(jnp.int32, (1, lanes), 1)
    return [(lane // HEAD_DIM == h).astype(BF16) for h in range(lanes // HEAD_DIM)]


def attend_kernel(
    low_ref, high_ref, code_ref, seg_ref, q_ref, k_ref, v_ref, ctx_ref, lse_ref, top, den, acc
):
    rows, lanes = q_ref.shape[1], q_ref.shape[2]
    heads = lanes // HEAD_DIM
    masks = head_masks(lanes)

    @pl.loop(0, rows // TILE)
    def _(qi):
        query0 = pl.multiple_of(qi * TILE, TILE)
        queries = q_ref[0, pl.ds(query0, TILE), :] * BF16(0.125)
        each = [queries * masks[h] for h in range(heads)]
        top[...] = jnp.full_like(top, -1e30)
        den[...] = jnp.zeros_like(den)
        acc[...] = jnp.zeros_like(acc)

        @pl.loop(low_ref[qi], high_ref[qi])
        def _(ki):
            key0 = pl.multiple_of(ki * TILE, TILE)
            allowed = allowed_tile(code_ref, seg_ref, key0, query0)
            keys = k_ref[0, pl.ds(key0, TILE), :]
            values_t = v_ref[0, pl.ds(key0, TILE), :].T
            for h in range(heads):
                scores = jnp.where(allowed, dot_nt(keys, each[h]), -1e30)
                old = top[h]
                new = jnp.maximum(old, jnp.max(scores, axis=0, keepdims=True))
                expo = jnp.exp(scores - new)
                shrink = jnp.exp(old - new)
                top[h] = new
                den[h] = den[h] * shrink + jnp.sum(expo, axis=0, keepdims=True)
                part = dot_nn(values_t[h * HEAD_DIM : (h + 1) * HEAD_DIM], expo.astype(BF16))
                acc[h] = acc[h] * shrink + part

        both = jnp.concatenate([acc[h] / den[h] for h in range(heads)], axis=0)
        ctx_ref[0, pl.ds(query0, TILE), :] = both.astype(BF16).T
        for h in range(heads):
            lse_ref[0, h : h + 1, pl.ds(query0, TILE)] = top[h] + jnp.log(den[h])


def attend(projected, low, high, codes, seg_row):
    parts, rows, wide = projected.shape
    lanes = 128
    heads = lanes // HEAD_DIM
    groups = wide // 3 // lanes
    return pl.pallas_call(
        attend_kernel,
        grid_spec=pltpu.PrefetchScalarGridSpec(
            num_scalar_prefetch=2,
            grid=(parts, groups),
            in_specs=[
                pl.BlockSpec((rows, 128), lambda t, j, lo, hi: (0, 0)),
                pl.BlockSpec((1, rows), lambda t, j, lo, hi: (0, 0)),
                pl.BlockSpec((1, rows, lanes), lambda t, j, lo, hi: (t, 0, j)),
                pl.BlockSpec((1, rows, lanes), lambda t, j, lo, hi: (t, 0, groups + j)),
                pl.BlockSpec((1, rows, lanes), lambda t, j, lo, hi: (t, 0, 2 * groups + j)),
            ],
            out_specs=[
                pl.BlockSpec((1, rows, lanes), lambda t, j, lo, hi: (t, 0, j)),
                pl.BlockSpec((1, heads, rows), lambda t, j, lo, hi: (t * groups + j, 0, 0)),
            ],
            scratch_shapes=[
                pltpu.VMEM((heads, 1, TILE), F32),
                pltpu.VMEM((heads, 1, TILE), F32),
                pltpu.VMEM((heads, HEAD_DIM, TILE), F32),
            ],
        ),
        out_shape=[
            jax.ShapeDtypeStruct((parts, rows, wide // 3), BF16),
            jax.ShapeDtypeStruct((parts * groups, heads, rows), F32),
        ],
        compiler_params=params(),
        name="attend",
    )(low, high, codes, seg_row, projected, projected, projected)


def attend_back_kernel(
    low_ref,
    high_ref,
    code_ref,
    seg_ref,
    q_ref,
    k_ref,
    v_ref,
    ctx_ref,
    g_ref,
    lse_ref,
    dq_ref,
    dk_ref,
    dv_ref,
    qsum_ref,
    vsum_ref,
    dq_acc,
    dk_acc,
    dv_acc,
):
    rows, lanes = q_ref.shape[1], q_ref.shape[2]
    heads = lanes // HEAD_DIM
    masks = head_masks(lanes)
    dk_acc[...] = jnp.zeros_like(dk_acc)
    dv_acc[...] = jnp.zeros_like(dv_acc)

    @pl.loop(0, rows // TILE)
    def _(qi):
        query0 = pl.multiple_of(qi * TILE, TILE)
        queries = q_ref[0, pl.ds(query0, TILE), :] * BF16(0.125)
        grads = g_ref[0, pl.ds(query0, TILE), :]
        prod_t = (grads.astype(F32) * ctx_ref[0, pl.ds(query0, TILE), :].astype(F32)).T
        q_each = [queries * masks[h] for h in range(heads)]
        g_each = [grads * masks[h] for h in range(heads)]
        inner = [
            jnp.sum(prod_t[h * HEAD_DIM : (h + 1) * HEAD_DIM], axis=0, keepdims=True)
            for h in range(heads)
        ]
        lse = [lse_ref[0, h : h + 1, pl.ds(query0, TILE)] for h in range(heads)]
        dq_acc[...] = jnp.zeros_like(dq_acc)

        @pl.loop(low_ref[qi], high_ref[qi])
        def _(ki):
            key0 = pl.multiple_of(ki * TILE, TILE)
            allowed = allowed_tile(code_ref, seg_ref, key0, query0)
            keys = k_ref[0, pl.ds(key0, TILE), :]
            values = v_ref[0, pl.ds(key0, TILE), :]
            keys_t = keys.T
            dk = dk_acc[pl.ds(key0, TILE), :]
            dv = dv_acc[pl.ds(key0, TILE), :]
            for h in range(heads):
                scores = jnp.where(allowed, dot_nt(keys, q_each[h]), -1e30)
                probs = jnp.exp(scores - lse[h])
                gprobs = dot_nt(values, g_each[h])
                gscores = (probs * (gprobs - inner[h])).astype(BF16)
                dv = dv + dot_nn(probs.astype(BF16), g_each[h])
                dk = dk + dot_nn(gscores, q_each[h])
                lanes_h = slice(h * HEAD_DIM, (h + 1) * HEAD_DIM)
                dq_acc[h] += dot_nn(keys_t[lanes_h], gscores)
            dk_acc[pl.ds(key0, TILE), :] = dk
            dv_acc[pl.ds(key0, TILE), :] = dv

        both = jnp.concatenate([dq_acc[h] for h in range(heads)], axis=0) * 0.125
        dq_ref[0, pl.ds(query0, TILE), :] = both.astype(BF16).T

    low_k = dk_acc[...].astype(BF16)
    low_v = dv_acc[...].astype(BF16)
    dk_ref[0] = low_k
    dv_ref[0] = low_v
    qsum_ref[0] = jnp.sum(dq_ref[0].astype(F32), axis=0, keepdims=True)
    vsum_ref[0] = jnp.sum(low_v.astype(F32), axis=0, keepdims=True)


def attend_back(projected, context, grad_context, lse, low, high, codes, seg_row):
    parts, rows, wide = projected.shape
    lanes = 128
    heads = lanes // HEAD_DIM
    groups = wide // 3 // lanes
    flat = pl.BlockSpec((1, rows, lanes), lambda t, j, lo, hi: (t, 0, j))
    sums = pl.BlockSpec((1, 1, lanes), lambda t, j, lo, hi: (t, 0, j))
    return pl.pallas_call(
        attend_back_kernel,
        grid_spec=pltpu.PrefetchScalarGridSpec(
            num_scalar_prefetch=2,
            grid=(parts, groups),
            in_specs=[
                pl.BlockSpec((rows, 128), lambda t, j, lo, hi: (0, 0)),
                pl.BlockSpec((1, rows), lambda t, j, lo, hi: (0, 0)),
                pl.BlockSpec((1, rows, lanes), lambda t, j, lo, hi: (t, 0, j)),
                pl.BlockSpec((1, rows, lanes), lambda t, j, lo, hi: (t, 0, groups + j)),
                pl.BlockSpec((1, rows, lanes), lambda t, j, lo, hi: (t, 0, 2 * groups + j)),
                flat,
                flat,
                pl.BlockSpec((1, heads, rows), lambda t, j, lo, hi: (t * groups + j, 0, 0)),
            ],
            out_specs=[flat, flat, flat, sums, sums],
            scratch_shapes=[
                pltpu.VMEM((heads, HEAD_DIM, TILE), F32),
                pltpu.VMEM((rows, lanes), F32),
                pltpu.VMEM((rows, lanes), F32),
            ],
        ),
        out_shape=[jax.ShapeDtypeStruct((parts, rows, wide // 3), BF16)] * 3
        + [jax.ShapeDtypeStruct((parts, 1, wide // 3), F32)] * 2,
        compiler_params=params(),
        name="attend_back",
    )(low, high, codes, seg_row, projected, projected, projected, context, grad_context, lse)


def norm_forward(v):
    mean = jnp.mean(v, axis=-1, keepdims=True)
    centered = v - mean
    factor = lax.rsqrt(jnp.mean(centered * centered, axis=-1, keepdims=True) + EPS)
    return centered * factor, factor


def norm_back(inner, normed, factor):
    return factor * (
        inner
        - jnp.mean(inner, axis=-1, keepdims=True)
        - normed * jnp.mean(inner * normed, axis=-1, keepdims=True)
    )


def col_sum(v):
    return jnp.sum(v, axis=0, keepdims=True)


UNIT_STEP = 512


def rows_kernel(
    x_ref,
    ctx_ref,
    g_ref,
    wo_ref,
    up_ref,
    down_ref,
    vec_ref,
    bup_ref,
    out_ref,
    hid_ref,
    sec_ref,
    first_ref,
    gfirst_ref,
    act_ref,
    gup_ref,
    gctx_ref,
    sums_ref,
    upsum_ref,
    slope,
):
    parts, _, units = act_ref.shape

    @pl.when(pl.program_id(0) == 0)
    def _():
        sums_ref[...] = jnp.zeros_like(sums_ref)
        upsum_ref[...] = jnp.zeros_like(upsum_ref)

    b_o, gain_one, shift_one = vec_ref[0:1], vec_ref[1:2], vec_ref[2:3]
    b_down, gain_two, shift_two = vec_ref[3:4], vec_ref[4:5], vec_ref[5:6]
    first_sum = x_ref[...].astype(F32) + b_o
    for t in range(parts):
        first_sum = first_sum + dot_nt(ctx_ref[t], wo_ref[t, 0])
    normed_one, factor_one = norm_forward(first_sum)
    hidden = normed_one * gain_one + shift_one
    hidden_low = hidden.astype(BF16)
    hid_ref[...] = hidden_low
    second_sum = hidden + b_down
    for t in range(parts):
        for u in range(0, units, UNIT_STEP):
            at = slice(u, u + UNIT_STEP)
            up = dot_nn(hidden_low, up_ref[t, 0, :, at]) + bup_ref[t, :, at]
            half = 0.5 * (1.0 + lax.erf(up * 0.7071067811865476))
            active = (up * half).astype(BF16)
            act_ref[t, :, at] = active
            slope[t, :, at] = half + up * jnp.exp(-0.5 * up * up) * 0.3989422804014327
            second_sum = second_sum + dot_nt(active, down_ref[t, 0, :, at])
    normed_two, factor_two = norm_forward(second_sum)
    out_ref[...] = (normed_two * gain_two + shift_two).astype(BF16)
    grad_out = g_ref[...].astype(F32)
    grad_second = norm_back(grad_out * gain_two, normed_two, factor_two)
    second_low = grad_second.astype(BF16)
    sec_ref[...] = second_low
    grad_hidden = grad_second
    for t in range(parts):
        for u in range(0, units, UNIT_STEP):
            at = slice(u, u + UNIT_STEP)
            grad_up = (dot_nn(second_low, down_ref[t, 0, :, at]) * slope[t, :, at]).astype(BF16)
            gup_ref[t, :, at] = grad_up
            upsum_ref[t, :, at] += col_sum(grad_up.astype(F32))
            grad_hidden = grad_hidden + dot_nt(grad_up, up_ref[t, 0, :, at])
    grad_first = norm_back(grad_hidden * gain_one, normed_one, factor_one)
    gfirst_ref[...] = grad_first
    first_low = grad_first.astype(BF16)
    first_ref[...] = first_low
    for t in range(parts):
        gctx_ref[t] = dot_nn(first_low, wo_ref[t, 0]).astype(BF16)
    sums_ref[0:1] += col_sum(grad_first)
    sums_ref[1:2] += col_sum(grad_hidden * normed_one)
    sums_ref[2:3] += col_sum(grad_hidden)
    sums_ref[3:4] += col_sum(grad_second)
    sums_ref[4:5] += col_sum(grad_out * normed_two)
    sums_ref[5:6] += col_sum(grad_out)


def rows_pass(x, context, grads, weights, vectors, bias_up):
    rows, width = x.shape
    parts, _, _, units = weights.shape
    part_width = context.shape[2]
    step = min(256, rows)
    row = pl.BlockSpec((step, width), lambda i: (i, 0))
    split = pl.BlockSpec((parts, step, part_width), lambda i: (0, i, 0))
    wide = pl.BlockSpec((parts, step, units), lambda i: (0, i, 0))
    once = pl.Buffered(1)
    last = units // part_width - 1
    return pl.pallas_call(
        rows_kernel,
        grid=(rows // step,),
        in_specs=[
            row,
            split,
            row,
            pl.BlockSpec(
                (parts, 1, width, part_width), lambda i: (0, 0, 0, last), pipeline_mode=once
            ),
            pl.BlockSpec((parts, 1, width, units), lambda i: (0, 1, 0, 0), pipeline_mode=once),
            pl.BlockSpec((parts, 1, width, units), lambda i: (0, 2, 0, 0), pipeline_mode=once),
            pl.BlockSpec((8, width), lambda i: (0, 0)),
            pl.BlockSpec((parts, 1, units), lambda i: (0, 0, 0)),
        ],
        out_specs=[
            row,
            row,
            row,
            row,
            row,
            wide,
            wide,
            split,
            pl.BlockSpec((8, width), lambda i: (0, 0)),
            pl.BlockSpec((parts, 1, units), lambda i: (0, 0, 0)),
        ],
        out_shape=[
            jax.ShapeDtypeStruct((rows, width), BF16),
            jax.ShapeDtypeStruct((rows, width), BF16),
            jax.ShapeDtypeStruct((rows, width), BF16),
            jax.ShapeDtypeStruct((rows, width), BF16),
            jax.ShapeDtypeStruct((rows, width), F32),
            jax.ShapeDtypeStruct((parts, rows, units), BF16),
            jax.ShapeDtypeStruct((parts, rows, units), BF16),
            jax.ShapeDtypeStruct((parts, rows, part_width), BF16),
            jax.ShapeDtypeStruct((8, width), F32),
            jax.ShapeDtypeStruct((parts, 1, units), F32),
        ],
        scratch_shapes=[pltpu.VMEM((parts, step, units), F32)],
        compiler_params=params(),
        name="rows_pass",
    )(x, context, grads, weights, weights, weights, vectors, bias_up)


GRAD_STEP = 256


def outer_kernel(rows_ref, cols_ref, out_ref):
    width = rows_ref.shape[1]
    for m in range(0, width, GRAD_STEP):
        at = slice(m, m + GRAD_STEP)
        out_ref[0, at, :] = dot_tn(rows_ref[:, at], cols_ref[0]).astype(BF16)


def outer(left, right):
    rows, width = left.shape
    parts, _, units = right.shape
    return pl.pallas_call(
        outer_kernel,
        grid=(parts,),
        in_specs=[
            pl.BlockSpec((rows, width), lambda t: (0, 0)),
            pl.BlockSpec((1, rows, units), lambda t: (t, 0, 0)),
        ],
        out_specs=pl.BlockSpec((1, width, units), lambda t: (t, 0, 0)),
        out_shape=jax.ShapeDtypeStruct((parts, width, units), BF16),
        compiler_params=params(),
        name="outer",
    )(left, right)


def outer_four_kernel(x_ref, first_ref, q_ref, k_ref, v_ref, ctx_ref, out_ref):
    width = x_ref.shape[1]
    part_width = q_ref.shape[2]
    for m in range(0, width, GRAD_STEP):
        at = slice(m, m + GRAD_STEP)
        for n, cols in enumerate((q_ref, k_ref, v_ref, ctx_ref)):
            left = first_ref if n == 3 else x_ref
            part = dot_tn(left[:, at], cols[0])
            out_ref[0, at, n * part_width : (n + 1) * part_width] = part.astype(BF16)


def outer_four(x, first_low, grad_q, grad_k, grad_v, context):
    rows, width = x.shape
    parts, _, part_width = context.shape
    row = pl.BlockSpec((rows, width), lambda t: (0, 0))
    split = pl.BlockSpec((1, rows, part_width), lambda t: (t, 0, 0))
    return pl.pallas_call(
        outer_four_kernel,
        grid=(parts,),
        in_specs=[row, row, split, split, split, split],
        out_specs=pl.BlockSpec((1, width, 4 * part_width), lambda t: (t, 0, 0)),
        out_shape=jax.ShapeDtypeStruct((parts, width, 4 * part_width), BF16),
        compiler_params=params(),
        name="outer_four",
    )(x, first_low, grad_q, grad_k, grad_v, context)


def input_grad_kernel(base_ref, q_ref, k_ref, v_ref, w_ref, out_ref):
    parts, _, part_width = q_ref.shape
    total = base_ref[...]
    for t in range(parts):
        for c, cols in enumerate((q_ref, k_ref, v_ref)):
            at = slice(c * part_width, (c + 1) * part_width)
            total = total + dot_nt(cols[t], w_ref[t, 0, :, at])
    out_ref[...] = total.astype(out_ref.dtype)


def input_grad(grad_first, grad_q, grad_k, grad_v, weights):
    rows, width = grad_first.shape
    parts, _, part_width = grad_q.shape
    step = min(256, rows)
    row = pl.BlockSpec((step, width), lambda i: (i, 0))
    split = pl.BlockSpec((parts, step, part_width), lambda i: (0, i, 0))
    return pl.pallas_call(
        input_grad_kernel,
        grid=(rows // step,),
        in_specs=[
            row,
            split,
            split,
            split,
            pl.BlockSpec((parts, 1, width, 3 * part_width), lambda i: (0, 0, 0, 0)),
        ],
        out_specs=row,
        out_shape=jax.ShapeDtypeStruct((rows, width), BF16),
        compiler_params=params(),
        name="input_grad",
    )(grad_first, grad_q, grad_k, grad_v, weights)


LINE = 4


class Place:
    def __init__(self):
        dp = lax.axis_index("dp")
        self.y = lax.axis_index("tensor")
        self.core = lax.rem(dp, 2)
        self.x = lax.rem(lax.div(dp, 2), 2)
        self.z = lax.div(dp, 4)
        self.fx = lax.rem(self.x + 1 - self.core, 2)
        self.fy = lax.rem(self.y + self.core, 2)
        self.sx = lax.rem(self.x + self.core, 2)
        self.sy = lax.rem(self.y + 1 - self.core, 2)

    @staticmethod
    def at(z, x, core, y):
        return ((z * 2 + x) * 2 + core, y)

    def up(self):
        return self.at(self.z + 1, self.x, self.core, self.y)

    def down(self):
        return self.at(self.z - 1, self.x, self.core, self.y)

    def first(self):
        return self.at(self.z, self.fx, self.core, self.fy)

    def second(self):
        return self.at(self.z, self.sx, self.core, self.sy)

    def partner(self):
        return self.at(self.z, self.x, 1 - self.core, self.y)

    def across_y(self):
        return self.at(self.z, self.x, self.core, 1 - self.y)

    def greet(self):
        barrier = pltpu.get_barrier_semaphore()

        def signal(device):
            pl.semaphore_signal(
                barrier, inc=1, device_id=device, device_id_type=pl.DeviceIdType.MESH
            )

        signal(self.first())
        signal(self.second())
        signal(self.partner())

        @pl.when(self.z < LINE - 1)
        def _():
            signal(self.up())

        @pl.when(self.z > 0)
        def _():
            signal(self.down())

        inner = ((self.z > 0) & (self.z < LINE - 1)).astype(jnp.int32)
        pl.semaphore_wait(barrier, 4 + inner)


def remote(src, dst, sends, recvs, slot, device):
    return pltpu.make_async_remote_copy(
        src_ref=src,
        dst_ref=dst,
        send_sem=sends.at[slot],
        recv_sem=recvs.at[slot],
        device_id=device,
        device_id_type=pl.DeviceIdType.MESH,
    )


def gather_kernel(
    shard_ref, in_ref, grad_ref, w_ref, x_ref, g_ref, z_send, z_recv, s_send, s_recv, local_sem
):
    place = Place()
    z, x, y, core = place.z, place.x, place.y, place.core
    chunks = shard_ref.shape[0]
    place.greet()

    trades = []
    for n, (src, dst) in enumerate(((in_ref, x_ref), (grad_ref, g_ref))):
        copy = remote(
            src.at[1 - y], dst.at[y], s_send, s_recv, chunks * 8 + n, place.across_y()
        )
        trades.append(copy)
    trades[0].start()
    local = [
        pltpu.make_async_copy(in_ref.at[y], x_ref.at[y], local_sem.at[0]),
        pltpu.make_async_copy(grad_ref.at[y], g_ref.at[y], local_sem.at[1]),
    ]
    for k in range(chunks):
        local.append(
            pltpu.make_async_copy(
                shard_ref.at[k], w_ref.at[y, k, z, x, core], local_sem.at[2 + k]
            )
        )
    for copy in local:
        copy.start()

    def piece(k, zz):
        return w_ref.at[y, k, zz, x, core]

    def upward(k, d):
        zz = jnp.maximum(z - d + 1, 0)
        src = shard_ref.at[k] if d == 1 else piece(k, zz)
        return remote(src, piece(k, zz), z_send, z_recv, (k * 2) * LINE + d, place.up())

    def downward(k, d):
        zz = jnp.minimum(z + d - 1, LINE - 1)
        src = shard_ref.at[k] if d == 1 else piece(k, zz)
        return remote(src, piece(k, zz), z_send, z_recv, (k * 2 + 1) * LINE + d, place.down())

    def from_below(k, d):
        here = piece(k, jnp.maximum(z - d, 0))
        return remote(here, here, z_send, z_recv, (k * 2) * LINE + d, place.up())

    def from_above(k, d):
        here = piece(k, jnp.minimum(z + d, LINE - 1))
        return remote(here, here, z_send, z_recv, (k * 2 + 1) * LINE + d, place.down())

    def line(k, yy, xx, cc):
        return w_ref.at[yy, k, :, xx, cc]

    def square(k, n, yy, xx, device, cc=None):
        ref = line(k, yy, xx, core if cc is None else cc)
        return remote(ref, ref, s_send, s_recv, k * 8 + n, device)

    def out_first(k):
        return square(k, 0, y, x, place.first())

    def in_first(k):
        return square(k, 0, place.fy, place.fx, place.first())

    def out_second(k, n):
        yy, xx = (y, x) if n == 0 else (place.fy, place.fx)
        return square(k, 1 + n, yy, xx, place.second())

    def in_second(k, n):
        yy, xx = (place.sy, place.sx) if n == 0 else (1 - y, 1 - x)
        return square(k, 1 + n, yy, xx, place.second())

    corners = ((y, x), (place.fy, place.fx), (place.sy, place.sx), (1 - y, 1 - x))

    def out_partner(k, n):
        yy, xx = corners[n]
        return square(k, 3 + n, yy, xx, place.partner())

    def in_partner(k, n):
        yy, xx = corners[(0, 2, 1, 3)[n]]
        return square(k, 3 + n, yy, xx, place.partner(), 1 - core)

    for k in range(chunks):
        @pl.when(z < LINE - 1)
        def _():
            upward(k, 1).start()

        @pl.when(z > 0)
        def _():
            downward(k, 1).start()

    for copy in local:
        copy.wait()

    def relay(k):
        for d in range(1, LINE):
            @pl.when(z >= d)
            def _():
                from_below(k, d).wait_recv()

            if d < LINE - 1:
                @pl.when((z >= d) & (z < LINE - 1))
                def _():
                    upward(k, d + 1).start()

            @pl.when(z + d < LINE)
            def _():
                from_above(k, d).wait_recv()

            if d < LINE - 1:
                @pl.when((z + d < LINE) & (z > 0))
                def _():
                    downward(k, d + 1).start()
        out_first(k).start()
        out_second(k, 0).start()
        out_partner(k, 0).start()

    def pass_first(k):
        in_first(k).wait_recv()
        out_second(k, 1).start()
        out_partner(k, 1).start()

    def pass_second(k):
        for n in range(2):
            in_second(k, n).wait_recv()
            out_partner(k, 2 + n).start()

    for k in range(chunks + 2):
        if k < chunks:
            relay(k)
            if k == 0:
                trades[1].start()
        if 0 <= k - 1 < chunks:
            pass_first(k - 1)
        if 0 <= k - 2 < chunks:
            pass_second(k - 2)
    for k in range(chunks):
        for n in range(4):
            in_partner(k, n).wait_recv()
    for k in range(chunks):
        for d in range(1, LINE):
            @pl.when((z >= d - 1) & (z < LINE - 1))
            def _():
                upward(k, d).wait_send()

            @pl.when((z + d - 1 < LINE) & (z > 0))
            def _():
                downward(k, d).wait_send()
        out_first(k).wait_send()
        for n in range(2):
            out_second(k, n).wait_send()
        for n in range(4):
            out_partner(k, n).wait_send()
    for copy in trades:
        copy.wait()


def gather_all(shard, halves, grad_halves):
    chunks, own_rows, units = shard.shape
    parts, rows, width = halves.shape
    anywhere = pl.BlockSpec(memory_space=pl.ANY)
    local = pl.BlockSpec(memory_space=pltpu.VMEM)
    weights, x, grads = pl.pallas_call(
        gather_kernel,
        in_specs=[local] * 3,
        out_specs=[anywhere] * 3,
        out_shape=[
            jax.ShapeDtypeStruct((parts, chunks, LINE, 2, 2, own_rows, units), BF16),
            jax.ShapeDtypeStruct((parts, rows, width), BF16),
            jax.ShapeDtypeStruct((parts, rows, width), BF16),
        ],
        scratch_shapes=[
            pltpu.SemaphoreType.DMA((chunks * 2 * LINE,)),
            pltpu.SemaphoreType.DMA((chunks * 2 * LINE,)),
            pltpu.SemaphoreType.DMA((chunks * 8 + 2,)),
            pltpu.SemaphoreType.DMA((chunks * 8 + 2,)),
            pltpu.SemaphoreType.DMA((chunks + 2,)),
        ],
        compiler_params=params(collective_id=0, has_side_effects=True),
        name="gather_all",
    )(shard, halves, grad_halves)
    return (
        weights.reshape(parts, chunks, -1, units),
        x.reshape(parts * rows, width),
        grads.reshape(parts * rows, width),
    )


def reduce_kernel(
    a_ref,
    b_ref,
    c_ref,
    xg_ref,
    small_ref,
    out_ref,
    xr_ref,
    total_ref,
    p_buf,
    s_buf,
    f_buf,
    u_buf,
    d_buf,
    t_buf,
    z_send,
    z_recv,
    s_send,
    s_recv,
    t_send,
    t_recv,
    local_sem,
):
    place = Place()
    z, x, y, core = place.z, place.x, place.y, place.core
    grads = (a_ref, b_ref, c_ref)
    chunks = len(grads)
    corners = ((y, x), (place.fy, place.fx), (place.sy, place.sx), (1 - y, 1 - x))
    place.greet()

    def swap(k, n, src, dst, device):
        return remote(src, dst, s_send, s_recv, k * 8 + n, device)

    def to_partner(k, n):
        yy, xx = corners[n]
        return swap(
            k, n, grads[k].at[yy, :, xx, 1 - core], p_buf.at[k, yy, :, xx], place.partner()
        )

    def from_partner(k, n):
        yy, xx = corners[n]
        here = p_buf.at[k, yy, :, xx]
        return swap(k, (0, 2, 1, 3)[n], here, here, place.partner())

    def to_second(k, n):
        yy, xx = corners[2 + n]
        return swap(k, 4 + n, p_buf.at[k, yy, :, xx], s_buf.at[k, n], place.second())

    def to_first(k):
        return swap(k, 6, s_buf.at[k, 1], f_buf.at[k], place.first())

    def up_copy(k, tt):
        src = u_buf.at[k, tt]
        return remote(src, src, z_send, z_recv, (k * 2) * LINE + tt, place.up())

    def down_copy(k, tt):
        src = d_buf.at[k, tt]
        return remote(src, src, z_send, z_recv, (k * 2 + 1) * LINE + tt, place.down())

    def small_copy(n, src, dst, device):
        return remote(src, dst, t_send, t_recv, n, device)

    over_x = place.at(z, 1 - x, core, y)
    hops = (
        small_copy(0, small_ref, t_buf.at[0], place.partner()),
        small_copy(1, t_buf.at[1], t_buf.at[2], over_x),
        small_copy(2, t_buf.at[3], t_buf.at[4], place.across_y()),
    )

    def small_up(d):
        piece = t_buf.at[5 + jnp.maximum(z - d + 1, 0)]
        return small_copy(2 + d, piece, piece, place.up())

    def small_down(d):
        piece = t_buf.at[5 + jnp.minimum(z + d - 1, LINE - 1)]
        return small_copy(2 + LINE + d, piece, piece, place.down())

    def small_below(d):
        piece = t_buf.at[5 + jnp.maximum(z - d, 0)]
        return small_copy(2 + d, piece, piece, place.up())

    def small_above(d):
        piece = t_buf.at[5 + jnp.minimum(z + d, LINE - 1)]
        return small_copy(2 + LINE + d, piece, piece, place.down())

    def small_step(step):
        if step == 0:
            hops[0].start()
        elif step == 1:
            hops[0].wait_recv()
            t_buf[1] = small_ref[...] + t_buf[0]
            hops[1].start()
        elif step == 2:
            hops[1].wait_recv()
            t_buf[3] = t_buf[1] + t_buf[2]
            hops[2].start()
        elif step == 3:
            hops[2].wait_recv()
            t_buf[5 + z] = t_buf[3] + t_buf[4]

            @pl.when(z < LINE - 1)
            def _():
                small_up(1).start()

            @pl.when(z > 0)
            def _():
                small_down(1).start()
        elif step == 4:
            for d in range(1, LINE):
                @pl.when(z >= d)
                def _():
                    small_below(d).wait_recv()

                if d < LINE - 1:
                    @pl.when((z >= d) & (z < LINE - 1))
                    def _():
                        small_up(d + 1).start()

                @pl.when(z + d < LINE)
                def _():
                    small_above(d).wait_recv()

                if d < LINE - 1:
                    @pl.when((z + d < LINE) & (z > 0))
                    def _():
                        small_down(d + 1).start()
            total_ref[...] = (t_buf[5] + t_buf[6]) + (t_buf[7] + t_buf[8])

    trade = remote(
        xg_ref.at[1 - y], xr_ref.at[y], t_send, t_recv, 3 + 2 * LINE, place.across_y()
    )
    arrive = remote(
        xg_ref.at[1 - y], xr_ref.at[1 - y], t_send, t_recv, 3 + 2 * LINE, place.across_y()
    )
    keep = pltpu.make_async_copy(xg_ref.at[y], xr_ref.at[y], local_sem.at[0])

    def accumulate(target, other):
        @pl.loop(0, LINE)
        def _(i):
            target[i] = target[i] + other[i]

    def stage_partner(k):
        for n in (3, 2, 1, 0):
            yy, xx = corners[n]
            from_partner(k, n).wait_recv()
            accumulate(p_buf.at[k, yy, :, xx], grads[k].at[yy, :, xx, core])
            if n >= 2:
                to_second(k, n - 2).start()

    def stage_second(k):
        for n in (1, 0):
            yy, xx = corners[n]
            to_second(k, n).wait_recv()
            accumulate(s_buf.at[k, n], p_buf.at[k, yy, :, xx])
            if n == 1:
                to_first(k).start()

    def stage_first(k):
        to_first(k).wait_recv()
        accumulate(f_buf.at[k], s_buf.at[k, 0])

    def stage_line(k):
        for tt_up, tt_down in ((3, 0), (2, 1), (1, 2)):
            @pl.when((z > 0) & (z <= tt_up))
            def _():
                up_copy(k, tt_up).wait_recv()

            @pl.when((z > 0) & (z < tt_up))
            def _():
                u_buf[k, tt_up] = u_buf[k, tt_up] + f_buf[k, tt_up]

            @pl.when(z == 0)
            def _():
                u_buf[k, tt_up] = f_buf[k, tt_up]

            @pl.when(z < tt_up)
            def _():
                up_copy(k, tt_up).start()

            @pl.when((z < LINE - 1) & (z >= tt_down))
            def _():
                down_copy(k, tt_down).wait_recv()

            @pl.when((z < LINE - 1) & (z > tt_down))
            def _():
                d_buf[k, tt_down] = d_buf[k, tt_down] + f_buf[k, tt_down]

            @pl.when(z == LINE - 1)
            def _():
                d_buf[k, tt_down] = f_buf[k, tt_down]

            @pl.when(z > tt_down)
            def _():
                down_copy(k, tt_down).start()

    def finish(k):
        own = f_buf[k, z].astype(F32)

        @pl.when(z == 0)
        def _():
            out_ref[k] = own + d_buf[k, 0].astype(F32)

        @pl.when(z == LINE - 1)
        def _():
            out_ref[k] = own + u_buf[k, LINE - 1].astype(F32)

        @pl.when((z > 0) & (z < LINE - 1))
        def _():
            out_ref[k] = own + u_buf[k, z].astype(F32) + d_buf[k, z].astype(F32)

    small_step(0)
    for k in range(chunks):
        for n in (3, 2, 1, 0):
            to_partner(k, n).start()
    keep.start()
    small_step(1)
    for i in range(chunks + 3):
        if i < chunks:
            stage_partner(i)
            if i == 0:
                trade.start()
        if 0 <= i - 1 < chunks:
            stage_second(i - 1)
        if 0 <= i - 2 < chunks:
            stage_first(i - 2)
        if 0 <= i - 3 < chunks:
            stage_line(i - 3)
        if i < 3:
            small_step(2 + i)
    for k in range(chunks):
        finish(k)

    keep.wait()
    trade.wait_send()
    arrive.wait_recv()
    for copy in hops:
        copy.wait_send()
    for d in range(1, LINE):
        @pl.when((z >= d - 1) & (z < LINE - 1))
        def _():
            small_up(d).wait_send()

        @pl.when((z + d - 1 < LINE) & (z > 0))
        def _():
            small_down(d).wait_send()
    for k in range(chunks):
        for n in range(4):
            to_partner(k, n).wait_send()
        for n in range(2):
            to_second(k, n).wait_send()
        to_first(k).wait_send()
        for tt in range(LINE):
            if tt > 0:
                @pl.when(z < tt)
                def _():
                    up_copy(k, tt).wait_send()

            if tt < LINE - 1:
                @pl.when(z > tt)
                def _():
                    down_copy(k, tt).wait_send()


def reduce_all(grads_a, grads_b, grads_c, halves, small):
    parts, width, units = grads_a.shape
    _, rows, model = halves.shape
    own_rows = width // (4 * LINE)
    chunks = 3
    folded = [g.reshape(parts, LINE, 2, 2, own_rows, units) for g in (grads_a, grads_b, grads_c)]
    small_rows = small.shape[0] // 128
    local = pl.BlockSpec(memory_space=pltpu.VMEM)
    line = (LINE, own_rows, units)
    own, x_rows, total = pl.pallas_call(
        reduce_kernel,
        in_specs=[local] * 5,
        out_specs=[local, pl.BlockSpec(memory_space=pl.ANY), local],
        out_shape=[
            jax.ShapeDtypeStruct((chunks, own_rows, units), F32),
            jax.ShapeDtypeStruct((parts, rows, model), BF16),
            jax.ShapeDtypeStruct((small_rows, 128), F32),
        ],
        scratch_shapes=[
            pltpu.VMEM((chunks, 2, LINE, 2, own_rows, units), BF16),
            pltpu.VMEM((chunks, 2) + line, BF16),
            pltpu.VMEM((chunks,) + line, BF16),
            pltpu.VMEM((chunks,) + line, BF16),
            pltpu.VMEM((chunks,) + line, BF16),
            pltpu.VMEM((5 + LINE, small_rows, 128), F32),
            pltpu.SemaphoreType.DMA((chunks * 2 * LINE,)),
            pltpu.SemaphoreType.DMA((chunks * 2 * LINE,)),
            pltpu.SemaphoreType.DMA((chunks * 8,)),
            pltpu.SemaphoreType.DMA((chunks * 8,)),
            pltpu.SemaphoreType.DMA((4 + 2 * LINE,)),
            pltpu.SemaphoreType.DMA((4 + 2 * LINE,)),
            pltpu.SemaphoreType.DMA((1,)),
        ],
        compiler_params=params(collective_id=1, has_side_effects=True),
        name="reduce_all",
    )(*folded, halves, small.reshape(small_rows, 128))
    return own, x_rows, total.reshape(-1)


def trade_in(halves):
    return lax.all_to_all(halves, "tensor", split_axis=0, concat_axis=1, tiled=True)[0]


def trade_out(whole):
    return lax.all_to_all(whole[None], "tensor", split_axis=1, concat_axis=0, tiled=True)


def gather_weights(shard):
    full = lax.all_gather(shard, "dp", axis=1, tiled=True)
    return lax.all_gather(full, "tensor", axis=0, tiled=False)


def scatter_grads(partial):
    own = lax.psum_scatter(partial, "tensor", scatter_dimension=0, tiled=False)
    return lax.psum_scatter(own, "dp", scatter_dimension=0, tiled=True)


def shards(
    inputs,
    seg_ids,
    keep_mask,
    w_qkv,
    b_qv,
    w_o,
    b_o,
    gain_one,
    shift_one,
    w_up,
    b_up,
    w_down,
    b_down,
    gain_two,
    shift_two,
    out_grad,
):
    parts = lax.axis_size("tensor")
    assert inputs.shape[0] == parts
    own_rows = w_qkv.shape[1]
    part_width = w_qkv.shape[2]
    units = w_up.shape[1]
    rank = lax.axis_index("tensor")

    shard_a = jnp.concatenate([w_qkv[0], w_qkv[1], w_qkv[2], w_o.T], axis=1)
    shard = jnp.stack([shard_a, w_up, w_down.T])
    linked = lax.axis_size("dp") == LINE * 4 and parts == 2
    if linked:
        weights, x, grads = gather_all(shard, inputs[:, 0], out_grad[:, 0])
    else:
        weights = gather_weights(shard)
        x = trade_in(inputs[:, 0])
        grads = trade_in(out_grad[:, 0])

    seg = lax.dynamic_index_in_dim(seg_ids[:, 0], rank, 0, keepdims=False)
    keep = lax.dynamic_index_in_dim(keep_mask[:, 0], rank, 0, keepdims=False)
    length = seg.shape[0]
    firsts, lasts = seg[::TILE], seg[TILE - 1 :: TILE]
    low = (jnp.sum(seg[None, :] < firsts[:, None], axis=1) // TILE).astype(jnp.int32)
    past = jnp.sum(seg[None, :] <= lasts[:, None], axis=1)
    high = ((past + TILE - 1) // TILE).astype(jnp.int32)
    codes = jnp.broadcast_to(jnp.where(keep == 1, seg, -1)[:, None], (length, 128))
    seg_row = seg[None, :]

    b_q = b_qv[0].reshape(parts, part_width)
    b_v = b_qv[1].reshape(parts, part_width)
    bias = jnp.concatenate([b_q, jnp.zeros_like(b_q), b_v], axis=1)[:, None, :]
    projected = project(x, weights, bias)
    context, lse = attend(projected, low, high, codes, seg_row)
    zero = jnp.zeros_like(b_o)
    vectors = jnp.stack([b_o, gain_one, shift_one, b_down, gain_two, shift_two, zero, zero])
    out, hidden_low, second_low, first_low, grad_first, active, grad_up, grad_context, sums, upsum = (
        rows_pass(x, context, grads, weights, vectors, b_up.reshape(parts, 1, units))
    )
    if linked:
        swapped = lax.ppermute(out.reshape(parts, -1, out.shape[1])[1 - rank], "tensor", ((0, 1), (1, 0)))
    partial_up = outer(hidden_low, grad_up)
    partial_down = outer(second_low, active)
    grad_q, grad_k, grad_v, qsum, vsum = attend_back(
        projected, context, grad_context, lse, low, high, codes, seg_row
    )
    partial_a = outer_four(x, first_low, grad_q, grad_k, grad_v, context)
    x_whole = input_grad(grad_first, grad_q, grad_k, grad_v, weights)
    small = jnp.concatenate(
        [sums[:6].reshape(-1), qsum.reshape(-1), vsum.reshape(-1), upsum.reshape(-1)]
    )
    if linked:
        halves = x_whole.reshape(parts, -1, x_whole.shape[1])
        own, x_rows, small = reduce_all(partial_a, partial_up, partial_down, halves, small)
        mine = out.reshape(parts, -1, out.shape[1])[rank]
        out_rows = jnp.where(rank == 0, jnp.stack([mine, swapped]), jnp.stack([swapped, mine]))
    else:
        own = jnp.stack(
            [scatter_grads(g).astype(F32) for g in (partial_a, partial_up, partial_down)]
        )
        x_rows = trade_out(x_whole)
        out_rows = trade_out(out)
        small = lax.psum(small, ("dp", "tensor"))
    width = sums.shape[1]
    vec = small[: 6 * width].reshape(6, width)
    flat = parts * part_width
    start = 6 * width
    q_all = lax.dynamic_slice(small, (start + rank * part_width,), (part_width,))
    v_all = lax.dynamic_slice(small, (start + flat + rank * part_width,), (part_width,))
    up_all = lax.dynamic_slice(small, (start + 2 * flat + rank * units,), (units,))

    own_a = own[0]
    qkv_grad = jnp.stack([own_a[:, c * part_width : (c + 1) * part_width] for c in range(3)])
    return (
        out_rows[:, None],
        x_rows.astype(F32)[:, None],
        qkv_grad,
        jnp.stack([q_all, v_all]),
        own_a[:, 3 * part_width :].T,
        vec[0],
        vec[1],
        vec[2],
        own[1],
        up_all,
        own[2].T,
        vec[3],
        vec[4],
        vec[5],
    )


def solution(mesh):
    placed = (
        P(None, "dp", "tensor", None),
        P(None, "dp", None),
        P(None, "dp", None),
        P(None, "dp", "tensor"),
        P(),
        P("tensor", "dp"),
        P(),
        P(),
        P(),
        P("dp", "tensor"),
        P(),
        P("tensor", "dp"),
        P(),
        P(),
        P(),
        P(None, "dp", "tensor", None),
    )
    return jax.shard_map(
        shards,
        mesh=mesh,
        in_specs=placed,
        out_specs=(
            P(None, "dp", "tensor", None),
            P(None, "dp", "tensor", None),
            P(None, "dp", "tensor"),
            P(None, "tensor"),
            P("tensor", "dp"),
            P(),
            P(),
            P(),
            P("dp", "tensor"),
            P("tensor"),
            P("tensor", "dp"),
            P(),
            P(),
            P(),
        ),
        check_vma=False,
    )
```

time: 1220 us -> 527 us (0.43)
  waiting for transfers between devices: 734 us -> 0.01 us
  Pallas kernels: 0 us -> 474 us
  matrix products: 246 us -> 0 us
  other arithmetic: 91.2 us -> 10.7 us
  blocking collectives: 65.9 us -> 0 us
  local copies, waits for them, and re-layouts: 59.4 us -> 15.2 us
  starting transfers between devices: 1.94 us -> 17.7 us
  between operations: 16.3 us -> 0.81 us
    pallas_call x0 -> x10, Pallas kernels: none -> 474 us  [the longest x1 200 us: reduce_all(): pl.pallas_call(reduce_kernel, in_specs=[local] * 5, out_specs=[local, pl....]
    reduce_scatter x11 -> x0, waiting for transfers between devices: 470 us -> none  [the longest x2 81 us: shards(): lax.psum_scatter(jnp.dot(active, full_down, preferred_element_type=jnp.fl...]
    dot_general x52 -> x0, matrix products: 246 us -> none  [the longest x4 25.1 us: per_block(): jnp.einsum('qhd,khd->hqk', g_rows, values, preferred_element_type=jnp.flo...]
    all_gather x11 -> x0, waiting for transfers between devices: 229 us -> none  [the longest x2 49.4 us: shards(): spread = lax.all_gather(hidden_low, 'tensor', axis=0, tiled=True)]
    reduce_sum x20 -> x1, other arithmetic: 45.5 us -> 0.22 us  [shards(): past = jnp.sum(seg[None, :] <= lasts[:, None], axis=1)]
    psum x1 -> x0, blocking collectives: 41 us -> none  [shards(): lax.psum((qv_full, small_totals[1], small_totals[2], small_totals[3], up_...]
    unnamed x24 -> x0, waiting for transfers between devices: 34.7 us -> none
    convert_element_type x11 -> x0, other arithmetic: 27.4 us -> none  [the longest x4 20.2 us: per_block(): grad_scores = (probs * (grad_probs - inner)).astype(jnp.bfloat16)]
  transfers between devices with their start and end apart: 23 -> 1, of which waited for: 21 -> 0; matrix products, arithmetic and copies ran while one was open for 22% -> 2% of each run, Pallas kernels for 0% -> 54%
where the time goes in v1:
time: 527 us; the launch traced here: 519 us
  Pallas kernels  474 us (90%)
  starting transfers between devices  17.7 us (3%)
  local copies, waits for them, and re-layouts  15.2 us (3%)
  other arithmetic  10.7 us (2%)
    pallas_call x1, Pallas kernels, reduce_all(): pl.pallas_call(reduce_kernel, in_specs=[local] * 5, out_specs=[local, pl....  200 us
    pallas_call x1, Pallas kernels, gather_all(): pl.pallas_call(gather_kernel, in_specs=[local] * 3, out_specs=[anywhere]...  102 us
    pallas_call x1, Pallas kernels, rows_pass(): pl.pallas_call(rows_kernel, grid=(rows // step,), in_specs=[row, split, r...  43.8 us
    pallas_call x1, Pallas kernels, attend_back(): pl.pallas_call(attend_back_kernel, grid_spec=pltpu.PrefetchScalarGridSpec...  41 us
    pallas_call x1, Pallas kernels, attend(): pl.pallas_call(attend_kernel, grid_spec=pltpu.PrefetchScalarGridSpec(num_...  40 us
    pallas_call x2, Pallas kernels, outer(): pl.pallas_call(outer_kernel, grid=(parts,), in_specs=[pl.BlockSpec((rows,...  18.1 us
    ppermute x1, starting transfers between devices, shards(): lax.ppermute(out.reshape(parts, -1, out.shape[1])[1 - rank], 'tensor', ((...  17.7 us
    pallas_call x1, Pallas kernels, outer_four(): pl.pallas_call(outer_four_kernel, grid=(parts,), in_specs=[row, row, spli...  11.7 us
  transfers between devices with their start and end apart: 1, of which 0 were waited for; matrix products, arithmetic and copies ran while one was open for 2% of the time, Pallas kernels for 54%

profile of v1, /device:TPU:0, one launch (start us, length us, event | category | flops | bytes accessed | tf_op | source)
XLA Modules:
  0.0 518.5 jit_solution(14676699707704642618)
XLA Ops:
  0.6 0.0 copy-start
  0.7 0.7 copy-done
  1.4 0.1 slice.81
  1.4 0.1 slice.80
  1.5 0.6 fusion.1.seg_ref
  2.1 0.8 slice_bitcast_fusion.9
  2.9 0.7 compare_reduce_fusion
  3.7 0.8 slice_reduce_fusion.1
  4.5 0.6 broadcast_in_dim.31.bias_ref
  5.1 0.7 stack.73
  5.8 0.7 stack.74
  6.5 0.7 stack.75
  7.2 0.7 stack.76
  7.9 0.7 stack.77
  8.6 0.7 stack.78
  9.3 0.2 convert_reduce_fusion
  9.5 0.5 and_select_fusion
  10.0 0.8 maximum_bitcast_fusion
  10.8 1.8 pad_maximum_fusion.shard_ref
  12.6 102.4 %gather_all.1 = (bf16[2,3,4,2,2,48,1536]{6,5,4,3,2,1,0:T(8,128)(2,1)}, bf16[2,512,768]{2,1,0:T(8,128)(2,1)}, bf16[2,512,768]{2,1,0:T(8,128)(2,1)}) custom-call(bf16[3,48,1536]{2,1,0:T(8,128)(2,1)} %pad_maximum_fusion.shard_ref, bf16[2,512,768]{2,1,0:T(8,128)(2,1)} %bitcast.83, bf16[2,512,768]{2,1,0:T(8,128)(2,1)} %bitcast.84), custom_call_target="tpu_custom_call" | custom-call | tf_op jit(solution)/shard_map/gather_all/pallas_call | solution.py:732
  115.0 7.9 %project.1.q_ref.k_ref.v_ref = bf16[2,1024,1152]{2,1,0:T(8,128)(2,1)} custom-call(bf16[1024,768]{1,0:T(8,128)(2,1)} %bitcast.79, bf16[2,3,768,1536]{3,2,1,0:T(8,128)(2,1)} %bitcast.71, f32[2,1,1152]{2,1,0:T(1,128)} %broadcast_in_dim.31.bias_ref), custom_call_target="tpu_custom_call" | custom-call | tf_op jit(solution)/shard_map/project/pallas_call | solution.py:45
  122.9 1.0 broadcast_in_dim.29.code_ref
  123.9 40.0 %attend.1 = (bf16[2,1024,384]{2,1,0:T(8,128)(2,1)}, f32[6,2,1024]{2,1,0:T(2,128)}) custom-call(s32[4]{0:T(128)} %get-tuple-element.113.low_ref, s32[4]{0:T(128)} %get-tuple-element.112.high_ref, s32[1024,128]{1,0:T(8,128)} %broadcast_in_dim.29.code_ref, s32[1,1024]{1,0:T(1,128)} %fusion.1.seg_ref, bf16[2,1024,1152]{2,1,0:T(8,128)(2,1)} %project.1.q_ref.k_ref.v_ref, ...), custom_call_target="tpu_custom_call" | custom-call | tf_op jit(solution)/shard_map/attend/pallas_call | solution.py:121
  163.8 0.6 stack.80.vec_ref
  164.5 43.8 %rows_pass.1 = (bf16[1024,768]{1,0:T(8,128)(2,1)}, bf16[1024,768]{1,0:T(8,128)(2,1)}, bf16[1024,768]{1,0:T(8,128)(2,1)}, bf16[1024,768]{1,0:T(8,128)(2,1)}, f32[...) custom-call(bf16[1024,768]{1,0:T(8,128)(2,1)} %bitcast.80, ...), custom_call_target="tpu_custom_call" | custom-call | tf_op jit(solution)/shard_map/rows_pass/pallas_call | solution.py:368
  208.3 1.5 dynamic-slice_bitcast_fusion.1
  209.8 17.7 %collective-permute-start = (bf16[512,768]{1,0:T(8,128)(2,1)S(1)}, bf16[512,768]{1,0:T(8,128)(2,1)}, u32[]{:S(2)}, u32[]{:S(2)}) collective-permute-start(bf16[512,768]{1,0:T(8,128)(2,1)S(1)} %get-tuple-element.93), channel_id=1, source_target_pairs={{0,1},{1,0},{2,3},{3,2},{4,5},{5,4},{6,7},{7,6},{8,9},{9,8},{10,11... | collective-permute-start | bytes 2359304 | tf_op jit(solution)/shard_map/ppermute | solution.py:1134
  227.5 41.0 %attend_back.1 = (bf16[2,1024,384]{2,1,0:T(8,128)(2,1)}, bf16[2,1024,384]{2,1,0:T(8,128)(2,1)}, bf16[2,1024,384]{2,1,0:T(8,128)(2,1)}, f32[2,1,384]{2,1,0:T(1,128)}, f32[2,1,384]{2,1,0:T(1,128)}) custom-call(s32[4]{0:T(128)} %get-tuple-element.113.low_ref, s32[4]{0:T(128)} %get-tuple-element.112.high_ref, s32[1024,128]{1,0:T(8,128)} %broadcast_in_dim.29.code_ref, ...), custom_call_target="tpu_custom_call" | custom-call | tf_op jit(solution)/shard_map/attend_back/pallas_call | solution.py:232
  268.5 11.7 %outer_four.1 = bf16[2,768,1536]{2,1,0:T(8,128)(2,1)} custom-call(bf16[1024,768]{1,0:T(8,128)(2,1)} %bitcast.81, bf16[1024,768]{1,0:T(8,128)(2,1)} %get-tuple-element.42.first_ref, bf16[2,1024,384]{2,1,0:T(8,128)(2,1)} %get-tuple-element.45.q_ref, bf16[2,1024,384]{2,1,0:T(8,128)(2,1)} %get-tuple-element.46.k_ref, ...), custom_call_target="tpu_custom_call" | custom-call | tf_op jit(solution)/shard_map/outer_four/pallas_call | solution.py:456
  280.3 0.0 copy-start.4
  280.3 9.3 %input_grad.1 = bf16[1024,768]{1,0:T(8,128)(2,1)} custom-call(f32[1024,768]{1,0:T(8,128)} %get-tuple-element.52.base_ref, bf16[2,1024,384]{2,1,0:T(8,128)(2,1)} %get-tuple-element.45.q_ref, bf16[2,1024,384]{2,1,0:T(8,128)(2,1)} %get-tuple-element.46.k_ref, bf16[2,1024,384]{2,1,0:T(8,128)(2,1)} %get-tuple-element.47.v_ref, bf16[2,3,768,1536]{3,2,1,0:T(8,128)(2,1)} %bitcast.75), custom_call_target="tpu_custom_call" | custom-call | tf_op jit(solution)/shard_map/input_grad/pallas_call | solution.py:483
  289.6 0.0 copy-done.7
  289.6 0.0 copy-done.6
  289.7 9.1 %outer.2 = bf16[2,768,1536]{2,1,0:T(8,128)(2,1)} custom-call(bf16[1024,768]{1,0:T(8,128)(2,1)} %get-tuple-element.48.rows_ref, bf16[2,1024,1536]{2,1,0:T(8,128)(2,1)} %get-tuple-element.49.cols_ref), custom_call_target="tpu_custom_call" | custom-call | tf_op jit(solution)/shard_map/outer/pallas_call | solution.py:426
  298.7 9.1 %outer.3 = bf16[2,768,1536]{2,1,0:T(8,128)(2,1)} custom-call(bf16[1024,768]{1,0:T(8,128)(2,1)} %get-tuple-element.50.rows_ref, bf16[2,1024,1536]{2,1,0:T(8,128)(2,1)} %get-tuple-element.51.cols_ref), custom_call_target="tpu_custom_call" | custom-call | tf_op jit(solution)/shard_map/outer/pallas_call | solution.py:426
  307.8 0.0 copy-done.5
  307.8 0.6 maximum_bitcast_fusion.1.small_ref
  308.4 199.9 %reduce_all.1 = (f32[3,48,1536]{2,1,0:T(8,128)}, bf16[2,512,768]{2,1,0:T(8,128)(2,1)}, f32[72,128]{1,0:T(8,128)}) custom-call(bf16[2,4,2,2,48,1536]{5,4,3,2,1,0:T(8,128)(2,1)} %bitcast.76, bf16[2,4,2,2,48,1536]{5,4,3,2,1,0:T(8,128)(2,1)} %bitcast.77, bf16[2,4,2,2,48,1536]{5,4,3,2,1,0:T(8,128)(2,1)} %bitcast.78, bf16[2,512,768]{2,1,0:T(8,128)(2,1)} %bitcast.82, ...), custom_call_target="tpu_custom_call" | custom-call | tf_op jit(solution)/shard_map/reduce_all/pallas_call | solution.py:1030
  508.4 2.1 slice_bitcast_fusion
  510.5 0.7 slice_bitcast_fusion.3
  511.1 0.1 fusion
  511.2 0.7 dynamic_slice.31
  511.9 0.6 pad_maximum_fusion.3
  512.5 0.7 pad_maximum_fusion.1
  513.2 0.6 slice_bitcast_fusion.10
  513.8 1.9 bitcast_convert_fusion
  515.7 0.0 collective-permute-done
  515.7 2.8 maximum_select_fusion
  (25 shorter events, 0.1 us)
Async XLA Ops:
  0.6 0.7 copy-start
  209.8 306.0 %collective-permute-start = (bf16[512,768]{1,0:T(8,128)(2,1)S(1)}, bf16[512,768]{1,0:T(8,128)(2,1)}, u32[]{:S(2)}, u32[]{:S(2)}) collective-permute-start(bf16[512,768]{1,0:T(8,128)(2,1)S(1)} %get-tuple-element.93), channel_id=1, source_target_pairs={{0,1},{1,0},{2,3},{3,2},{4,5},{5,4},{6,7},{7,6},{8,9},{9,8},{10,11... | collective-permute-start | bytes 2359304 | tf_op jit(solution)/shard_map/ppermute | solution.py:1134
  280.3 9.3 %copy-start.7 = (f32[2,1,384]{2,1,0:T(1,128)S(1)}, f32[2,1,384]{2,1,0:T(1,128)}, u32[]{:S(2)}) copy-start(f32[2,1,384]{2,1,0:T(1,128)} %get-tuple-element.55) | copy-start | bytes 9220
  280.3 9.4 %copy-start.6 = (f32[2,1,384]{2,1,0:T(1,128)S(1)}, f32[2,1,384]{2,1,0:T(1,128)}, u32[]{:S(2)}) copy-start(f32[2,1,384]{2,1,0:T(1,128)} %get-tuple-element.54) | copy-start | bytes 9220
  280.3 9.4 %copy-start.4 = (f32[8,768]{1,0:T(8,128)S(1)}, f32[8,768]{1,0:T(8,128)}, u32[]{:S(2)}) copy-start(f32[8,768]{1,0:T(8,128)} %get-tuple-element.53) | copy-start | bytes 73732
  298.7 9.1 %copy-start.5 = (f32[2,1,1536]{2,1,0:T(1,128)S(1)}, f32[2,1,1536]{2,1,0:T(1,128)}, u32[]{:S(2)}) copy-start(f32[2,1,1536]{2,1,0:T(1,128)} %get-tuple-element.56) | copy-start | bytes 36868
  508.3 2.8 copy-start.3
  508.3 5.5 %copy-start.2 = (bf16[2,512,768]{2,1,0:T(8,128)(2,1)S(1)}, bf16[2,512,768]{2,1,0:T(8,128)(2,1)}, u32[]{:S(2)}) copy-start(bf16[2,512,768]{2,1,0:T(8,128)(2,1)} %get-tuple-element.57) | copy-start | bytes 4718596
  515.7 2.8 copy-start.1

commit v2 on v1

--- a/solution.py
+++ b/solution.py
@@ -58,6 +58,8 @@
 
 
 TILE = 256
+DOC_MOST = 512
+REACH = -(-(DOC_MOST - 1) // TILE)
 
 
 def allowed_tile(code_ref, seg_ref, key0, query0):
@@ -355,9 +357,9 @@
     sums_ref[5:6] += col_sum(grad_out)
 
 
-def rows_pass(x, context, grads, weights, vectors, bias_up):
+def rows_pass(x, context, grads, first, rest, vectors, bias_up):
     rows, width = x.shape
-    parts, _, _, units = weights.shape
+    parts, _, _, units = rest.shape
     part_width = context.shape[2]
     step = min(256, rows)
     row = pl.BlockSpec((step, width), lambda i: (i, 0))
@@ -375,8 +377,8 @@
             pl.BlockSpec(
                 (parts, 1, width, part_width), lambda i: (0, 0, 0, last), pipeline_mode=once
             ),
+            pl.BlockSpec((parts, 1, width, units), lambda i: (0, 0, 0, 0), pipeline_mode=once),
             pl.BlockSpec((parts, 1, width, units), lambda i: (0, 1, 0, 0), pipeline_mode=once),
-            pl.BlockSpec((parts, 1, width, units), lambda i: (0, 2, 0, 0), pipeline_mode=once),
             pl.BlockSpec((8, width), lambda i: (0, 0)),
             pl.BlockSpec((parts, 1, units), lambda i: (0, 0, 0)),
         ],
@@ -407,7 +409,7 @@
         scratch_shapes=[pltpu.VMEM((parts, step, units), F32)],
         compiler_params=params(),
         name="rows_pass",
-    )(x, context, grads, weights, weights, weights, vectors, bias_up)
+    )(x, context, grads, first, rest, rest, vectors, bias_up)
 
 
 GRAD_STEP = 256
@@ -498,6 +500,7 @@
 
 
 LINE = 4
+REDUCE_MIXED = (1, 0, 1)
 
 
 class Place:
@@ -507,55 +510,48 @@
         self.core = lax.rem(dp, 2)
         self.x = lax.rem(lax.div(dp, 2), 2)
         self.z = lax.div(dp, 4)
-        self.fx = lax.rem(self.x + 1 - self.core, 2)
-        self.fy = lax.rem(self.y + self.core, 2)
-        self.sx = lax.rem(self.x + self.core, 2)
-        self.sy = lax.rem(self.y + 1 - self.core, 2)
 
     @staticmethod
     def at(z, x, core, y):
         return ((z * 2 + x) * 2 + core, y)
 
-    def up(self):
-        return self.at(self.z + 1, self.x, self.core, self.y)
-
-    def down(self):
-        return self.at(self.z - 1, self.x, self.core, self.y)
-
-    def first(self):
-        return self.at(self.z, self.fx, self.core, self.fy)
-
-    def second(self):
-        return self.at(self.z, self.sx, self.core, self.sy)
+    def corners(self, mixed, core=None):
+        core = self.core if core is None else core
+        side = 1 - (1 - core) * mixed
+        first = (lax.rem(self.y + side, 2), lax.rem(self.x + 1 - side, 2))
+        second = (lax.rem(self.y + 1 - side, 2), lax.rem(self.x + side, 2))
+        return ((self.y, self.x), first, second, (1 - self.y, 1 - self.x))
+
+    def chip(self, corner):
+        return self.at(self.z, corner[1], self.core, corner[0])
+
+    def along(self, o):
+        return lax.rem(self.z + o, LINE)
+
+    def back(self, o):
+        return lax.rem(self.z + LINE - o, LINE)
+
+    def line(self, o):
+        return self.at(self.along(o), self.x, self.core, self.y)
 
     def partner(self):
         return self.at(self.z, self.x, 1 - self.core, self.y)
 
+    def across_x(self):
+        return self.at(self.z, 1 - self.x, self.core, self.y)
+
     def across_y(self):
         return self.at(self.z, self.x, self.core, 1 - self.y)
 
     def greet(self):
         barrier = pltpu.get_barrier_semaphore()
-
-        def signal(device):
+        others = [self.across_x(), self.across_y(), self.partner()]
+        others += [self.line(o) for o in range(1, LINE)]
+        for device in others:
             pl.semaphore_signal(
                 barrier, inc=1, device_id=device, device_id_type=pl.DeviceIdType.MESH
             )
-
-        signal(self.first())
-        signal(self.second())
-        signal(self.partner())
-
-        @pl.when(self.z < LINE - 1)
-        def _():
-            signal(self.up())
-
-        @pl.when(self.z > 0)
-        def _():
-            signal(self.down())
-
-        inner = ((self.z > 0) & (self.z < LINE - 1)).astype(jnp.int32)
-        pl.semaphore_wait(barrier, 4 + inner)
+        pl.semaphore_wait(barrier, len(others))
 
 
 def remote(src, dst, sends, recvs, slot, device):
@@ -569,190 +565,284 @@
     )
 
 
+PER_PIECE = 8
+
+
 def gather_kernel(
-    shard_ref, in_ref, grad_ref, w_ref, x_ref, g_ref, z_send, z_recv, s_send, s_recv, local_sem
+    shard_ref,
+    in_ref,
+    bias_ref,
+    code_ref,
+    seg_ref,
+    first_ref,
+    rest_ref,
+    x_ref,
+    proj_ref,
+    ctx_ref,
+    lse_ref,
+    sends,
+    recvs,
+    local_sem,
+    top,
+    den,
+    acc,
 ):
     place = Place()
     z, x, y, core = place.z, place.x, place.y, place.core
     chunks = shard_ref.shape[0]
+    parts, rows, wide = proj_ref.shape
+    last = chunks * LINE * PER_PIECE
     place.greet()
 
-    trades = []
-    for n, (src, dst) in enumerate(((in_ref, x_ref), (grad_ref, g_ref))):
-        copy = remote(
-            src.at[1 - y], dst.at[y], s_send, s_recv, chunks * 8 + n, place.across_y()
-        )
-        trades.append(copy)
-    trades[0].start()
-    local = [
-        pltpu.make_async_copy(in_ref.at[y], x_ref.at[y], local_sem.at[0]),
-        pltpu.make_async_copy(grad_ref.at[y], g_ref.at[y], local_sem.at[1]),
-    ]
+    def copy(k, o, n, src, dst, device):
+        return remote(src, dst, sends, recvs, (k * LINE + o) * PER_PIECE + n, device)
+
+    def slot(k, yy, zz, xx, cc):
+        if isinstance(k, int) and k == 0:
+            return first_ref.at[yy, zz, xx, cc]
+        return rest_ref.at[yy, k - 1, zz, xx, cc]
+
+    def where(k, cc=None):
+        mixed = (k + 1) % 2 if isinstance(k, int) else lax.rem(k + 1, 2)
+        return place.corners(mixed, cc)
+
+    def held(k, o, corner, cc=core):
+        return slot(k, corner[0], place.back(o), corner[1], cc)
+
+    def to_line(k, o):
+        here = slot(k, y, z, x, core)
+        return copy(k, o, 0, shard_ref.at[k], here, place.line(o))
+
+    def from_line(k, o):
+        here = held(k, o, (y, x))
+        return copy(k, o, 0, here, here, place.line(o))
+
+    def hop(k, o, n, corner, device):
+        here = held(k, o, where(k)[corner])
+        return copy(k, o, n, here, here, device)
+
+    def to_first(k, o):
+        return hop(k, o, 1, 0, place.chip(where(k)[1]))
+
+    def from_first(k, o):
+        return hop(k, o, 1, 1, place.chip(where(k)[1]))
+
+    def to_second(k, o, n):
+        return hop(k, o, 2 + n, n, place.chip(where(k)[2]))
+
+    def from_second(k, o, n):
+        return hop(k, o, 2 + n, 2 + n, place.chip(where(k)[2]))
+
+    def to_partner(k, o, n):
+        return hop(k, o, 4 + n, n, place.partner())
+
+    def from_partner(k, o, n):
+        here = held(k, o, where(k, 1 - core)[n], 1 - core)
+        return copy(k, o, 4 + n, here, here, place.partner())
+
+    trade = remote(in_ref.at[1 - y], x_ref.at[y], sends, recvs, last, place.across_y())
+    arrive = remote(in_ref.at[y], x_ref.at[1 - y], sends, recvs, last, place.across_y())
+    local = [pltpu.make_async_copy(in_ref.at[y], x_ref.at[y], local_sem.at[chunks])]
     for k in range(chunks):
-        local.append(
-            pltpu.make_async_copy(
-                shard_ref.at[k], w_ref.at[y, k, z, x, core], local_sem.at[2 + k]
-            )
-        )
-    for copy in local:
-        copy.start()
-
-    def piece(k, zz):
-        return w_ref.at[y, k, zz, x, core]
-
-    def upward(k, d):
-        zz = jnp.maximum(z - d + 1, 0)
-        src = shard_ref.at[k] if d == 1 else piece(k, zz)
-        return remote(src, piece(k, zz), z_send, z_recv, (k * 2) * LINE + d, place.up())
-
-    def downward(k, d):
-        zz = jnp.minimum(z + d - 1, LINE - 1)
-        src = shard_ref.at[k] if d == 1 else piece(k, zz)
-        return remote(src, piece(k, zz), z_send, z_recv, (k * 2 + 1) * LINE + d, place.down())
-
-    def from_below(k, d):
-        here = piece(k, jnp.maximum(z - d, 0))
-        return remote(here, here, z_send, z_recv, (k * 2) * LINE + d, place.up())
-
-    def from_above(k, d):
-        here = piece(k, jnp.minimum(z + d, LINE - 1))
-        return remote(here, here, z_send, z_recv, (k * 2 + 1) * LINE + d, place.down())
-
-    def line(k, yy, xx, cc):
-        return w_ref.at[yy, k, :, xx, cc]
-
-    def square(k, n, yy, xx, device, cc=None):
-        ref = line(k, yy, xx, core if cc is None else cc)
-        return remote(ref, ref, s_send, s_recv, k * 8 + n, device)
-
-    def out_first(k):
-        return square(k, 0, y, x, place.first())
-
-    def in_first(k):
-        return square(k, 0, place.fy, place.fx, place.first())
-
-    def out_second(k, n):
-        yy, xx = (y, x) if n == 0 else (place.fy, place.fx)
-        return square(k, 1 + n, yy, xx, place.second())
-
-    def in_second(k, n):
-        yy, xx = (place.sy, place.sx) if n == 0 else (1 - y, 1 - x)
-        return square(k, 1 + n, yy, xx, place.second())
-
-    corners = ((y, x), (place.fy, place.fx), (place.sy, place.sx), (1 - y, 1 - x))
-
-    def out_partner(k, n):
-        yy, xx = corners[n]
-        return square(k, 3 + n, yy, xx, place.partner())
-
-    def in_partner(k, n):
-        yy, xx = corners[(0, 2, 1, 3)[n]]
-        return square(k, 3 + n, yy, xx, place.partner(), 1 - core)
-
+        own = slot(k, y, z, x, core)
+        local.append(pltpu.make_async_copy(shard_ref.at[k], own, local_sem.at[k]))
+    for part in local:
+        part.start()
     for k in range(chunks):
-        @pl.when(z < LINE - 1)
+        for o in (2, 1, 3):
+            to_line(k, o).start()
+    for part in local:
+        part.wait()
+
+    def start_line(k, o):
+        to_first(k, o).start()
+        to_second(k, o, 0).start()
+        to_partner(k, o, 0).start()
+
+    def arrive_first(k, o):
+        from_first(k, o).wait_recv()
+        to_second(k, o, 1).start()
+        to_partner(k, o, 1).start()
+
+    def arrive_second(k, o):
+        for n in range(2):
+            from_second(k, o, n).wait_recv()
+            to_partner(k, o, 2 + n).start()
+
+    order = (0, 1, 3, 2)
+    for i in range(LINE + 2):
+        if i < LINE:
+            if order[i] > 0:
+                from_line(0, order[i]).wait_recv()
+            start_line(0, order[i])
+            if i == 0:
+                trade.start()
+        if 0 <= i - 1 < LINE:
+            arrive_first(0, order[i - 1])
+        if 0 <= i - 2 < LINE:
+            arrive_second(0, order[i - 2])
+    arrive.wait_recv()
+    for o in order:
+        for n in range(4):
+            from_partner(0, o, n).wait_recv()
+
+    step = 256
+    for t in range(parts):
+        @pl.loop(0, rows // step)
+        def _(i):
+            half = lax.div(i, 2)
+            row0 = pl.multiple_of(lax.rem(i, 2) * step, step)
+            left = x_ref[half, pl.ds(row0, step), :]
+            right = first_ref[t, :, :, :, :, :wide].reshape(-1, wide)
+            value = dot_nn(left, right) + bias_ref[t]
+            proj_ref[t, pl.ds(pl.multiple_of(i * step, step), step), :] = value.astype(BF16)
+
+    lanes = 128
+    groups = wide // 3 // lanes
+    heads = lanes // HEAD_DIM
+    tiles = rows // TILE
+    masks = head_masks(lanes)
+
+    def attend_slice(i):
+        group = lax.div(i, tiles)
+        qi = lax.rem(i, tiles)
+        t = lax.div(group, groups)
+        j = lax.rem(group, groups)
+        query0 = pl.multiple_of(qi * TILE, TILE)
+
+        def lane(c):
+            return pl.ds(pl.multiple_of((c * groups + j) * lanes, lanes), lanes)
+
+        queries = proj_ref[t, pl.ds(query0, TILE), lane(0)] * BF16(0.125)
+        each = [queries * masks[h] for h in range(heads)]
+        top[...] = jnp.full_like(top, -1e30)
+        den[...] = jnp.zeros_like(den)
+        acc[...] = jnp.zeros_like(acc)
+
+        @pl.loop(jnp.maximum(qi - REACH, 0), jnp.minimum(qi + REACH + 1, tiles))
+        def _(ki):
+            key0 = pl.multiple_of(ki * TILE, TILE)
+            allowed = allowed_tile(code_ref, seg_ref, key0, query0)
+            keys = proj_ref[t, pl.ds(key0, TILE), lane(1)]
+            values_t = proj_ref[t, pl.ds(key0, TILE), lane(2)].T
+            for h in range(heads):
+                scores = jnp.where(allowed, dot_nt(keys, each[h]), -1e30)
+                old = top[h]
+                new = jnp.maximum(old, jnp.max(scores, axis=0, keepdims=True))
+                expo = jnp.exp(scores - new)
+                shrink = jnp.exp(old - new)
+                top[h] = new
+                den[h] = den[h] * shrink + jnp.sum(expo, axis=0, keepdims=True)
+                part = dot_nn(values_t[h * HEAD_DIM : (h + 1) * HEAD_DIM], expo.astype(BF16))
+                acc[h] = acc[h] * shrink + part
+
+        both = jnp.concatenate([acc[h] / den[h] for h in range(heads)], axis=0)
+        ctx_ref[t, pl.ds(query0, TILE), lane(0)] = both.astype(BF16).T
+        for h in range(heads):
+            lse_ref[group, h : h + 1, pl.ds(query0, TILE)] = top[h] + jnp.log(den[h])
+
+    count = (chunks - 1) * LINE
+    slices = parts * groups * tiles
+    share = slices // count
+
+    def split(p):
+        k = 1 + lax.div(p, LINE)
+        r = lax.rem(p, LINE)
+        return k, jnp.where(r < 2, r, 5 - r)
+
+    @pl.loop(0, count + 2)
+    def _(p):
+        @pl.when(p < count)
         def _():
-            upward(k, 1).start()
-
-        @pl.when(z > 0)
+            k, o = split(p)
+
+            @pl.when(o > 0)
+            def _():
+                from_line(k, o).wait_recv()
+
+            start_line(k, o)
+
+        @pl.when((p >= 1) & (p <= count))
         def _():
-            downward(k, 1).start()
-
-    for copy in local:
-        copy.wait()
-
-    def relay(k):
-        for d in range(1, LINE):
-            @pl.when(z >= d)
-            def _():
-                from_below(k, d).wait_recv()
-
-            if d < LINE - 1:
-                @pl.when((z >= d) & (z < LINE - 1))
-                def _():
-                    upward(k, d + 1).start()
-
-            @pl.when(z + d < LINE)
-            def _():
-                from_above(k, d).wait_recv()
-
-            if d < LINE - 1:
-                @pl.when((z + d < LINE) & (z > 0))
-                def _():
-                    downward(k, d + 1).start()
-        out_first(k).start()
-        out_second(k, 0).start()
-        out_partner(k, 0).start()
-
-    def pass_first(k):
-        in_first(k).wait_recv()
-        out_second(k, 1).start()
-        out_partner(k, 1).start()
-
-    def pass_second(k):
+            arrive_first(*split(p - 1))
+
+        @pl.when(p >= 2)
+        def _():
+            arrive_second(*split(p - 2))
+
+        @pl.when(p < count)
+        def _():
+            @pl.loop(0, share)
+            def _(n):
+                attend_slice(p * share + n)
+
+    @pl.loop(0, count)
+    def _(p):
+        k, o = split(p)
+        for n in range(4):
+            from_partner(k, o, n).wait_recv()
+
+    @pl.loop(0, count)
+    def _(p):
+        k, o = split(p)
+
+        @pl.when(o > 0)
+        def _():
+            to_line(k, o).wait_send()
+
+        to_first(k, o).wait_send()
         for n in range(2):
-            in_second(k, n).wait_recv()
-            out_partner(k, 2 + n).start()
-
-    for k in range(chunks + 2):
-        if k < chunks:
-            relay(k)
-            if k == 0:
-                trades[1].start()
-        if 0 <= k - 1 < chunks:
-            pass_first(k - 1)
-        if 0 <= k - 2 < chunks:
-            pass_second(k - 2)
-    for k in range(chunks):
+            to_second(k, o, n).wait_send()
         for n in range(4):
-            in_partner(k, n).wait_recv()
-    for k in range(chunks):
-        for d in range(1, LINE):
-            @pl.when((z >= d - 1) & (z < LINE - 1))
-            def _():
-                upward(k, d).wait_send()
-
-            @pl.when((z + d - 1 < LINE) & (z > 0))
-            def _():
-                downward(k, d).wait_send()
-        out_first(k).wait_send()
+            to_partner(k, o, n).wait_send()
+
+    for o in order:
+        if o > 0:
+            to_line(0, o).wait_send()
+        to_first(0, o).wait_send()
         for n in range(2):
-            out_second(k, n).wait_send()
+            to_second(0, o, n).wait_send()
         for n in range(4):
-            out_partner(k, n).wait_send()
-    for copy in trades:
-        copy.wait()
-
-
-def gather_all(shard, halves, grad_halves):
+            to_partner(0, o, n).wait_send()
+    trade.wait_send()
+
+
+def gather_all(shard, halves, bias, codes, seg_row):
     chunks, own_rows, units = shard.shape
     parts, rows, width = halves.shape
+    wide = bias.shape[-1]
+    length = parts * rows
+    groups = wide // 3 // 128
     anywhere = pl.BlockSpec(memory_space=pl.ANY)
     local = pl.BlockSpec(memory_space=pltpu.VMEM)
-    weights, x, grads = pl.pallas_call(
+    copies = chunks * LINE * PER_PIECE + 1
+    places = (LINE, 2, 2, own_rows, units)
+    first, rest, x, projected, context, lse = pl.pallas_call(
         gather_kernel,
-        in_specs=[local] * 3,
-        out_specs=[anywhere] * 3,
+        in_specs=[local] * 5,
+        out_specs=[local, anywhere, local, local, local, local],
         out_shape=[
-            jax.ShapeDtypeStruct((parts, chunks, LINE, 2, 2, own_rows, units), BF16),
+            jax.ShapeDtypeStruct((parts,) + places, BF16),
+            jax.ShapeDtypeStruct((parts, chunks - 1) + places, BF16),
             jax.ShapeDtypeStruct((parts, rows, width), BF16),
-            jax.ShapeDtypeStruct((parts, rows, width), BF16),
+            jax.ShapeDtypeStruct((parts, length, wide), BF16),
+            jax.ShapeDtypeStruct((parts, length, wide // 3), BF16),
+            jax.ShapeDtypeStruct((parts * groups, 2, length), F32),
         ],
         scratch_shapes=[
-            pltpu.SemaphoreType.DMA((chunks * 2 * LINE,)),
-            pltpu.SemaphoreType.DMA((chunks * 2 * LINE,)),
-            pltpu.SemaphoreType.DMA((chunks * 8 + 2,)),
-            pltpu.SemaphoreType.DMA((chunks * 8 + 2,)),
-            pltpu.SemaphoreType.DMA((chunks + 2,)),
+            pltpu.SemaphoreType.DMA((copies,)),
+            pltpu.SemaphoreType.DMA((copies,)),
+            pltpu.SemaphoreType.DMA((chunks + 1,)),
+            pltpu.VMEM((2, 1, TILE), F32),
+            pltpu.VMEM((2, 1, TILE), F32),
+            pltpu.VMEM((2, HEAD_DIM, TILE), F32),
         ],
         compiler_params=params(collective_id=0, has_side_effects=True),
         name="gather_all",
-    )(shard, halves, grad_halves)
-    return (
-        weights.reshape(parts, chunks, -1, units),
-        x.reshape(parts * rows, width),
-        grads.reshape(parts * rows, width),
-    )
+    )(shard, halves, bias, codes, seg_row)
+    first = first.reshape(parts, 1, -1, units)
+    rest = rest.reshape(parts, chunks - 1, -1, units)
+    return first, rest, x.reshape(length, width), projected, context, lse
 
 
 def reduce_kernel(
@@ -767,13 +857,10 @@
     p_buf,
     s_buf,
     f_buf,
-    u_buf,
-    d_buf,
+    z_buf,
     t_buf,
-    z_send,
-    z_recv,
-    s_send,
-    s_recv,
+    sends,
+    recvs,
     t_send,
     t_recv,
     local_sem,
@@ -782,63 +869,45 @@
     z, x, y, core = place.z, place.x, place.y, place.core
     grads = (a_ref, b_ref, c_ref)
     chunks = len(grads)
-    corners = ((y, x), (place.fy, place.fx), (place.sy, place.sx), (1 - y, 1 - x))
     place.greet()
 
-    def swap(k, n, src, dst, device):
-        return remote(src, dst, s_send, s_recv, k * 8 + n, device)
-
-    def to_partner(k, n):
-        yy, xx = corners[n]
-        return swap(
-            k, n, grads[k].at[yy, :, xx, 1 - core], p_buf.at[k, yy, :, xx], place.partner()
-        )
-
-    def from_partner(k, n):
-        yy, xx = corners[n]
-        here = p_buf.at[k, yy, :, xx]
-        return swap(k, (0, 2, 1, 3)[n], here, here, place.partner())
-
-    def to_second(k, n):
-        yy, xx = corners[2 + n]
-        return swap(k, 4 + n, p_buf.at[k, yy, :, xx], s_buf.at[k, n], place.second())
-
-    def to_first(k):
-        return swap(k, 6, s_buf.at[k, 1], f_buf.at[k], place.first())
-
-    def up_copy(k, tt):
-        src = u_buf.at[k, tt]
-        return remote(src, src, z_send, z_recv, (k * 2) * LINE + tt, place.up())
-
-    def down_copy(k, tt):
-        src = d_buf.at[k, tt]
-        return remote(src, src, z_send, z_recv, (k * 2 + 1) * LINE + tt, place.down())
+    def where(k):
+        return place.corners(REDUCE_MIXED[k])
+
+    def copy(k, o, n, src, dst, device):
+        return remote(src, dst, sends, recvs, (k * LINE + o) * PER_PIECE + n, device)
+
+    def to_partner(k, o):
+        src = grads[k].at[:, place.along(o), :, 1 - core]
+        return copy(k, o, 0, src, p_buf.at[k, o], place.partner())
+
+    def to_second(k, o, n):
+        yy, xx = where(k)[2 + n]
+        device = place.chip(where(k)[2])
+        return copy(k, o, 1 + n, p_buf.at[k, o, yy, xx], s_buf.at[k, o, n], device)
+
+    def to_first(k, o):
+        device = place.chip(where(k)[1])
+        return copy(k, o, 3, s_buf.at[k, o, 1], f_buf.at[k, o], device)
+
+    def to_line(k, o):
+        return copy(k, o, 4, f_buf.at[k, o], z_buf.at[k, o - 1], place.line(o))
 
     def small_copy(n, src, dst, device):
         return remote(src, dst, t_send, t_recv, n, device)
 
-    over_x = place.at(z, 1 - x, core, y)
     hops = (
         small_copy(0, small_ref, t_buf.at[0], place.partner()),
-        small_copy(1, t_buf.at[1], t_buf.at[2], over_x),
+        small_copy(1, t_buf.at[1], t_buf.at[2], place.across_x()),
         small_copy(2, t_buf.at[3], t_buf.at[4], place.across_y()),
     )
 
-    def small_up(d):
-        piece = t_buf.at[5 + jnp.maximum(z - d + 1, 0)]
-        return small_copy(2 + d, piece, piece, place.up())
-
-    def small_down(d):
-        piece = t_buf.at[5 + jnp.minimum(z + d - 1, LINE - 1)]
-        return small_copy(2 + LINE + d, piece, piece, place.down())
-
-    def small_below(d):
-        piece = t_buf.at[5 + jnp.maximum(z - d, 0)]
-        return small_copy(2 + d, piece, piece, place.up())
-
-    def small_above(d):
-        piece = t_buf.at[5 + jnp.minimum(z + d, LINE - 1)]
-        return small_copy(2 + LINE + d, piece, piece, place.down())
+    def small_line(o):
+        return small_copy(2 + o, t_buf.at[5 + z], t_buf.at[5 + z], place.line(o))
+
+    def small_from(o):
+        here = t_buf.at[5 + place.back(o)]
+        return small_copy(2 + o, here, here, place.line(o))
 
     def small_step(step):
         if step == 0:
@@ -854,168 +923,81 @@
         elif step == 3:
             hops[2].wait_recv()
             t_buf[5 + z] = t_buf[3] + t_buf[4]
-
-            @pl.when(z < LINE - 1)
-            def _():
-                small_up(1).start()
-
-            @pl.when(z > 0)
-            def _():
-                small_down(1).start()
+            for o in range(1, LINE):
+                small_line(o).start()
         elif step == 4:
-            for d in range(1, LINE):
-                @pl.when(z >= d)
-                def _():
-                    small_below(d).wait_recv()
-
-                if d < LINE - 1:
-                    @pl.when((z >= d) & (z < LINE - 1))
-                    def _():
-                        small_up(d + 1).start()
-
-                @pl.when(z + d < LINE)
-                def _():
-                    small_above(d).wait_recv()
-
-                if d < LINE - 1:
-                    @pl.when((z + d < LINE) & (z > 0))
-                    def _():
-                        small_down(d + 1).start()
+            for o in range(1, LINE):
+                small_from(o).wait_recv()
             total_ref[...] = (t_buf[5] + t_buf[6]) + (t_buf[7] + t_buf[8])
 
-    trade = remote(
-        xg_ref.at[1 - y], xr_ref.at[y], t_send, t_recv, 3 + 2 * LINE, place.across_y()
-    )
-    arrive = remote(
-        xg_ref.at[1 - y], xr_ref.at[1 - y], t_send, t_recv, 3 + 2 * LINE, place.across_y()
-    )
+    trade = small_copy(2 + LINE, xg_ref.at[1 - y], xr_ref.at[y], place.across_y())
+    arrive = small_copy(2 + LINE, xg_ref.at[1 - y], xr_ref.at[1 - y], place.across_y())
     keep = pltpu.make_async_copy(xg_ref.at[y], xr_ref.at[y], local_sem.at[0])
 
-    def accumulate(target, other):
-        @pl.loop(0, LINE)
-        def _(i):
-            target[i] = target[i] + other[i]
-
-    def stage_partner(k):
+    def stage_partner(k, o):
+        to_partner(k, o).wait_recv()
+        zz = place.along(o)
         for n in (3, 2, 1, 0):
-            yy, xx = corners[n]
-            from_partner(k, n).wait_recv()
-            accumulate(p_buf.at[k, yy, :, xx], grads[k].at[yy, :, xx, core])
+            yy, xx = where(k)[n]
+            p_buf[k, o, yy, xx] = p_buf[k, o, yy, xx] + grads[k][yy, zz, xx, core]
             if n >= 2:
-                to_second(k, n - 2).start()
-
-    def stage_second(k):
+                to_second(k, o, n - 2).start()
+
+    def stage_second(k, o):
         for n in (1, 0):
-            yy, xx = corners[n]
-            to_second(k, n).wait_recv()
-            accumulate(s_buf.at[k, n], p_buf.at[k, yy, :, xx])
+            yy, xx = where(k)[n]
+            to_second(k, o, n).wait_recv()
+            s_buf[k, o, n] = s_buf[k, o, n] + p_buf[k, o, yy, xx]
             if n == 1:
-                to_first(k).start()
-
-    def stage_first(k):
-        to_first(k).wait_recv()
-        accumulate(f_buf.at[k], s_buf.at[k, 0])
-
-    def stage_line(k):
-        for tt_up, tt_down in ((3, 0), (2, 1), (1, 2)):
-            @pl.when((z > 0) & (z <= tt_up))
-            def _():
-                up_copy(k, tt_up).wait_recv()
-
-            @pl.when((z > 0) & (z < tt_up))
-            def _():
-                u_buf[k, tt_up] = u_buf[k, tt_up] + f_buf[k, tt_up]
-
-            @pl.when(z == 0)
-            def _():
-                u_buf[k, tt_up] = f_buf[k, tt_up]
-
-            @pl.when(z < tt_up)
-            def _():
-                up_copy(k, tt_up).start()
-
-            @pl.when((z < LINE - 1) & (z >= tt_down))
-            def _():
-                down_copy(k, tt_down).wait_recv()
-
-            @pl.when((z < LINE - 1) & (z > tt_down))
-            def _():
-                d_buf[k, tt_down] = d_buf[k, tt_down] + f_buf[k, tt_down]
-
-            @pl.when(z == LINE - 1)
-            def _():
-                d_buf[k, tt_down] = f_buf[k, tt_down]
-
-            @pl.when(z > tt_down)
-            def _():
-                down_copy(k, tt_down).start()
+                to_first(k, o).start()
+
+    def stage_first(k, o):
+        to_first(k, o).wait_recv()
+        f_buf[k, o] = f_buf[k, o] + s_buf[k, o, 0]
+        if o > 0:
+            to_line(k, o).start()
 
     def finish(k):
-        own = f_buf[k, z].astype(F32)
-
-        @pl.when(z == 0)
-        def _():
-            out_ref[k] = own + d_buf[k, 0].astype(F32)
-
-        @pl.when(z == LINE - 1)
-        def _():
-            out_ref[k] = own + u_buf[k, LINE - 1].astype(F32)
-
-        @pl.when((z > 0) & (z < LINE - 1))
-        def _():
-            out_ref[k] = own + u_buf[k, z].astype(F32) + d_buf[k, z].astype(F32)
-
+        total = f_buf[k, 0].astype(F32)
+        for o in range(1, LINE):
+            to_line(k, o).wait_recv()
+            total = total + z_buf[k, o - 1].astype(F32)
+        out_ref[k] = total
+
+    steps = [(k, o) for k in range(chunks) for o in (2, 1, 3, 0)]
     small_step(0)
-    for k in range(chunks):
-        for n in (3, 2, 1, 0):
-            to_partner(k, n).start()
+    for k, o in steps:
+        to_partner(k, o).start()
     keep.start()
     small_step(1)
-    for i in range(chunks + 3):
-        if i < chunks:
-            stage_partner(i)
-            if i == 0:
-                trade.start()
-        if 0 <= i - 1 < chunks:
-            stage_second(i - 1)
-        if 0 <= i - 2 < chunks:
-            stage_first(i - 2)
-        if 0 <= i - 3 < chunks:
-            stage_line(i - 3)
-        if i < 3:
-            small_step(2 + i)
+    for i in range(len(steps) + 4):
+        if i < len(steps):
+            stage_partner(*steps[i])
+        if i == 1:
+            trade.start()
+        if 0 <= i - 2 < len(steps):
+            stage_second(*steps[i - 2])
+        if 0 <= i - 4 < len(steps):
+            stage_first(*steps[i - 4])
+        if i in (3, 6, 9):
+            small_step(1 + i // 3)
     for k in range(chunks):
         finish(k)
 
     keep.wait()
     trade.wait_send()
     arrive.wait_recv()
-    for copy in hops:
-        copy.wait_send()
-    for d in range(1, LINE):
-        @pl.when((z >= d - 1) & (z < LINE - 1))
-        def _():
-            small_up(d).wait_send()
-
-        @pl.when((z + d - 1 < LINE) & (z > 0))
-        def _():
-            small_down(d).wait_send()
-    for k in range(chunks):
-        for n in range(4):
-            to_partner(k, n).wait_send()
+    for part in hops:
+        part.wait_send()
+    for o in range(1, LINE):
+        small_line(o).wait_send()
+    for k, o in steps:
+        to_partner(k, o).wait_send()
         for n in range(2):
-            to_second(k, n).wait_send()
-        to_first(k).wait_send()
-        for tt in range(LINE):
-            if tt > 0:
-                @pl.when(z < tt)
-                def _():
-                    up_copy(k, tt).wait_send()
-
-            if tt < LINE - 1:
-                @pl.when(z > tt)
-                def _():
-                    down_copy(k, tt).wait_send()
+            to_second(k, o, n).wait_send()
+        to_first(k, o).wait_send()
+        if o > 0:
+            to_line(k, o).wait_send()
 
 
 def reduce_all(grads_a, grads_b, grads_c, halves, small):
@@ -1026,7 +1008,8 @@
     folded = [g.reshape(parts, LINE, 2, 2, own_rows, units) for g in (grads_a, grads_b, grads_c)]
     small_rows = small.shape[0] // 128
     local = pl.BlockSpec(memory_space=pltpu.VMEM)
-    line = (LINE, own_rows, units)
+    piece = (own_rows, units)
+    copies = chunks * LINE * PER_PIECE
     own, x_rows, total = pl.pallas_call(
         reduce_kernel,
         in_specs=[local] * 5,
@@ -1037,18 +1020,15 @@
             jax.ShapeDtypeStruct((small_rows, 128), F32),
         ],
         scratch_shapes=[
-            pltpu.VMEM((chunks, 2, LINE, 2, own_rows, units), BF16),
-            pltpu.VMEM((chunks, 2) + line, BF16),
-            pltpu.VMEM((chunks,) + line, BF16),
-            pltpu.VMEM((chunks,) + line, BF16),
-            pltpu.VMEM((chunks,) + line, BF16),
+            pltpu.VMEM((chunks, LINE, 2, 2) + piece, BF16),
+            pltpu.VMEM((chunks, LINE, 2) + piece, BF16),
+            pltpu.VMEM((chunks, LINE) + piece, BF16),
+            pltpu.VMEM((chunks, LINE - 1) + piece, BF16),
             pltpu.VMEM((5 + LINE, small_rows, 128), F32),
-            pltpu.SemaphoreType.DMA((chunks * 2 * LINE,)),
-            pltpu.SemaphoreType.DMA((chunks * 2 * LINE,)),
-            pltpu.SemaphoreType.DMA((chunks * 8,)),
-            pltpu.SemaphoreType.DMA((chunks * 8,)),
-            pltpu.SemaphoreType.DMA((4 + 2 * LINE,)),
-            pltpu.SemaphoreType.DMA((4 + 2 * LINE,)),
+            pltpu.SemaphoreType.DMA((copies,)),
+            pltpu.SemaphoreType.DMA((copies,)),
+            pltpu.SemaphoreType.DMA((3 + LINE,)),
+            pltpu.SemaphoreType.DMA((3 + LINE,)),
             pltpu.SemaphoreType.DMA((1,)),
         ],
         compiler_params=params(collective_id=1, has_side_effects=True),
@@ -1102,14 +1082,6 @@
 
     shard_a = jnp.concatenate([w_qkv[0], w_qkv[1], w_qkv[2], w_o.T], axis=1)
     shard = jnp.stack([shard_a, w_up, w_down.T])
-    linked = lax.axis_size("dp") == LINE * 4 and parts == 2
-    if linked:
-        weights, x, grads = gather_all(shard, inputs[:, 0], out_grad[:, 0])
-    else:
-        weights = gather_weights(shard)
-        x = trade_in(inputs[:, 0])
-        grads = trade_in(out_grad[:, 0])
-
     seg = lax.dynamic_index_in_dim(seg_ids[:, 0], rank, 0, keepdims=False)
     keep = lax.dynamic_index_in_dim(keep_mask[:, 0], rank, 0, keepdims=False)
     length = seg.shape[0]
@@ -1123,12 +1095,26 @@
     b_q = b_qv[0].reshape(parts, part_width)
     b_v = b_qv[1].reshape(parts, part_width)
     bias = jnp.concatenate([b_q, jnp.zeros_like(b_q), b_v], axis=1)[:, None, :]
-    projected = project(x, weights, bias)
-    context, lse = attend(projected, low, high, codes, seg_row)
+    linked = lax.axis_size("dp") == LINE * 4 and parts == 2
+    if linked:
+        first, rest, x, projected, context, lse = gather_all(
+            shard, inputs[:, 0], bias, codes, seg_row
+        )
+        theirs = lax.ppermute(out_grad[1 - rank, 0], "tensor", ((0, 1), (1, 0)))
+        own_half = out_grad[rank, 0]
+        grads = jnp.concatenate([own_half, theirs])
+        grads = jnp.where(rank == 0, grads, jnp.concatenate([theirs, own_half]))
+    else:
+        weights = gather_weights(shard)
+        first, rest = weights[:, :1], weights[:, 1:]
+        x = trade_in(inputs[:, 0])
+        grads = trade_in(out_grad[:, 0])
+        projected = project(x, first, bias)
+        context, lse = attend(projected, low, high, codes, seg_row)
     zero = jnp.zeros_like(b_o)
     vectors = jnp.stack([b_o, gain_one, shift_one, b_down, gain_two, shift_two, zero, zero])
     out, hidden_low, second_low, first_low, grad_first, active, grad_up, grad_context, sums, upsum = (
-        rows_pass(x, context, grads, weights, vectors, b_up.reshape(parts, 1, units))
+        rows_pass(x, context, grads, first, rest, vectors, b_up.reshape(parts, 1, units))
     )
     if linked:
         swapped = lax.ppermute(out.reshape(parts, -1, out.shape[1])[1 - rank], "tensor", ((0, 1), (1, 0)))
@@ -1138,7 +1124,7 @@
         projected, context, grad_context, lse, low, high, codes, seg_row
     )
     partial_a = outer_four(x, first_low, grad_q, grad_k, grad_v, context)
-    x_whole = input_grad(grad_first, grad_q, grad_k, grad_v, weights)
+    x_whole = input_grad(grad_first, grad_q, grad_k, grad_v, first)
     small = jnp.concatenate(
         [sums[:6].reshape(-1), qsum.reshape(-1), vsum.reshape(-1), upsum.reshape(-1)]
     )

time: 527 us -> 390 us (0.74); the launches traced: 519 us -> 390 us
  Pallas kernels: 474 us -> 348 us
    pallas_call x1, Pallas kernels: 200 us -> 89.5 us  [reduce_all(): pl.pallas_call(reduce_kernel, in_specs=[local] * 5, out_specs=[local, pl....]
    pallas_call x3 -> x1, Pallas kernels: 150 us -> 134 us  [gather_all(): pl.pallas_call(gather_kernel, in_specs=[local] * 5, out_specs=[local, any...]
  transfers between devices with their start and end apart: 1 -> 2, of which waited for: 0 -> 0; matrix products, arithmetic and copies ran while one was open for 2% -> 4% of each run, Pallas kernels for 54% -> 62%
where the time goes in v2:
time: 390 us
  Pallas kernels  348 us (89%)
  starting transfers between devices  20.2 us (5%)
  local copies, waits for them, and re-layouts  11.1 us (3%)
  other arithmetic  10.1 us (3%)
    pallas_call x1, Pallas kernels, gather_all(): pl.pallas_call(gather_kernel, in_specs=[local] * 5, out_specs=[local, any...  134 us
    pallas_call x1, Pallas kernels, reduce_all(): pl.pallas_call(reduce_kernel, in_specs=[local] * 5, out_specs=[local, pl....  89.5 us
    pallas_call x1, Pallas kernels, rows_pass(): pl.pallas_call(rows_kernel, grid=(rows // step,), in_specs=[row, split, r...  43.8 us
    pallas_call x1, Pallas kernels, attend_back(): pl.pallas_call(attend_back_kernel, grid_spec=pltpu.PrefetchScalarGridSpec...  41.1 us
    pallas_call x2, Pallas kernels, outer(): pl.pallas_call(outer_kernel, grid=(parts,), in_specs=[pl.BlockSpec((rows,...  18.2 us
    ppermute x1, starting transfers between devices, shards(): lax.ppermute(out.reshape(parts, -1, out.shape[1])[1 - rank], 'tensor', ((...  17.1 us
    pallas_call x1, Pallas kernels, outer_four(): pl.pallas_call(outer_four_kernel, grid=(parts,), in_specs=[row, row, spli...  11.6 us
    pallas_call x1, Pallas kernels, input_grad(): pl.pallas_call(input_grad_kernel, grid=(rows // step,), in_specs=[row, sp...  9.45 us
  transfers between devices with their start and end apart: 2, of which 0 were waited for; matrix products, arithmetic and copies ran while one was open for 4% of the time, Pallas kernels for 62%

profile of v2, /device:TPU:0, one launch (start us, length us, event | category | flops | bytes accessed | tf_op | source)
XLA Modules:
  0.0 389.9 jit_solution(7556111819300330460)
XLA Ops:
  0.7 0.0 copy-start
  0.7 0.0 copy-start.18
  0.7 0.0 copy-start.12
  0.7 0.0 copy-start.13
  0.7 0.0 copy-start.14
  0.7 0.0 copy-start.15
  0.7 0.0 copy-start.16
  0.7 0.0 copy-start.17
  0.8 1.6 dynamic-slice_bitcast_fusion.3
  2.4 3.1 collective-permute-start
  5.5 0.6 fusion.1.seg_ref
  6.0 0.1 slice.83
  6.1 0.1 slice.82
  6.2 0.0 copy-done.18
  6.3 0.0 copy-done.15
  6.5 0.6 broadcast_in_dim.29.bias_ref
  7.2 0.8 pad_maximum_fusion.shard_ref
  8.0 1.0 broadcast_in_dim.31.code_ref
  9.0 134.0 %gather_all.1 = (bf16[2,4,2,2,48,1536]{5,4,3,2,1,0:T(8,128)(2,1)}, bf16[2,2,4,2,2,48,1536]{6,5,4,3,2,1,0:T(8,128)(2,1)}, bf16[2,512,768]{2,1,0:T(8,128)(2,1)}, b...) custom-call(bf16[3,48,1536]{2,1,0:T(8,128)(2,1)} %pad_maximum_fusion.shard_ref, ...), custom_call_target="tpu_custom_call" | custom-call | tf_op jit(solution)/shard_map/gather_all/pallas_call | solution.py:820
  143.0 0.6 stack.80.vec_ref
  143.7 0.2 convert_reduce_fusion
  143.9 0.5 and_select_fusion
  144.4 0.0 collective-permute-done
  144.4 1.8 maximum_select_fusion.g_ref
  146.3 43.8 %rows_pass.1 = (bf16[1024,768]{1,0:T(8,128)(2,1)}, bf16[1024,768]{1,0:T(8,128)(2,1)}, bf16[1024,768]{1,0:T(8,128)(2,1)}, bf16[1024,768]{1,0:T(8,128)(2,1)}, f32[...) custom-call(bf16[1024,768]{1,0:T(8,128)(2,1)} %bitcast.81, ...), custom_call_target="tpu_custom_call" | custom-call | tf_op jit(solution)/shard_map/rows_pass/pallas_call | solution.py:370
  190.0 41.1 %attend_back.1 = (bf16[2,1024,384]{2,1,0:T(8,128)(2,1)}, bf16[2,1024,384]{2,1,0:T(8,128)(2,1)}, bf16[2,1024,384]{2,1,0:T(8,128)(2,1)}, f32[2,1,384]{2,1,0:T(1,128)}, f32[2,1,384]{2,1,0:T(1,128)}) custom-call(s32[4]{0:T(128)} %get-tuple-element.117.low_ref, s32[4]{0:T(128)} %get-tuple-element.116.high_ref, s32[1024,128]{1,0:T(8,128)} %broadcast_in_dim.31.code_ref, ...), custom_call_target="tpu_custom_call" | custom-call | tf_op jit(solution)/shard_map/attend_back/pallas_call | solution.py:234
  231.1 0.7 reduce.3
  231.8 0.7 reduce.4
  232.5 9.4 %input_grad.1 = bf16[1024,768]{1,0:T(8,128)(2,1)} custom-call(f32[1024,768]{1,0:T(8,128)} %get-tuple-element.54.base_ref, bf16[2,1024,384]{2,1,0:T(8,128)(2,1)} %get-tuple-element.47.q_ref, bf16[2,1024,384]{2,1,0:T(8,128)(2,1)} %get-tuple-element.48.k_ref, bf16[2,1024,384]{2,1,0:T(8,128)(2,1)} %get-tuple-element.49.v_ref, bf16[2,1,768,1536]{3,2,1,0:T(8,128)(2,1)} %bitcast.77), custom_call_target="tpu_custom_call" | custom-call | tf_op jit(solution)/shard_map/input_grad/pallas_call | solution.py:485
  242.0 11.6 %outer_four.1 = bf16[2,768,1536]{2,1,0:T(8,128)(2,1)} custom-call(bf16[1024,768]{1,0:T(8,128)(2,1)} %bitcast.82, bf16[1024,768]{1,0:T(8,128)(2,1)} %get-tuple-element.43.first_ref, bf16[2,1024,384]{2,1,0:T(8,128)(2,1)} %get-tuple-element.47.q_ref, bf16[2,1024,384]{2,1,0:T(8,128)(2,1)} %get-tuple-element.48.k_ref, ...), custom_call_target="tpu_custom_call" | custom-call | tf_op jit(solution)/shard_map/outer_four/pallas_call | solution.py:458
  253.6 0.1 dynamic-slice_bitcast_fusion.1
  253.7 0.6 copy-done.9
  254.3 17.1 %collective-permute-start.1 = (bf16[512,768]{1,0:T(8,128)(2,1)S(1)}, bf16[512,768]{1,0:T(8,128)(2,1)S(1)}, u32[]{:S(2)}, u32[]{:S(2)}) collective-permute-start(bf16[512,768]{1,0:T(8,128)(2,1)S(1)} %get-tuple-element.95), channel_id=1, source_target_pairs={{0,1},{1,0},{2,3},{3,2},{4,5},{5,4},{6,7},{7,6},{8,9},{9,8},{10,11... | collective-permute-start | bytes 2359304 | tf_op jit(solution)/shard_map/ppermute | solution.py:1120
  271.4 9.1 %outer.2 = bf16[2,768,1536]{2,1,0:T(8,128)(2,1)} custom-call(bf16[1024,768]{1,0:T(8,128)(2,1)} %get-tuple-element.50.rows_ref, bf16[2,1024,1536]{2,1,0:T(8,128)(2,1)} %get-tuple-element.51.cols_ref), custom_call_target="tpu_custom_call" | custom-call | tf_op jit(solution)/shard_map/outer/pallas_call | solution.py:428
  280.6 9.1 %outer.3 = bf16[2,768,1536]{2,1,0:T(8,128)(2,1)} custom-call(bf16[1024,768]{1,0:T(8,128)(2,1)} %get-tuple-element.52.rows_ref, bf16[2,1024,1536]{2,1,0:T(8,128)(2,1)} %get-tuple-element.53.cols_ref), custom_call_target="tpu_custom_call" | custom-call | tf_op jit(solution)/shard_map/outer/pallas_call | solution.py:428
  289.6 0.0 copy-done.10
  289.6 0.6 maximum_bitcast_fusion.1.small_ref
  290.2 89.5 %reduce_all.1 = (f32[3,48,1536]{2,1,0:T(8,128)}, bf16[2,512,768]{2,1,0:T(8,128)(2,1)}, f32[72,128]{1,0:T(8,128)}) custom-call(bf16[2,4,2,2,48,1536]{5,4,3,2,1,0:T(8,128)(2,1)} %bitcast.78, bf16[2,4,2,2,48,1536]{5,4,3,2,1,0:T(8,128)(2,1)} %bitcast.79, bf16[2,4,2,2,48,1536]{5,4,3,2,1,0:T(8,128)(2,1)} %bitcast.80, bf16[2,512,768]{2,1,0:T(8,128)(2,1)} %bitcast.83, ...), custom_call_target="tpu_custom_call" | custom-call | tf_op jit(solution)/shard_map/reduce_all/pallas_call | solution.py:1013
  379.8 0.9 fusion
  380.7 1.4 dynamic_slice.39
  382.1 2.0 slice_bitcast_fusion
  384.1 0.7 slice_bitcast_fusion.3
  384.7 0.6 pad_maximum_fusion.3
  385.3 0.7 pad_maximum_fusion.1
  386.0 0.6 slice_bitcast_fusion.10
  386.6 1.9 bitcast_convert_fusion
  388.5 0.0 collective-permute-done.1
  388.6 1.4 maximum_select_fusion.1
  (49 shorter events, 0.2 us)
Async XLA Ops:
  0.7 4.8 %copy-start = (s32[2,1,1024]{2,1,0:T(1,128)S(1)}, s32[2,1,1024]{2,1,0:T(1,128)}, u32[]{:S(2)}) copy-start(s32[2,1,1024]{2,1,0:T(1,128)} %param.17) | copy-start | bytes 24580
  0.7 5.6 %copy-start.18 = (s32[2,1,1024]{2,1,0:T(1,128)S(1)}, s32[2,1,1024]{2,1,0:T(1,128)}, u32[]{:S(2)}) copy-start(s32[2,1,1024]{2,1,0:T(1,128)} %param.18) | copy-start | bytes 24580
  0.7 5.6 %copy-start.12 = (f32[768]{0:T(1024)S(1)}, f32[768]{0:T(1024)}, u32[]{:S(2)}) copy-start(f32[768]{0:T(1024)} %param.22) | copy-start | bytes 9220
  0.7 5.6 %copy-start.13 = (f32[768]{0:T(1024)S(1)}, f32[768]{0:T(1024)}, u32[]{:S(2)}) copy-start(f32[768]{0:T(1024)} %param.23) | copy-start | bytes 9220
  0.7 5.6 %copy-start.14 = (f32[768]{0:T(1024)S(1)}, f32[768]{0:T(1024)}, u32[]{:S(2)}) copy-start(f32[768]{0:T(1024)} %param.24) | copy-start | bytes 9220
  0.7 5.6 %copy-start.15 = (f32[768]{0:T(1024)S(1)}, f32[768]{0:T(1024)}, u32[]{:S(2)}) copy-start(f32[768]{0:T(1024)} %param.28) | copy-start | bytes 9220
  0.7 5.6 %copy-start.16 = (f32[768]{0:T(1024)S(1)}, f32[768]{0:T(1024)}, u32[]{:S(2)}) copy-start(f32[768]{0:T(1024)} %param.29) | copy-start | bytes 9220
  0.7 5.6 %copy-start.17 = (f32[768]{0:T(1024)S(1)}, f32[768]{0:T(1024)}, u32[]{:S(2)}) copy-start(f32[768]{0:T(1024)} %param.30) | copy-start | bytes 9220
  0.7 5.7 %copy-start.11 = (f32[2,768]{1,0:T(2,128)S(1)}, f32[2,768]{1,0:T(2,128)}, u32[]{:S(2)}) copy-start(f32[2,768]{1,0:T(2,128)} %param.20) | copy-start | bytes 18436
  0.8 6.4 %copy-start.6 = (bf16[3,48,384]{2,1,0:T(8,128)(2,1)S(1)}, bf16[3,48,384]{2,1,0:T(8,128)(2,1)}, u32[]{:S(2)}) copy-start(bf16[3,48,384]{2,1,0:T(8,128)(2,1)} %param.19) | copy-start | bytes 331780
  0.8 6.4 %copy-start.7 = (bf16[384,48]{0,1:T(8,128)(2,1)S(1)}, bf16[384,48]{0,1:T(8,128)(2,1)}, u32[]{:S(2)}) copy-start(bf16[384,48]{0,1:T(8,128)(2,1)} %param.21) | copy-start | bytes 110596
  0.8 6.4 %copy-start.4 = (bf16[1536,48]{0,1:T(8,128)(2,1)S(1)}, bf16[1536,48]{0,1:T(8,128)(2,1)}, u32[]{:S(2)}) copy-start(bf16[1536,48]{0,1:T(8,128)(2,1)} %param.27) | copy-start | bytes 442372
  0.8 6.4 %copy-start.5 = (bf16[48,1536]{1,0:T(8,128)(2,1)S(1)}, bf16[48,1536]{1,0:T(8,128)(2,1)}, u32[]{:S(2)}) copy-start(bf16[48,1536]{1,0:T(8,128)(2,1)} %param.25) | copy-start | bytes 442372
  2.4 142.1 %collective-permute-start = (bf16[512,768]{1,0:T(8,128)(2,1)S(1)}, bf16[512,768]{1,0:T(8,128)(2,1)S(1)}, u32[]{:S(2)}, u32[]{:S(2)}) collective-permute-start(bf16[512,768]{1,0:T(8,128)(2,1)S(1)} %get-tuple-element.97), channel_id=1, source_target_pairs={{0,1},{1,0},{2,3},{3,2},{4,5},{5,4},{6,7},{7,6},{8,9},{9,8},{10,11... | collective-permute-start | bytes 2359304 | tf_op jit(solution)/shard_map/ppermute | solution.py:1103
  242.0 11.6 %copy-start.2 = (bf16[1024,768]{1,0:T(8,128)(2,1)S(1)}, bf16[1024,768]{1,0:T(8,128)(2,1)}, u32[]{:S(2)}) copy-start(bf16[1024,768]{1,0:T(8,128)(2,1)} %get-tuple-element.42) | copy-start | bytes 4718596
  253.6 0.7 copy-start.9
  254.3 134.2 %collective-permute-start.1 = (bf16[512,768]{1,0:T(8,128)(2,1)S(1)}, bf16[512,768]{1,0:T(8,128)(2,1)S(1)}, u32[]{:S(2)}, u32[]{:S(2)}) collective-permute-start(bf16[512,768]{1,0:T(8,128)(2,1)S(1)} %get-tuple-element.95), channel_id=1, source_target_pairs={{0,1},{1,0},{2,3},{3,2},{4,5},{5,4},{6,7},{7,6},{8,9},{9,8},{10,11... | collective-permute-start | bytes 2359304 | tf_op jit(solution)/shard_map/ppermute | solution.py:1120
  280.6 9.1 %copy-start.10 = (f32[2,1,1536]{2,1,0:T(1,128)S(1)}, f32[2,1,1536]{2,1,0:T(1,128)}, u32[]{:S(2)}) copy-start(f32[2,1,1536]{2,1,0:T(1,128)} %get-tuple-element.58) | copy-start | bytes 36868
  379.8 6.3 %copy-start.8 = (f32[72,128]{1,0:T(8,128)S(1)}, f32[72,128]{1,0:T(8,128)}, u32[]{:S(2)}) copy-start(f32[72,128]{1,0:T(8,128)} %get-tuple-element.61) | copy-start | bytes 110596
  379.8 6.9 %copy-start.3 = (bf16[2,512,768]{2,1,0:T(8,128)(2,1)S(1)}, bf16[2,512,768]{2,1,0:T(8,128)(2,1)}, u32[]{:S(2)}) copy-start(bf16[2,512,768]{2,1,0:T(8,128)(2,1)} %get-tuple-element.59) | copy-start | bytes 4718596
  388.6 1.4 copy-start.1

commit v3 on v2

--- a/solution.py
+++ b/solution.py
@@ -282,26 +282,93 @@
 UNIT_STEP = 512
 
 
+def forward_block(x, context, out_weight, up_weight, vec_ref, bup_ref, rows_at, refs):
+    normed_ref, factor_ref, act_ref, slope_ref = refs
+    parts, _, units = act_ref.shape
+    first_sum = x.astype(F32) + vec_ref[0:1]
+    for t in range(parts):
+        first_sum = first_sum + dot_nt(context(t), out_weight(t))
+    normed, factor = norm_forward(first_sum)
+    normed_ref[rows_at, :] = normed
+    factor_ref[rows_at, :] = jnp.broadcast_to(factor, (factor.shape[0], 128))
+    hidden_low = (normed * vec_ref[1:2] + vec_ref[2:3]).astype(BF16)
+    for t in range(parts):
+        for u in range(0, units, UNIT_STEP):
+            at = slice(u, u + UNIT_STEP)
+            up = dot_nn(hidden_low, up_weight(t, at)) + bup_ref[t, :, at]
+            half = 0.5 * (1.0 + lax.erf(up * 0.7071067811865476))
+            act_ref[t, rows_at, at] = (up * half).astype(BF16)
+            slope = half + up * jnp.exp(-0.5 * up * up) * 0.3989422804014327
+            slope_ref[t, rows_at, at] = slope
+
+
+def forward_kernel(x_ref, ctx_ref, wo_ref, up_ref, vec_ref, bup_ref, *refs):
+    forward_block(
+        x_ref[...],
+        lambda t: ctx_ref[t],
+        lambda t: wo_ref[t, 0],
+        lambda t, at: up_ref[t, 0, :, at],
+        vec_ref,
+        bup_ref,
+        slice(None),
+        refs,
+    )
+
+
+def forward_shapes(parts, rows, width, units):
+    return [
+        jax.ShapeDtypeStruct((rows, width), F32),
+        jax.ShapeDtypeStruct((rows, 128), F32),
+        jax.ShapeDtypeStruct((parts, rows, units), BF16),
+        jax.ShapeDtypeStruct((parts, rows, units), F32),
+    ]
+
+
+def rows_forward(x, context, first, rest, vectors, bias_up):
+    rows, width = x.shape
+    parts, _, _, units = rest.shape
+    part_width = context.shape[2]
+    step = min(256, rows)
+    last = units // part_width - 1
+    row = pl.BlockSpec((step, width), lambda i: (i, 0))
+    wide = pl.BlockSpec((parts, step, units), lambda i: (0, i, 0))
+    return pl.pallas_call(
+        forward_kernel,
+        grid=(rows // step,),
+        in_specs=[
+            row,
+            pl.BlockSpec((parts, step, part_width), lambda i: (0, i, 0)),
+            pl.BlockSpec((parts, 1, width, part_width), lambda i: (0, 0, 0, last)),
+            pl.BlockSpec((parts, 1, width, units), lambda i: (0, 0, 0, 0)),
+            pl.BlockSpec((8, width), lambda i: (0, 0)),
+            pl.BlockSpec((parts, 1, units), lambda i: (0, 0, 0)),
+        ],
+        out_specs=[row, pl.BlockSpec((step, 128), lambda i: (i, 0)), wide, wide],
+        out_shape=forward_shapes(parts, rows, width, units),
+        compiler_params=params(),
+        name="rows_forward",
+    )(x, context, first, rest, vectors, bias_up)
+
+
 def rows_kernel(
-    x_ref,
-    ctx_ref,
+    normed_ref,
+    factor_ref,
+    act_ref,
+    slope_ref,
     g_ref,
     wo_ref,
     up_ref,
     down_ref,
     vec_ref,
-    bup_ref,
     out_ref,
     hid_ref,
     sec_ref,
     first_ref,
     gfirst_ref,
-    act_ref,
     gup_ref,
     gctx_ref,
     sums_ref,
     upsum_ref,
-    slope,
 ):
     parts, _, units = act_ref.shape
 
@@ -310,25 +377,13 @@
         sums_ref[...] = jnp.zeros_like(sums_ref)
         upsum_ref[...] = jnp.zeros_like(upsum_ref)
 
-    b_o, gain_one, shift_one = vec_ref[0:1], vec_ref[1:2], vec_ref[2:3]
+    gain_one, shift_one = vec_ref[1:2], vec_ref[2:3]
     b_down, gain_two, shift_two = vec_ref[3:4], vec_ref[4:5], vec_ref[5:6]
-    first_sum = x_ref[...].astype(F32) + b_o
-    for t in range(parts):
-        first_sum = first_sum + dot_nt(ctx_ref[t], wo_ref[t, 0])
-    normed_one, factor_one = norm_forward(first_sum)
-    hidden = normed_one * gain_one + shift_one
-    hidden_low = hidden.astype(BF16)
-    hid_ref[...] = hidden_low
+    hidden = normed_ref[...] * gain_one + shift_one
+    hid_ref[...] = hidden.astype(BF16)
     second_sum = hidden + b_down
     for t in range(parts):
-        for u in range(0, units, UNIT_STEP):
-            at = slice(u, u + UNIT_STEP)
-            up = dot_nn(hidden_low, up_ref[t, 0, :, at]) + bup_ref[t, :, at]
-            half = 0.5 * (1.0 + lax.erf(up * 0.7071067811865476))
-            active = (up * half).astype(BF16)
-            act_ref[t, :, at] = active
-            slope[t, :, at] = half + up * jnp.exp(-0.5 * up * up) * 0.3989422804014327
-            second_sum = second_sum + dot_nt(active, down_ref[t, 0, :, at])
+        second_sum = second_sum + dot_nt(act_ref[t], down_ref[t, 0])
     normed_two, factor_two = norm_forward(second_sum)
     out_ref[...] = (normed_two * gain_two + shift_two).astype(BF16)
     grad_out = g_ref[...].astype(F32)
@@ -339,11 +394,12 @@
     for t in range(parts):
         for u in range(0, units, UNIT_STEP):
             at = slice(u, u + UNIT_STEP)
-            grad_up = (dot_nn(second_low, down_ref[t, 0, :, at]) * slope[t, :, at]).astype(BF16)
+            grad_up = (dot_nn(second_low, down_ref[t, 0, :, at]) * slope_ref[t, :, at]).astype(BF16)
             gup_ref[t, :, at] = grad_up
             upsum_ref[t, :, at] += col_sum(grad_up.astype(F32))
             grad_hidden = grad_hidden + dot_nt(grad_up, up_ref[t, 0, :, at])
-    grad_first = norm_back(grad_hidden * gain_one, normed_one, factor_one)
+    normed_one = normed_ref[...]
+    grad_first = norm_back(grad_hidden * gain_one, normed_one, factor_ref[:, 0:1])
     gfirst_ref[...] = grad_first
     first_low = grad_first.astype(BF16)
     first_ref[...] = first_low
@@ -357,10 +413,10 @@
     sums_ref[5:6] += col_sum(grad_out)
 
 
-def rows_pass(x, context, grads, first, rest, vectors, bias_up):
-    rows, width = x.shape
-    parts, _, _, units = rest.shape
-    part_width = context.shape[2]
+def rows_pass(normed, factor, active, slope, grads, first, rest, vectors):
+    rows, width = normed.shape
+    parts, _, units = active.shape
+    part_width = first.shape[3] // 4
     step = min(256, rows)
     row = pl.BlockSpec((step, width), lambda i: (i, 0))
     split = pl.BlockSpec((parts, step, part_width), lambda i: (0, i, 0))
@@ -372,7 +428,9 @@
         grid=(rows // step,),
         in_specs=[
             row,
-            split,
+            pl.BlockSpec((step, 128), lambda i: (i, 0)),
+            wide,
+            wide,
             row,
             pl.BlockSpec(
                 (parts, 1, width, part_width), lambda i: (0, 0, 0, last), pipeline_mode=once
@@ -380,7 +438,6 @@
             pl.BlockSpec((parts, 1, width, units), lambda i: (0, 0, 0, 0), pipeline_mode=once),
             pl.BlockSpec((parts, 1, width, units), lambda i: (0, 1, 0, 0), pipeline_mode=once),
             pl.BlockSpec((8, width), lambda i: (0, 0)),
-            pl.BlockSpec((parts, 1, units), lambda i: (0, 0, 0)),
         ],
         out_specs=[
             row,
@@ -388,7 +445,6 @@
             row,
             row,
             row,
-            wide,
             wide,
             split,
             pl.BlockSpec((8, width), lambda i: (0, 0)),
@@ -401,15 +457,13 @@
             jax.ShapeDtypeStruct((rows, width), BF16),
             jax.ShapeDtypeStruct((rows, width), F32),
             jax.ShapeDtypeStruct((parts, rows, units), BF16),
-            jax.ShapeDtypeStruct((parts, rows, units), BF16),
             jax.ShapeDtypeStruct((parts, rows, part_width), BF16),
             jax.ShapeDtypeStruct((8, width), F32),
             jax.ShapeDtypeStruct((parts, 1, units), F32),
         ],
-        scratch_shapes=[pltpu.VMEM((parts, step, units), F32)],
         compiler_params=params(),
         name="rows_pass",
-    )(x, context, grads, first, rest, rest, vectors, bias_up)
+    )(normed, factor, active, slope, grads, first, rest, rest, vectors)
 
 
 GRAD_STEP = 256
@@ -500,7 +554,7 @@
 
 
 LINE = 4
-REDUCE_MIXED = (1, 0, 1)
+CHUNK = 64
 
 
 class Place:
@@ -574,18 +628,34 @@
     bias_ref,
     code_ref,
     seg_ref,
+    docs_ref,
+    bars_ref,
+    vec_ref,
+    bup_ref,
+    grad_ref,
     first_ref,
-    rest_ref,
+    rest_out,
     x_ref,
+    g_ref,
     proj_ref,
     ctx_ref,
     lse_ref,
+    normed_out,
+    factor_out,
+    act_out,
+    slope_out,
+    rest_ref,
+    normed_buf,
+    factor_buf,
+    act_buf,
+    slope_buf,
     sends,
     recvs,
     local_sem,
-    top,
-    den,
-    acc,
+    rows_sem,
+    turned,
+    score_buf,
+    expo_buf,
 ):
     place = Place()
     z, x, y, core = place.z, place.x, place.y, place.core
@@ -603,7 +673,7 @@
         return rest_ref.at[yy, k - 1, zz, xx, cc]
 
     def where(k, cc=None):
-        mixed = (k + 1) % 2 if isinstance(k, int) else lax.rem(k + 1, 2)
+        mixed = k // 2 if isinstance(k, int) else lax.div(k, 2)
         return place.corners(mixed, cc)
 
     def held(k, o, corner, cc=core):
@@ -642,6 +712,12 @@
 
     trade = remote(in_ref.at[1 - y], x_ref.at[y], sends, recvs, last, place.across_y())
     arrive = remote(in_ref.at[y], x_ref.at[1 - y], sends, recvs, last, place.across_y())
+    trade_g = remote(grad_ref.at[1 - y], g_ref.at[y], sends, recvs, last + 1, place.across_y())
+    arrive_g = remote(
+        grad_ref.at[y], g_ref.at[1 - y], sends, recvs, last + 1, place.across_y()
+    )
+    keep_g = pltpu.make_async_copy(grad_ref.at[y], g_ref.at[y], local_sem.at[chunks + 1])
+    keep_g.start()
     local = [pltpu.make_async_copy(in_ref.at[y], x_ref.at[y], local_sem.at[chunks])]
     for k in range(chunks):
         own = slot(k, y, z, x, core)
@@ -670,32 +746,34 @@
             to_partner(k, o, 2 + n).start()
 
     order = (0, 1, 3, 2)
-    for i in range(LINE + 2):
-        if i < LINE:
-            if order[i] > 0:
-                from_line(0, order[i]).wait_recv()
-            start_line(0, order[i])
-            if i == 0:
-                trade.start()
-        if 0 <= i - 1 < LINE:
-            arrive_first(0, order[i - 1])
-        if 0 <= i - 2 < LINE:
-            arrive_second(0, order[i - 2])
+    lead = 2
+    for i in range(LINE + lead):
+        k, o = i // LINE, order[i % LINE]
+        if o > 0:
+            from_line(k, o).wait_recv()
+        start_line(k, o)
+        if i == 0:
+            trade.start()
+        if i >= 1:
+            arrive_first((i - 1) // LINE, order[(i - 1) % LINE])
+        if i >= 2:
+            arrive_second((i - 2) // LINE, order[(i - 2) % LINE])
     arrive.wait_recv()
     for o in order:
         for n in range(4):
             from_partner(0, o, n).wait_recv()
 
     step = 256
-    for t in range(parts):
-        @pl.loop(0, rows // step)
-        def _(i):
-            half = lax.div(i, 2)
-            row0 = pl.multiple_of(lax.rem(i, 2) * step, step)
-            left = x_ref[half, pl.ds(row0, step), :]
-            right = first_ref[t, :, :, :, :, :wide].reshape(-1, wide)
-            value = dot_nn(left, right) + bias_ref[t]
-            proj_ref[t, pl.ds(pl.multiple_of(i * step, step), step), :] = value.astype(BF16)
+
+    def project_slice(i):
+        t = lax.div(i, rows // step)
+        row = lax.rem(i, rows // step)
+        half = lax.div(row * step, x_ref.shape[1])
+        row0 = pl.multiple_of(lax.rem(row * step, x_ref.shape[1]), step)
+        left = x_ref[half, pl.ds(row0, step), :]
+        right = first_ref[t, :, :, :, :, :wide].reshape(-1, wide)
+        value = dot_nn(left, right) + bias_ref[t]
+        proj_ref[t, pl.ds(pl.multiple_of(row * step, step), step), :] = value.astype(BF16)
 
     lanes = 128
     groups = wide // 3 // lanes
@@ -708,53 +786,110 @@
         qi = lax.rem(i, tiles)
         t = lax.div(group, groups)
         j = lax.rem(group, groups)
-        query0 = pl.multiple_of(qi * TILE, TILE)
 
         def lane(c):
             return pl.ds(pl.multiple_of((c * groups + j) * lanes, lanes), lanes)
 
-        queries = proj_ref[t, pl.ds(query0, TILE), lane(0)] * BF16(0.125)
-        each = [queries * masks[h] for h in range(heads)]
-        top[...] = jnp.full_like(top, -1e30)
-        den[...] = jnp.zeros_like(den)
-        acc[...] = jnp.zeros_like(acc)
-
-        @pl.loop(jnp.maximum(qi - REACH, 0), jnp.minimum(qi + REACH + 1, tiles))
-        def _(ki):
-            key0 = pl.multiple_of(ki * TILE, TILE)
-            allowed = allowed_tile(code_ref, seg_ref, key0, query0)
-            keys = proj_ref[t, pl.ds(key0, TILE), lane(1)]
-            values_t = proj_ref[t, pl.ds(key0, TILE), lane(2)].T
-            for h in range(heads):
-                scores = jnp.where(allowed, dot_nt(keys, each[h]), -1e30)
-                old = top[h]
-                new = jnp.maximum(old, jnp.max(scores, axis=0, keepdims=True))
-                expo = jnp.exp(scores - new)
-                shrink = jnp.exp(old - new)
-                top[h] = new
-                den[h] = den[h] * shrink + jnp.sum(expo, axis=0, keepdims=True)
-                part = dot_nn(values_t[h * HEAD_DIM : (h + 1) * HEAD_DIM], expo.astype(BF16))
-                acc[h] = acc[h] * shrink + part
-
-        both = jnp.concatenate([acc[h] / den[h] for h in range(heads)], axis=0)
-        ctx_ref[t, pl.ds(query0, TILE), lane(0)] = both.astype(BF16).T
+        def at(ki):
+            return pl.ds(pl.multiple_of(ki * TILE, TILE), TILE)
+
+        @pl.when(qi == 0)
+        def _():
+            for ki in range(tiles):
+                turned[ki] = proj_ref[t, ki * TILE : (ki + 1) * TILE, lane(2)].T
+
+        here = at(qi)
+        queries = proj_ref[t, here, lane(0)] * BF16(0.125)
+        own_docs = docs_ref[here, :]
+        allowed = allowed_tile(code_ref, seg_ref, qi * TILE, qi * TILE)
+        others = [lax.rem(qi + r, tiles) for r in range(tiles)]
+        keys = [proj_ref[t, at(ki), lane(1)] for ki in others]
+        values_t = jnp.concatenate([turned[ki] for ki in others], axis=1)
+        for r in range(1, tiles):
+            keys[r] = jnp.concatenate([keys[r], bars_ref[at(others[r]), :]], axis=1)
+        most = []
         for h in range(heads):
-            lse_ref[group, h : h + 1, pl.ds(query0, TILE)] = top[h] + jnp.log(den[h])
-
+            plain = queries * masks[h]
+            marked = jnp.concatenate([plain, own_docs], axis=1)
+            peak = None
+            for r in range(tiles):
+                if r == 0:
+                    scores = jnp.where(allowed, dot_nt(keys[0], plain), -1e30)
+                else:
+                    scores = dot_nt(keys[r], marked)
+                score_buf[h, r * TILE : (r + 1) * TILE, :] = scores
+                part = jnp.max(scores.reshape(-1, 8, TILE), axis=0)
+                peak = part if peak is None else jnp.maximum(peak, part)
+            most.append(jnp.max(peak, axis=0, keepdims=True))
+        done = []
+        for h in range(heads):
+            total = None
+            for c in range(0, tiles * TILE, CHUNK):
+                expo = jnp.exp(score_buf[h, c : c + CHUNK, :] - most[h])
+                expo_buf[h, c : c + CHUNK, :] = expo.astype(BF16)
+                part = jnp.sum(expo.reshape(-1, 8, TILE), axis=0)
+                total = part if total is None else total + part
+            total = jnp.sum(total, axis=0, keepdims=True)
+            part = dot_nn(values_t[h * HEAD_DIM : (h + 1) * HEAD_DIM], expo_buf[h])
+            done.append(part / total)
+            lse_ref[group, h : h + 1, here] = most[h] + jnp.log(total)
+        ctx_ref[t, here, lane(0)] = jnp.concatenate(done, axis=0).astype(BF16).T
+
+    def rows_copies(i):
+        at = pl.ds(pl.multiple_of(i * step, step), step)
+        pairs = (
+            (normed_buf.at[at, :], normed_out.at[at, :]),
+            (factor_buf.at[at, :], factor_out.at[at, :]),
+            (act_buf.at[:, at, :], act_out.at[:, at, :]),
+            (slope_buf.at[:, at, :], slope_out.at[:, at, :]),
+        )
+        return [
+            pltpu.make_async_copy(src, dst, rows_sem.at[i * 4 + n])
+            for n, (src, dst) in enumerate(pairs)
+        ]
+
+    def rows_slice(i):
+        at = pl.ds(pl.multiple_of(i * step, step), step)
+        half = lax.div(i * step, x_ref.shape[1])
+        row0 = pl.multiple_of(lax.rem(i * step, x_ref.shape[1]), step)
+        forward_block(
+            x_ref[half, pl.ds(row0, step), :],
+            lambda t: ctx_ref[t, at, :],
+            lambda t: first_ref[t, :, :, :, :, wide:].reshape(-1, wide // 3),
+            lambda t, cols: rest_ref[t, 0, :, :, :, :, cols].reshape(-1, UNIT_STEP),
+            vec_ref,
+            bup_ref,
+            at,
+            (normed_buf, factor_buf, act_buf, slope_buf),
+        )
+        for part in rows_copies(i):
+            part.start()
+
+    keep_rest = [
+        pltpu.make_async_copy(
+            rest_ref.at[t, k], rest_out.at[t, k], local_sem.at[chunks + 2 + parts * k + t]
+        )
+        for k in range(chunks - 1)
+        for t in range(parts)
+    ]
     count = (chunks - 1) * LINE
-    slices = parts * groups * tiles
-    share = slices // count
+    heavy = 2
+    calm = 3
+    project_share = parts * (rows // step) // heavy
+    attend_share = parts * groups * tiles // calm
+    row_slices = rows // step
+    rows_from = heavy + calm
 
     def split(p):
         k = 1 + lax.div(p, LINE)
         r = lax.rem(p, LINE)
         return k, jnp.where(r < 2, r, 5 - r)
 
-    @pl.loop(0, count + 2)
+    @pl.loop(0, count)
     def _(p):
-        @pl.when(p < count)
+        @pl.when(p + lead < count)
         def _():
-            k, o = split(p)
+            k, o = split(p + lead)
 
             @pl.when(o > 0)
             def _():
@@ -762,25 +897,47 @@
 
             start_line(k, o)
 
-        @pl.when((p >= 1) & (p <= count))
+        @pl.when(p + lead - 1 < count)
         def _():
-            arrive_first(*split(p - 1))
-
-        @pl.when(p >= 2)
+            arrive_first(*split(p + lead - 1))
+
+        arrive_second(*split(p + lead - 2))
+
+        @pl.when(p == LINE - lead)
         def _():
-            arrive_second(*split(p - 2))
-
-        @pl.when(p < count)
+            trade_g.start()
+
+        @pl.when(p < heavy)
         def _():
-            @pl.loop(0, share)
+            @pl.loop(0, project_share)
             def _(n):
-                attend_slice(p * share + n)
-
-    @pl.loop(0, count)
-    def _(p):
-        k, o = split(p)
+                project_slice(p * project_share + n)
+
+        @pl.when((p >= heavy) & (p < rows_from))
+        def _():
+            @pl.loop(0, attend_share)
+            def _(n):
+                attend_slice((p - heavy) * attend_share + n)
+
+        @pl.when(p == rows_from)
+        def _():
+            for o in order:
+                for n in range(4):
+                    from_partner(1, o, n).wait_recv()
+
+        @pl.when(p >= rows_from)
+        def _():
+            rows_slice(p - rows_from)
+
+    for i in range(count - rows_from, row_slices):
+        rows_slice(i)
+    for part in keep_rest[:parts]:
+        part.start()
+    for o in order:
         for n in range(4):
-            from_partner(k, o, n).wait_recv()
+            from_partner(2, o, n).wait_recv()
+    for part in keep_rest[parts:]:
+        part.start()
 
     @pl.loop(0, count)
     def _(p):
@@ -805,9 +962,17 @@
         for n in range(4):
             to_partner(0, o, n).wait_send()
     trade.wait_send()
-
-
-def gather_all(shard, halves, bias, codes, seg_row):
+    trade_g.wait_send()
+    arrive_g.wait_recv()
+    keep_g.wait()
+    for part in keep_rest:
+        part.wait()
+    for i in range(row_slices):
+        for part in rows_copies(i):
+            part.wait()
+
+
+def gather_all(shard, halves, bias, codes, seg_row, docs, bars, vectors, bias_up, grad_halves):
     chunks, own_rows, units = shard.shape
     parts, rows, width = halves.shape
     wide = bias.shape[-1]
@@ -815,50 +980,81 @@
     groups = wide // 3 // 128
     anywhere = pl.BlockSpec(memory_space=pl.ANY)
     local = pl.BlockSpec(memory_space=pltpu.VMEM)
-    copies = chunks * LINE * PER_PIECE + 1
+    copies = chunks * LINE * PER_PIECE + 2
     places = (LINE, 2, 2, own_rows, units)
-    first, rest, x, projected, context, lse = pl.pallas_call(
+    forward = forward_shapes(parts, length, width, units)
+    first, rest, x, grads, projected, context, lse, *state = pl.pallas_call(
         gather_kernel,
-        in_specs=[local] * 5,
-        out_specs=[local, anywhere, local, local, local, local],
+        in_specs=[local] * 9 + [anywhere],
+        out_specs=[local, anywhere, local, anywhere, local, local, local] + [anywhere] * 4,
         out_shape=[
             jax.ShapeDtypeStruct((parts,) + places, BF16),
             jax.ShapeDtypeStruct((parts, chunks - 1) + places, BF16),
             jax.ShapeDtypeStruct((parts, rows, width), BF16),
+            jax.ShapeDtypeStruct((parts, rows, width), BF16),
             jax.ShapeDtypeStruct((parts, length, wide), BF16),
             jax.ShapeDtypeStruct((parts, length, wide // 3), BF16),
             jax.ShapeDtypeStruct((parts * groups, 2, length), F32),
-        ],
+        ]
+        + forward,
         scratch_shapes=[
+            pltpu.VMEM((parts, chunks - 1) + places, BF16),
+        ]
+        + [pltpu.VMEM(s.shape, s.dtype) for s in forward]
+        + [
             pltpu.SemaphoreType.DMA((copies,)),
             pltpu.SemaphoreType.DMA((copies,)),
-            pltpu.SemaphoreType.DMA((chunks + 1,)),
-            pltpu.VMEM((2, 1, TILE), F32),
-            pltpu.VMEM((2, 1, TILE), F32),
-            pltpu.VMEM((2, HEAD_DIM, TILE), F32),
+            pltpu.SemaphoreType.DMA((chunks + 2 + parts * (chunks - 1),)),
+            pltpu.SemaphoreType.DMA((length // 256 * 4,)),
+            pltpu.VMEM((length // TILE, 128, TILE), BF16),
+            pltpu.VMEM((2, length, TILE), F32),
+            pltpu.VMEM((2, length, TILE), BF16),
         ],
         compiler_params=params(collective_id=0, has_side_effects=True),
         name="gather_all",
-    )(shard, halves, bias, codes, seg_row)
+    )(shard, halves, bias, codes, seg_row, docs, bars, vectors, bias_up, grad_halves)
     first = first.reshape(parts, 1, -1, units)
     rest = rest.reshape(parts, chunks - 1, -1, units)
-    return first, rest, x.reshape(length, width), projected, context, lse
-
-
-def reduce_kernel(
-    a_ref,
+    x, grads = x.reshape(length, width), grads.reshape(length, width)
+    return first, rest, x, grads, projected, context, lse, state
+
+
+def back_kernel(
     b_ref,
     c_ref,
-    xg_ref,
+    x_ref,
+    first_ref,
+    base_ref,
+    proj_ref,
+    ctx_ref,
+    g_ref,
+    lse_ref,
+    code_ref,
+    seg_ref,
+    docs_ref,
+    bars_ref,
+    w_ref,
     small_ref,
+    res_ref,
     out_ref,
     xr_ref,
+    rr_ref,
     total_ref,
+    a_buf,
+    dp_buf,
+    xg_buf,
     p_buf,
     s_buf,
     f_buf,
     z_buf,
     t_buf,
+    turned,
+    score_buf,
+    gprob_buf,
+    prob_buf,
+    gscore_buf,
+    dk_acc,
+    dv_acc,
     sends,
     recvs,
     t_send,
@@ -867,18 +1063,31 @@
 ):
     place = Place()
     z, x, y, core = place.z, place.x, place.y, place.core
-    grads = (a_ref, b_ref, c_ref)
-    chunks = len(grads)
+    chunks = out_ref.shape[0]
+    own_rows = out_ref.shape[1]
+    parts, rows, wide = proj_ref.shape
+    part_width = wide // 3
+    width = x_ref.shape[1]
     place.greet()
 
     def where(k):
-        return place.corners(REDUCE_MIXED[k])
+        return place.corners(int(k > 0) if isinstance(k, int) else 1)
 
     def copy(k, o, n, src, dst, device):
         return remote(src, dst, sends, recvs, (k * LINE + o) * PER_PIECE + n, device)
 
-    def to_partner(k, o):
-        src = grads[k].at[:, place.along(o), :, 1 - core]
+    def a_rows(zz, xx, cc):
+        start = pl.multiple_of(((zz * 2 + xx) * 2 + cc) * own_rows, own_rows)
+        return pl.ds(start, own_rows)
+
+    def to_partner_a(o, n):
+        yy, xx = n // 2, n % 2
+        src = a_buf.at[yy, a_rows(place.along(o), xx, 1 - core)]
+        slot = (0, 5, 6, 7)[n]
+        return copy(0, o, slot, src, p_buf.at[0, o, yy, xx], place.partner())
+
+    def to_partner(source, k, o):
+        src = source.at[:, place.along(o), :, 1 - core]
         return copy(k, o, 0, src, p_buf.at[k, o], place.partner())
 
     def to_second(k, o, n):
@@ -897,7 +1106,7 @@
         return remote(src, dst, t_send, t_recv, n, device)
 
     hops = (
-        small_copy(0, small_ref, t_buf.at[0], place.partner()),
+        small_copy(0, t_buf.at[9], t_buf.at[0], place.partner()),
         small_copy(1, t_buf.at[1], t_buf.at[2], place.across_x()),
         small_copy(2, t_buf.at[3], t_buf.at[4], place.across_y()),
     )
@@ -914,7 +1123,7 @@
             hops[0].start()
         elif step == 1:
             hops[0].wait_recv()
-            t_buf[1] = small_ref[...] + t_buf[0]
+            t_buf[1] = t_buf[9] + t_buf[0]
             hops[1].start()
         elif step == 2:
             hops[1].wait_recv()
@@ -930,18 +1139,24 @@
                 small_from(o).wait_recv()
             total_ref[...] = (t_buf[5] + t_buf[6]) + (t_buf[7] + t_buf[8])
 
-    trade = small_copy(2 + LINE, xg_ref.at[1 - y], xr_ref.at[y], place.across_y())
-    arrive = small_copy(2 + LINE, xg_ref.at[1 - y], xr_ref.at[1 - y], place.across_y())
-    keep = pltpu.make_async_copy(xg_ref.at[y], xr_ref.at[y], local_sem.at[0])
-
-    def stage_partner(k, o):
-        to_partner(k, o).wait_recv()
-        zz = place.along(o)
+    trade = small_copy(2 + LINE, xg_buf.at[1 - y], xr_ref.at[y], place.across_y())
+    arrive = small_copy(2 + LINE, xg_buf.at[1 - y], xr_ref.at[1 - y], place.across_y())
+    keep = pltpu.make_async_copy(xg_buf.at[y], xr_ref.at[y], local_sem.at[0])
+    trade_r = small_copy(3 + LINE, res_ref.at[1 - y], rr_ref.at[y], place.across_y())
+    arrive_r = small_copy(3 + LINE, res_ref.at[1 - y], rr_ref.at[1 - y], place.across_y())
+    keep_r = pltpu.make_async_copy(res_ref.at[y], rr_ref.at[y], local_sem.at[1])
+
+    def add_partner(k, o, own):
         for n in (3, 2, 1, 0):
             yy, xx = where(k)[n]
-            p_buf[k, o, yy, xx] = p_buf[k, o, yy, xx] + grads[k][yy, zz, xx, core]
+            p_buf[k, o, yy, xx] = p_buf[k, o, yy, xx] + own(yy, xx)
             if n >= 2:
                 to_second(k, o, n - 2).start()
+
+    def stage_partner(source, k, o):
+        to_partner(source, k, o).wait_recv()
+        zz = place.along(o)
+        add_partner(k, o, lambda yy, xx: source[yy, zz, xx, core])
 
     def stage_second(k, o):
         for n in (1, 0):
@@ -954,8 +1169,6 @@
     def stage_first(k, o):
         to_first(k, o).wait_recv()
         f_buf[k, o] = f_buf[k, o] + s_buf[k, o, 0]
-        if o > 0:
-            to_line(k, o).start()
 
     def finish(k):
         total = f_buf[k, 0].astype(F32)
@@ -964,77 +1177,299 @@
             total = total + z_buf[k, o - 1].astype(F32)
         out_ref[k] = total
 
-    steps = [(k, o) for k in range(chunks) for o in (2, 1, 3, 0)]
+    lanes = 128
+    groups = part_width // lanes
+    heads = lanes // HEAD_DIM
+    tiles = rows // TILE
+    masks = head_masks(lanes)
+    q_row = small_ref.shape[0] - (2 * parts * groups + parts * w_ref.shape[3] // lanes)
+
+    def lane(c, j):
+        return pl.ds(pl.multiple_of((c * groups + j) * lanes, lanes), lanes)
+
+    def at(ki):
+        return pl.ds(pl.multiple_of(ki * TILE, TILE), TILE)
+
+    def attend_slice(i):
+        group = lax.div(i, tiles)
+        qi = lax.rem(i, tiles)
+        t = lax.div(group, groups)
+        j = lax.rem(group, groups)
+
+        @pl.when(qi == 0)
+        def _():
+            dk_acc[...] = jnp.zeros_like(dk_acc)
+            dv_acc[...] = jnp.zeros_like(dv_acc)
+            for ki in range(tiles):
+                turned[ki] = proj_ref[t, ki * TILE : (ki + 1) * TILE, lane(1, j)].T
+
+        here = at(qi)
+        queries = proj_ref[t, here, lane(0, j)] * BF16(0.125)
+        grads = g_ref[t, here, lane(0, j)]
+        own_docs = docs_ref[here, :]
+        prod_t = (grads.astype(F32) * ctx_ref[t, here, lane(0, j)].astype(F32)).T
+        plain = [queries * masks[h] for h in range(heads)]
+        g_each = [grads * masks[h] for h in range(heads)]
+        marked = [jnp.concatenate([plain[h], own_docs], axis=1) for h in range(heads)]
+        q_tall = jnp.concatenate(plain, axis=0)
+        g_tall = jnp.concatenate(g_each, axis=0)
+        inner = [
+            jnp.sum(prod_t[h * HEAD_DIM : (h + 1) * HEAD_DIM], axis=0, keepdims=True)
+            for h in range(heads)
+        ]
+        lse = [lse_ref[group, h : h + 1, here] for h in range(heads)]
+        allowed = allowed_tile(code_ref, seg_ref, qi * TILE, qi * TILE)
+        dq = [None] * heads
+
+        for r in range(tiles):
+            there = at(lax.rem(qi + r, tiles))
+            keys = proj_ref[t, there, lane(1, j)]
+            values = proj_ref[t, there, lane(2, j)]
+            if r > 0:
+                keys = jnp.concatenate([keys, bars_ref[there, :]], axis=1)
+            for h in range(heads):
+                scores = dot_nt(keys, marked[h] if r > 0 else plain[h])
+                if r == 0:
+                    scores = jnp.where(allowed, scores, -1e30)
+                score_buf[r % 2, h] = scores
+                gprob_buf[r % 2, h] = dot_nt(values, g_each[h])
+            for h in range(heads):
+                cols = slice(h * TILE, (h + 1) * TILE)
+                for c in range(0, TILE, CHUNK):
+                    rows_c = slice(c, c + CHUNK)
+                    probs = jnp.exp(score_buf[r % 2, h, rows_c, :] - lse[h])
+                    gscores = probs * (gprob_buf[r % 2, h, rows_c, :] - inner[h])
+                    prob_buf[r, rows_c, cols] = probs.astype(BF16)
+                    gscore_buf[r, rows_c, cols] = gscores.astype(BF16)
+            dv_acc[there, :] += dot_nn(prob_buf[r], g_tall)
+            dk_acc[there, :] += dot_nn(gscore_buf[r], q_tall)
+        keys_t = jnp.concatenate([turned[lax.rem(qi + r, tiles)] for r in range(tiles)], axis=1)
+        dq = []
+        for h in range(heads):
+            tall = gscore_buf[:, :, h * TILE : (h + 1) * TILE].reshape(tiles * TILE, TILE)
+            dq.append(dot_nn(keys_t[h * HEAD_DIM : (h + 1) * HEAD_DIM], tall))
+        both = jnp.concatenate(dq, axis=0) * 0.125
+        dp_buf[t, here, lane(0, j)] = both.astype(BF16).T
+
+        @pl.when(qi == tiles - 1)
+        def _():
+            low_k = dk_acc[...].astype(BF16)
+            low_v = dv_acc[...].astype(BF16)
+            low_q = dp_buf[t, :, lane(0, j)]
+            dp_buf[t, :, lane(1, j)] = low_k
+            dp_buf[t, :, lane(2, j)] = low_v
+            t_buf[9, pl.ds(q_row + group, 1), :] = col_sum(low_q.astype(F32))
+            v_row = q_row + parts * groups + group
+            t_buf[9, pl.ds(v_row, 1), :] = col_sum(low_v.astype(F32))
+
+    order = (2, 1, 3, 0)
+
+    def split(p):
+        r = lax.rem(p, LINE)
+        o = jnp.where(r == 0, 2, jnp.where(r == 1, 1, jnp.where(r == 2, 3, 0)))
+        return 1 + lax.div(p, LINE), o
+
+    for source, k in ((b_ref, 1), (c_ref, 2)):
+        for o in order:
+            to_partner(source, k, o).start()
+    trade_r.start()
+    keep_r.start()
+    t_buf[9] = small_ref[...]
+    count = (chunks - 1) * LINE
+    share = parts * groups * tiles // count
+
+    def pass_second(p):
+        stage_second(*split(p))
+
+    def pass_first(p):
+        k, o = split(p)
+        stage_first(k, o)
+
+        @pl.when(o > 0)
+        def _():
+            to_line(k, o).start()
+
+    @pl.loop(0, count)
+    def _(p):
+        k, o = split(p)
+
+        @pl.when(p < LINE)
+        def _():
+            stage_partner(b_ref, k, o)
+
+        @pl.when(p >= LINE)
+        def _():
+            stage_partner(c_ref, k, o)
+
+        @pl.when(p >= 1)
+        def _():
+            pass_second(p - 1)
+
+        @pl.when(p >= 2)
+        def _():
+            pass_first(p - 2)
+
+        @pl.loop(0, share)
+        def _(n):
+            attend_slice(p * share + n)
+
     small_step(0)
-    for k, o in steps:
-        to_partner(k, o).start()
-    keep.start()
-    small_step(1)
-    for i in range(len(steps) + 4):
-        if i < len(steps):
-            stage_partner(*steps[i])
-        if i == 1:
+    pass_second(count - 1)
+    pass_first(count - 2)
+    for t in range(parts):
+        for m in range(0, width, GRAD_STEP):
+            at = slice(m, m + GRAD_STEP)
+            left = x_ref[:, at]
+            part = dot_tn(left, dp_buf[t])
+            a_buf[t, at, :wide] = part.astype(BF16)
+            part = dot_tn(first_ref[:, at], ctx_ref[t])
+            a_buf[t, at, wide:] = part.astype(BF16)
+        small_step(1 + t)
+        if t == 0:
+            pass_first(count - 1)
+    for o in order:
+        for n in range(4):
+            to_partner_a(o, n).start()
+    small_step(3)
+
+    step = 256
+    half_rows = rows // parts
+
+    def input_slice(i):
+        at = slice(i * step, (i + 1) * step)
+        value = base_ref[at, :]
+        for t in range(parts):
+            value = value + dot_nt(dp_buf[t, at, :], w_ref[t, 0, :, :wide])
+        half, row0 = i * step // half_rows, i * step % half_rows
+        xg_buf[half, row0 : row0 + step, :] = value.astype(BF16)
+
+    for i in range(LINE + 2):
+        if i < LINE:
+            o = order[i]
+            for n in range(4):
+                to_partner_a(o, n).wait_recv()
+            zz = place.along(o)
+            add_partner(0, o, lambda yy, xx: a_buf[yy, a_rows(zz, xx, core), :])
+        if 0 <= i - 1 < LINE:
+            stage_second(0, order[i - 1])
+        if 0 <= i - 2 < LINE:
+            stage_first(0, order[i - 2])
+            if order[i - 2] > 0:
+                to_line(0, order[i - 2]).start()
+        if i < rows // step:
+            input_slice(i)
+        if i == rows // step - 1:
             trade.start()
-        if 0 <= i - 2 < len(steps):
-            stage_second(*steps[i - 2])
-        if 0 <= i - 4 < len(steps):
-            stage_first(*steps[i - 4])
-        if i in (3, 6, 9):
-            small_step(1 + i // 3)
-    for k in range(chunks):
+            keep.start()
+            small_step(4)
+    for k in (1, 2, 0):
         finish(k)
 
-    keep.wait()
-    trade.wait_send()
-    arrive.wait_recv()
+    for part in (keep, keep_r):
+        part.wait()
+    for part in (trade, trade_r):
+        part.wait_send()
+    for part in (arrive, arrive_r):
+        part.wait_recv()
     for part in hops:
         part.wait_send()
     for o in range(1, LINE):
         small_line(o).wait_send()
-    for k, o in steps:
-        to_partner(k, o).wait_send()
-        for n in range(2):
-            to_second(k, o, n).wait_send()
-        to_first(k, o).wait_send()
-        if o > 0:
-            to_line(k, o).wait_send()
-
-
-def reduce_all(grads_a, grads_b, grads_c, halves, small):
-    parts, width, units = grads_a.shape
-    _, rows, model = halves.shape
+    for k in range(chunks):
+        for o in order:
+            if k == 0:
+                for n in range(4):
+                    to_partner_a(o, n).wait_send()
+            else:
+                to_partner((b_ref, c_ref)[k - 1], k, o).wait_send()
+            for n in range(2):
+                to_second(k, o, n).wait_send()
+            to_first(k, o).wait_send()
+            if o > 0:
+                to_line(k, o).wait_send()
+
+
+def back_all(
+    grads_b,
+    grads_c,
+    x,
+    first_low,
+    grad_first,
+    projected,
+    context,
+    grad_context,
+    lse,
+    codes,
+    seg_row,
+    docs,
+    bars,
+    first,
+    small,
+    result,
+):
+    parts, width, units = grads_b.shape
+    rows, model = x.shape
+    wide = projected.shape[2]
     own_rows = width // (4 * LINE)
     chunks = 3
-    folded = [g.reshape(parts, LINE, 2, 2, own_rows, units) for g in (grads_a, grads_b, grads_c)]
+    folded = [g.reshape(parts, LINE, 2, 2, own_rows, units) for g in (grads_b, grads_c)]
     small_rows = small.shape[0] // 128
     local = pl.BlockSpec(memory_space=pltpu.VMEM)
+    anywhere = pl.BlockSpec(memory_space=pl.ANY)
     piece = (own_rows, units)
     copies = chunks * LINE * PER_PIECE
-    own, x_rows, total = pl.pallas_call(
-        reduce_kernel,
-        in_specs=[local] * 5,
-        out_specs=[local, pl.BlockSpec(memory_space=pl.ANY), local],
+    own, x_rows, out_rows, total = pl.pallas_call(
+        back_kernel,
+        in_specs=[local] * 15 + [anywhere],
+        out_specs=[local, anywhere, anywhere, local],
         out_shape=[
             jax.ShapeDtypeStruct((chunks, own_rows, units), F32),
-            jax.ShapeDtypeStruct((parts, rows, model), BF16),
+            jax.ShapeDtypeStruct((parts, rows // parts, model), BF16),
+            jax.ShapeDtypeStruct((parts, rows // parts, model), BF16),
             jax.ShapeDtypeStruct((small_rows, 128), F32),
         ],
         scratch_shapes=[
+            pltpu.VMEM((parts, width, units), BF16),
+            pltpu.VMEM((parts, rows, wide), BF16),
+            pltpu.VMEM((parts, rows // parts, model), BF16),
             pltpu.VMEM((chunks, LINE, 2, 2) + piece, BF16),
             pltpu.VMEM((chunks, LINE, 2) + piece, BF16),
             pltpu.VMEM((chunks, LINE) + piece, BF16),
             pltpu.VMEM((chunks, LINE - 1) + piece, BF16),
-            pltpu.VMEM((5 + LINE, small_rows, 128), F32),
+            pltpu.VMEM((6 + LINE, small_rows, 128), F32),
+            pltpu.VMEM((rows // TILE, 128, TILE), BF16),
+            pltpu.VMEM((2, 2, TILE, TILE), F32),
+            pltpu.VMEM((2, 2, TILE, TILE), F32),
+            pltpu.VMEM((rows // TILE, TILE, 2 * TILE), BF16),
+            pltpu.VMEM((rows // TILE, TILE, 2 * TILE), BF16),
+            pltpu.VMEM((rows, 128), F32),
+            pltpu.VMEM((rows, 128), F32),
             pltpu.SemaphoreType.DMA((copies,)),
             pltpu.SemaphoreType.DMA((copies,)),
-            pltpu.SemaphoreType.DMA((3 + LINE,)),
-            pltpu.SemaphoreType.DMA((3 + LINE,)),
-            pltpu.SemaphoreType.DMA((1,)),
+            pltpu.SemaphoreType.DMA((4 + LINE,)),
+            pltpu.SemaphoreType.DMA((4 + LINE,)),
+            pltpu.SemaphoreType.DMA((2,)),
         ],
         compiler_params=params(collective_id=1, has_side_effects=True),
-        name="reduce_all",
-    )(*folded, halves, small.reshape(small_rows, 128))
-    return own, x_rows, total.reshape(-1)
+        name="back_all",
+    )(
+        *folded,
+        x,
+        first_low,
+        grad_first,
+        projected,
+        context,
+        grad_context,
+        lse,
+        codes,
+        seg_row,
+        docs,
+        bars,
+        first,
+        small.reshape(small_rows, 128),
+        result.reshape(parts, rows // parts, model),
+    )
+    return own, x_rows, out_rows, total.reshape(-1)
 
 
 def trade_in(halves):
@@ -1095,15 +1530,26 @@
     b_q = b_qv[0].reshape(parts, part_width)
     b_v = b_qv[1].reshape(parts, part_width)
     bias = jnp.concatenate([b_q, jnp.zeros_like(b_q), b_v], axis=1)[:, None, :]
+    zero = jnp.zeros_like(b_o)
+    vectors = jnp.stack([b_o, gain_one, shift_one, b_down, gain_two, shift_two, zero, zero])
+    bias_up = b_up.reshape(parts, 1, units)
     linked = lax.axis_size("dp") == LINE * 4 and parts == 2
     if linked:
-        first, rest, x, projected, context, lse = gather_all(
-            shard, inputs[:, 0], bias, codes, seg_row
+        number = lax.broadcasted_iota(jnp.int32, (1, 128), 1)
+        docs = (seg[:, None] == number).astype(BF16)
+        bars = jnp.where(codes == number, 0.0, -1e30).astype(BF16)
+        first, rest, x, grads, projected, context, lse, state = gather_all(
+            shard,
+            inputs[:, 0],
+            bias,
+            codes,
+            seg_row,
+            docs,
+            bars,
+            vectors,
+            bias_up,
+            out_grad[:, 0],
         )
-        theirs = lax.ppermute(out_grad[1 - rank, 0], "tensor", ((0, 1), (1, 0)))
-        own_half = out_grad[rank, 0]
-        grads = jnp.concatenate([own_half, theirs])
-        grads = jnp.where(rank == 0, grads, jnp.concatenate([theirs, own_half]))
     else:
         weights = gather_weights(shard)
         first, rest = weights[:, :1], weights[:, 1:]
@@ -1111,34 +1557,47 @@
         grads = trade_in(out_grad[:, 0])
         projected = project(x, first, bias)
         context, lse = attend(projected, low, high, codes, seg_row)
-    zero = jnp.zeros_like(b_o)
-    vectors = jnp.stack([b_o, gain_one, shift_one, b_down, gain_two, shift_two, zero, zero])
-    out, hidden_low, second_low, first_low, grad_first, active, grad_up, grad_context, sums, upsum = (
-        rows_pass(x, context, grads, first, rest, vectors, b_up.reshape(parts, 1, units))
+        state = rows_forward(x, context, first, rest, vectors, bias_up)
+    normed, factor, active, slope = state
+    out, hidden_low, second_low, first_low, grad_first, grad_up, grad_context, sums, upsum = (
+        rows_pass(normed, factor, active, slope, grads, first, rest, vectors)
     )
-    if linked:
-        swapped = lax.ppermute(out.reshape(parts, -1, out.shape[1])[1 - rank], "tensor", ((0, 1), (1, 0)))
     partial_up = outer(hidden_low, grad_up)
     partial_down = outer(second_low, active)
-    grad_q, grad_k, grad_v, qsum, vsum = attend_back(
-        projected, context, grad_context, lse, low, high, codes, seg_row
-    )
-    partial_a = outer_four(x, first_low, grad_q, grad_k, grad_v, context)
-    x_whole = input_grad(grad_first, grad_q, grad_k, grad_v, first)
-    small = jnp.concatenate(
-        [sums[:6].reshape(-1), qsum.reshape(-1), vsum.reshape(-1), upsum.reshape(-1)]
-    )
     if linked:
-        halves = x_whole.reshape(parts, -1, x_whole.shape[1])
-        own, x_rows, small = reduce_all(partial_a, partial_up, partial_down, halves, small)
-        mine = out.reshape(parts, -1, out.shape[1])[rank]
-        out_rows = jnp.where(rank == 0, jnp.stack([mine, swapped]), jnp.stack([swapped, mine]))
+        zeros = jnp.zeros((4 * part_width,), F32)
+        small = jnp.concatenate([sums[:6].reshape(-1), zeros, upsum.reshape(-1)])
+        own, x_rows, out_rows, small = back_all(
+            partial_up,
+            partial_down,
+            x,
+            first_low,
+            grad_first,
+            projected,
+            context,
+            grad_context,
+            lse,
+            codes,
+            seg_row,
+            docs,
+            bars,
+            first,
+            small,
+            out,
+        )
     else:
+        grad_q, grad_k, grad_v, qsum, vsum = attend_back(
+            projected, context, grad_context, lse, low, high, codes, seg_row
+        )
+        partial_a = outer_four(x, first_low, grad_q, grad_k, grad_v, context)
         own = jnp.stack(
             [scatter_grads(g).astype(F32) for g in (partial_a, partial_up, partial_down)]
         )
-        x_rows = trade_out(x_whole)
+        x_rows = trade_out(input_grad(grad_first, grad_q, grad_k, grad_v, first))
         out_rows = trade_out(out)
+        small = jnp.concatenate(
+            [sums[:6].reshape(-1), qsum.reshape(-1), vsum.reshape(-1), upsum.reshape(-1)]
+        )
         small = lax.psum(small, ("dp", "tensor"))
     width = sums.shape[1]
     vec = small[: 6 * width].reshape(6, width)

time: 390 us -> 334 us (0.86)
  Pallas kernels: 348 us -> 310 us
  starting transfers between devices: 20.2 us -> 0 us
    pallas_call x6 -> x3, Pallas kernels: 329 us -> 292 us  [the longest x1 131 us: back_all(): pl.pallas_call(back_kernel, in_specs=[local] * 15 + [anywhere], out_specs...]
    ppermute x2 -> x0, starting transfers between devices: 20.2 us -> none  [the longest x1 17.1 us: shards(): lax.ppermute(out.reshape(parts, -1, out.shape[1])[1 - rank], 'tensor', ((...]
  transfers between devices with their start and end apart: 2 -> 0, of which waited for: 0 -> 0; matrix products, arithmetic and copies ran while one was open for 4% -> 0% of each run, Pallas kernels for 62% -> 0%
where the time goes in v3:
time: 334 us; the launch traced here: 331 us
  Pallas kernels  310 us (93%)
  local copies, waits for them, and re-layouts  11.2 us (3%)
  other arithmetic  8.65 us (3%)
    pallas_call x1, Pallas kernels, back_all(): pl.pallas_call(back_kernel, in_specs=[local] * 15 + [anywhere], out_specs...  131 us
    pallas_call x1, Pallas kernels, gather_all(): pl.pallas_call(gather_kernel, in_specs=[local] * 9 + [anywhere], out_spec...  128 us
    pallas_call x1, Pallas kernels, rows_pass(): pl.pallas_call(rows_kernel, grid=(rows // step,), in_specs=[row, pl.Block...  33.3 us
    pallas_call x2, Pallas kernels, outer(): pl.pallas_call(outer_kernel, grid=(parts,), in_specs=[pl.BlockSpec((rows,...  18.2 us

profile of v3, /device:TPU:0, one launch (start us, length us, event | category | flops | bytes accessed | tf_op | source)
XLA Modules:
  0.0 331.2 jit_solution(10225803195128059257)
XLA Ops:
  0.6 0.0 copy-start
  0.7 0.0 copy-start.5
  0.7 0.0 copy-start.4
  0.7 0.0 copy-start.7
  0.7 0.0 copy-start.8
  0.7 0.0 copy-start.9
  0.7 0.0 copy-start.10
  0.7 0.0 copy-start.11
  0.7 0.0 copy-start.12
  0.7 0.0 copy-start.13
  0.8 0.6 copy-done
  1.4 0.7 compare_reduce_fusion
  2.1 1.0 broadcast_in_dim.41.code_ref
  3.1 0.9 select_convert_fusion.bars_ref
  4.0 0.9 fusion.docs_ref
  4.9 0.6 fusion.2.seg_ref
  5.5 0.8 slice_bitcast_fusion.9
  6.3 0.8 maximum_bitcast_fusion
  7.1 0.0 copy-done.5
  7.1 0.0 copy-done.4
  7.1 0.8 pad_maximum_fusion.shard_ref
  7.9 0.0 copy-done.7
  8.0 0.6 broadcast_in_dim.39.bias_ref
  8.6 0.0 copy-done.8
  8.6 0.0 copy-done.9
  8.7 0.0 copy-done.10
  8.7 0.0 copy-done.11
  8.7 0.0 copy-done.12
  8.7 0.0 copy-done.13
  8.8 0.6 stack.68.vec_ref
  9.4 128.1 %gather_all.1 = (bf16[2,4,2,2,48,1536]{5,4,3,2,1,0:T(8,128)(2,1)}, bf16[2,2,4,2,2,48,1536]{6,5,4,3,2,1,0:T(8,128)(2,1)}, bf16[2,512,768]{2,1,0:T(8,128)(2,1)}, b...) custom-call(bf16[3,48,1536]{2,1,0:T(8,128)(2,1)} %pad_maximum_fusion, ...), custom_call_target="tpu_custom_call" | custom-call | tf_op jit(solution)/shard_map/gather_all/pallas_call | solution.py:986
  137.5 33.3 %rows_pass.1 = (bf16[1024,768]{1,0:T(8,128)(2,1)}, bf16[1024,768]{1,0:T(8,128)(2,1)}, bf16[1024,768]{1,0:T(8,128)(2,1)}, bf16[1024,768]{1,0:T(8,128)(2,1)}, f32[...) custom-call(f32[1024,768]{1,0:T(8,128)} %get-tuple-element.38.normed, ...), custom_call_target="tpu_custom_call" | custom-call | tf_op jit(solution)/shard_map/rows_pass/pallas_call | solution.py:426
  170.8 0.7 reshape.104
  171.6 1.3 maximum_bitcast_fusion.1.small_ref
  172.9 9.0 %outer.3 = bf16[2,768,1536]{2,1,0:T(8,128)(2,1)} custom-call(bf16[1024,768]{1,0:T(8,128)(2,1)} %get-tuple-element.47.rows_ref, bf16[2,1024,1536]{2,1,0:T(8,128)(2,1)} %get-tuple-element.40.act_ref.cols_ref), custom_call_target="tpu_custom_call" | custom-call | tf_op jit(solution)/shard_map/outer/pallas_call | solution.py:482
  181.9 9.1 %outer.2 = bf16[2,768,1536]{2,1,0:T(8,128)(2,1)} custom-call(bf16[1024,768]{1,0:T(8,128)(2,1)} %get-tuple-element.45.rows_ref, bf16[2,1024,1536]{2,1,0:T(8,128)(2,1)} %get-tuple-element.46.cols_ref), custom_call_target="tpu_custom_call" | custom-call | tf_op jit(solution)/shard_map/outer/pallas_call | solution.py:482
  191.1 130.9 %back_all.1 = (f32[3,48,1536]{2,1,0:T(8,128)}, bf16[2,512,768]{2,1,0:T(8,128)(2,1)}, bf16[2,512,768]{2,1,0:T(8,128)(2,1)}, f32[72,128]{1,0:T(8,128)}) custom-call(bf16[2,4,2,2,48,1536]{5,4,3,2,1,0:T(8,128)(2,1)} %bitcast.73, bf16[2,4,2,2,48,1536]{5,4,3,2,1,0:T(8,128)(2,1)} %bitcast.72, bf16[1024,768]{1,0:T(8,128)(2,1)} %bitcast.74, ...), custom_call_target="tpu_custom_call" | custom-call | tf_op jit(solution)/shard_map/back_all/pallas_call | solution.py:1421
  322.0 0.0 copy-start.3
  322.0 0.9 fusion.1
  322.9 0.6 pad_maximum_fusion.3
  323.5 2.0 slice_bitcast_fusion
  325.5 0.7 slice_bitcast_fusion.3
  326.2 0.7 pad_maximum_fusion.1
  326.9 1.9 bitcast_convert_fusion
  328.8 0.6 slice_bitcast_fusion.10
  329.4 0.7 dynamic_slice.23
  330.1 0.0 copy-done.2
  330.1 1.1 copy.33
  (24 shorter events, 0.1 us)
Async XLA Ops:
  0.6 0.7 copy-start
  0.7 6.4 %copy-start.5 = (bf16[48,1536]{1,0:T(8,128)(2,1)S(1)}, bf16[48,1536]{1,0:T(8,128)(2,1)}, u32[]{:S(2)}) copy-start(bf16[48,1536]{1,0:T(8,128)(2,1)} %param.25) | copy-start | bytes 442372
  0.7 6.4 %copy-start.4 = (bf16[1536,48]{0,1:T(8,128)(2,1)S(1)}, bf16[1536,48]{0,1:T(8,128)(2,1)}, u32[]{:S(2)}) copy-start(bf16[1536,48]{0,1:T(8,128)(2,1)} %param.27) | copy-start | bytes 442372
  0.7 7.2 %copy-start.7 = (f32[2,768]{1,0:T(2,128)S(1)}, f32[2,768]{1,0:T(2,128)}, u32[]{:S(2)}) copy-start(f32[2,768]{1,0:T(2,128)} %param.20) | copy-start | bytes 18436
  0.7 7.9 %copy-start.8 = (f32[768]{0:T(1024)S(1)}, f32[768]{0:T(1024)}, u32[]{:S(2)}) copy-start(f32[768]{0:T(1024)} %param.22) | copy-start | bytes 9220
  0.7 7.9 %copy-start.9 = (f32[768]{0:T(1024)S(1)}, f32[768]{0:T(1024)}, u32[]{:S(2)}) copy-start(f32[768]{0:T(1024)} %param.23) | copy-start | bytes 9220
  0.7 7.9 %copy-start.10 = (f32[768]{0:T(1024)S(1)}, f32[768]{0:T(1024)}, u32[]{:S(2)}) copy-start(f32[768]{0:T(1024)} %param.24) | copy-start | bytes 9220
  0.7 8.0 %copy-start.11 = (f32[768]{0:T(1024)S(1)}, f32[768]{0:T(1024)}, u32[]{:S(2)}) copy-start(f32[768]{0:T(1024)} %param.28) | copy-start | bytes 9220
  0.7 8.0 %copy-start.12 = (f32[768]{0:T(1024)S(1)}, f32[768]{0:T(1024)}, u32[]{:S(2)}) copy-start(f32[768]{0:T(1024)} %param.29) | copy-start | bytes 9220
  0.7 8.0 %copy-start.13 = (f32[768]{0:T(1024)S(1)}, f32[768]{0:T(1024)}, u32[]{:S(2)}) copy-start(f32[768]{0:T(1024)} %param.30) | copy-start | bytes 9220
  322.0 4.9 %copy-start.3 = (bf16[2,512,768]{2,1,0:T(8,128)(2,1)S(1)}, bf16[2,512,768]{2,1,0:T(8,128)(2,1)}, u32[]{:S(2)}) copy-start(bf16[2,512,768]{2,1,0:T(8,128)(2,1)} %get-tuple-element.59) | copy-start | bytes 4718596
  326.9 1.9 copy-start.6
  326.9 3.2 copy-start.2
  329.4 1.8 copy-start.1

commit v4 on v3

--- a/solution.py
+++ b/solution.py
@@ -673,8 +673,7 @@
         return rest_ref.at[yy, k - 1, zz, xx, cc]
 
     def where(k, cc=None):
-        mixed = k // 2 if isinstance(k, int) else lax.div(k, 2)
-        return place.corners(mixed, cc)
+        return place.corners(0, cc)
 
     def held(k, o, corner, cc=core):
         return slot(k, corner[0], place.back(o), corner[1], cc)
@@ -709,6 +708,23 @@
     def from_partner(k, o, n):
         here = held(k, o, where(k, 1 - core)[n], 1 - core)
         return copy(k, o, 4 + n, here, here, place.partner())
+
+    final = chunks - 1
+
+    def corner_of(n):
+        return lax.rem(y + lax.rem(n, 2), 2), lax.rem(x + lax.div(n, 2), 2)
+
+    def final_line(o, n):
+        here = held(final, 0, corner_of(n))
+        return copy(final, o, n, here, here, place.line(o))
+
+    def final_from(o, n):
+        here = held(final, o, corner_of(n))
+        return copy(final, o, n, here, here, place.line(o))
+
+    def final_partner(o, n):
+        here = held(final, o, corner_of(n))
+        return copy(final, o, 4 + n, here, here, place.partner())
 
     trade = remote(in_ref.at[1 - y], x_ref.at[y], sends, recvs, last, place.across_y())
     arrive = remote(in_ref.at[y], x_ref.at[1 - y], sends, recvs, last, place.across_y())
@@ -724,7 +740,7 @@
         local.append(pltpu.make_async_copy(shard_ref.at[k], own, local_sem.at[k]))
     for part in local:
         part.start()
-    for k in range(chunks):
+    for k in range(final):
         for o in (2, 1, 3):
             to_line(k, o).start()
     for part in local:
@@ -753,7 +769,15 @@
             from_line(k, o).wait_recv()
         start_line(k, o)
         if i == 0:
+            start_line(final, 0)
             trade.start()
+        if i == 2:
+            arrive_first(final, 0)
+        if i == 3:
+            arrive_second(final, 0)
+            for n in range(4):
+                for oo in (2, 1, 3):
+                    final_line(oo, n).start()
         if i >= 1:
             arrive_first((i - 1) // LINE, order[(i - 1) % LINE])
         if i >= 2:
@@ -873,37 +897,50 @@
         for t in range(parts)
     ]
     count = (chunks - 1) * LINE
-    heavy = 2
-    calm = 3
+    heavy = 1
+    calm = 2
     project_share = parts * (rows // step) // heavy
     attend_share = parts * groups * tiles // calm
     row_slices = rows // step
-    rows_from = heavy + calm
-
-    def split(p):
-        k = 1 + lax.div(p, LINE)
-        r = lax.rem(p, LINE)
-        return k, jnp.where(r < 2, r, 5 - r)
+    rows_from = count - row_slices
+
+    late = 2 * (LINE - 1)
+
+    def split(r):
+        return jnp.where(r < 2, r, 5 - r)
+
+    def pass_final(q):
+        n, r = lax.div(q, LINE - 1), lax.rem(q, LINE - 1)
+        o = jnp.where(r == 0, 2, jnp.where(r == 1, 1, 3))
+        final_from(o, n).wait_recv()
+        final_partner(o, n).start()
 
     @pl.loop(0, count)
     def _(p):
-        @pl.when(p + lead < count)
-        def _():
-            k, o = split(p + lead)
+        @pl.when(p + lead < LINE)
+        def _():
+            o = split(p + lead)
 
             @pl.when(o > 0)
             def _():
-                from_line(k, o).wait_recv()
-
-            start_line(k, o)
-
-        @pl.when(p + lead - 1 < count)
-        def _():
-            arrive_first(*split(p + lead - 1))
-
-        arrive_second(*split(p + lead - 2))
-
-        @pl.when(p == LINE - lead)
+                from_line(1, o).wait_recv()
+
+            start_line(1, o)
+
+        @pl.when(p + lead - 1 < LINE)
+        def _():
+            arrive_first(1, split(p + lead - 1))
+
+        @pl.when(p + lead - 2 < LINE)
+        def _():
+            arrive_second(1, split(p + lead - 2))
+
+        @pl.when(p >= count - late)
+        def _():
+            for e in range(2):
+                pass_final(2 * (p - count + late) + e)
+
+        @pl.when(p == heavy + calm)
         def _():
             trade_g.start()
 
@@ -913,7 +950,7 @@
             def _(n):
                 project_slice(p * project_share + n)
 
-        @pl.when((p >= heavy) & (p < rows_from))
+        @pl.when((p >= heavy) & (p < heavy + calm))
         def _():
             @pl.loop(0, attend_share)
             def _(n):
@@ -924,43 +961,36 @@
             for o in order:
                 for n in range(4):
                     from_partner(1, o, n).wait_recv()
+            for part in keep_rest[:parts]:
+                part.start()
 
         @pl.when(p >= rows_from)
         def _():
             rows_slice(p - rows_from)
 
-    for i in range(count - rows_from, row_slices):
-        rows_slice(i)
-    for part in keep_rest[:parts]:
-        part.start()
     for o in order:
         for n in range(4):
             from_partner(2, o, n).wait_recv()
     for part in keep_rest[parts:]:
         part.start()
 
-    @pl.loop(0, count)
-    def _(p):
-        k, o = split(p)
-
-        @pl.when(o > 0)
-        def _():
-            to_line(k, o).wait_send()
-
-        to_first(k, o).wait_send()
-        for n in range(2):
-            to_second(k, o, n).wait_send()
-        for n in range(4):
-            to_partner(k, o, n).wait_send()
-
-    for o in order:
-        if o > 0:
-            to_line(0, o).wait_send()
-        to_first(0, o).wait_send()
-        for n in range(2):
-            to_second(0, o, n).wait_send()
-        for n in range(4):
-            to_partner(0, o, n).wait_send()
+    for k in range(final):
+        for o in order:
+            if o > 0:
+                to_line(k, o).wait_send()
+            to_first(k, o).wait_send()
+            for n in range(2):
+                to_second(k, o, n).wait_send()
+            for n in range(4):
+                to_partner(k, o, n).wait_send()
+    to_first(final, 0).wait_send()
+    for n in range(2):
+        to_second(final, 0, n).wait_send()
+    for n in range(4):
+        to_partner(final, 0, n).wait_send()
+        for o in range(1, LINE):
+            final_line(o, n).wait_send()
+            final_partner(o, n).wait_send()
     trade.wait_send()
     trade_g.wait_send()
     arrive_g.wait_recv()
@@ -1071,7 +1101,7 @@
     place.greet()
 
     def where(k):
-        return place.corners(int(k > 0) if isinstance(k, int) else 1)
+        return place.corners(int(k == 0) if isinstance(k, int) else 0)
 
     def copy(k, o, n, src, dst, device):
         return remote(src, dst, sends, recvs, (k * LINE + o) * PER_PIECE + n, device)
@@ -1276,7 +1306,8 @@
     keep_r.start()
     t_buf[9] = small_ref[...]
     count = (chunks - 1) * LINE
-    share = parts * groups * tiles // count
+    calm = count - 2
+    share = parts * groups * tiles // calm
 
     def pass_second(p):
         stage_second(*split(p))
@@ -1289,6 +1320,18 @@
         def _():
             to_line(k, o).start()
 
+    step = 256
+    half_rows = rows // parts
+
+    def input_slice(i):
+        at_rows = pl.ds(pl.multiple_of(i * step, step), step)
+        value = base_ref[at_rows, :]
+        for t in range(parts):
+            value = value + dot_nt(dp_buf[t, at_rows, :], w_ref[t, 0, :, :wide])
+        half = lax.div(i * step, half_rows)
+        row0 = pl.multiple_of(lax.rem(i * step, half_rows), step)
+        xg_buf[half, pl.ds(row0, step), :] = value.astype(BF16)
+
     @pl.loop(0, count)
     def _(p):
         k, o = split(p)
@@ -1309,13 +1352,22 @@
         def _():
             pass_first(p - 2)
 
-        @pl.loop(0, share)
-        def _(n):
-            attend_slice(p * share + n)
-
-    small_step(0)
-    pass_second(count - 1)
-    pass_first(count - 2)
+        @pl.when(p < calm)
+        def _():
+            @pl.loop(0, share)
+            def _(n):
+                attend_slice(p * share + n)
+
+        @pl.when(p == calm)
+        def _():
+            @pl.loop(0, rows // step)
+            def _(n):
+                input_slice(n)
+
+            trade.start()
+            keep.start()
+            small_step(0)
+
     for t in range(parts):
         for m in range(0, width, GRAD_STEP):
             at = slice(m, m + GRAD_STEP)
@@ -1324,24 +1376,16 @@
             a_buf[t, at, :wide] = part.astype(BF16)
             part = dot_tn(first_ref[:, at], ctx_ref[t])
             a_buf[t, at, wide:] = part.astype(BF16)
+        for o in order:
+            for n in (2 * t, 2 * t + 1):
+                to_partner_a(o, n).start()
         small_step(1 + t)
         if t == 0:
+            pass_second(count - 1)
+            pass_first(count - 2)
+        else:
             pass_first(count - 1)
-    for o in order:
-        for n in range(4):
-            to_partner_a(o, n).start()
     small_step(3)
-
-    step = 256
-    half_rows = rows // parts
-
-    def input_slice(i):
-        at = slice(i * step, (i + 1) * step)
-        value = base_ref[at, :]
-        for t in range(parts):
-            value = value + dot_nt(dp_buf[t, at, :], w_ref[t, 0, :, :wide])
-        half, row0 = i * step // half_rows, i * step % half_rows
-        xg_buf[half, row0 : row0 + step, :] = value.astype(BF16)
 
     for i in range(LINE + 2):
         if i < LINE:
@@ -1356,11 +1400,7 @@
             stage_first(0, order[i - 2])
             if order[i - 2] > 0:
                 to_line(0, order[i - 2]).start()
-        if i < rows // step:
-            input_slice(i)
-        if i == rows // step - 1:
-            trade.start()
-            keep.start()
+        if i == 2:
             small_step(4)
     for k in (1, 2, 0):
         finish(k)

time: 334 us -> 316 us (0.946)
  Pallas kernels: 310 us -> 294 us
    pallas_call x1, Pallas kernels: 128 us -> 118 us  [gather_all(): pl.pallas_call(gather_kernel, in_specs=[local] * 9 + [anywhere], out_spec...]
    pallas_call x1, Pallas kernels: 131 us -> 125 us  [back_all(): pl.pallas_call(back_kernel, in_specs=[local] * 15 + [anywhere], out_specs...]
where the time goes in v4:
time: 316 us; the launch traced here: 315 us
  Pallas kernels  294 us (93%)
  local copies, waits for them, and re-layouts  11.2 us (4%)
  other arithmetic  8.65 us (3%)
    pallas_call x1, Pallas kernels, back_all(): pl.pallas_call(back_kernel, in_specs=[local] * 15 + [anywhere], out_specs...  125 us
    pallas_call x1, Pallas kernels, gather_all(): pl.pallas_call(gather_kernel, in_specs=[local] * 9 + [anywhere], out_spec...  118 us
    pallas_call x1, Pallas kernels, rows_pass(): pl.pallas_call(rows_kernel, grid=(rows // step,), in_specs=[row, pl.Block...  33.1 us
    pallas_call x2, Pallas kernels, outer(): pl.pallas_call(outer_kernel, grid=(parts,), in_specs=[pl.BlockSpec((rows,...  18.2 us

profile of v4, /device:TPU:0, one launch (start us, length us, event | category | flops | bytes accessed | tf_op | source)
XLA Modules:
  0.0 315.1 jit_solution(15051491303153714054)
XLA Ops:
  0.6 0.0 copy-start
  0.7 0.0 copy-start.5
  0.7 0.0 copy-start.4
  0.7 0.0 copy-start.7
  0.7 0.0 copy-start.8
  0.7 0.0 copy-start.9
  0.7 0.0 copy-start.10
  0.7 0.0 copy-start.11
  0.7 0.0 copy-start.12
  0.7 0.0 copy-start.13
  0.8 0.6 copy-done
  1.4 0.7 compare_reduce_fusion
  2.1 1.0 broadcast_in_dim.41.code_ref
  3.1 0.9 select_convert_fusion.bars_ref
  4.0 0.9 fusion.docs_ref
  4.9 0.6 fusion.2.seg_ref
  5.5 0.8 slice_bitcast_fusion.9
  6.3 0.8 maximum_bitcast_fusion
  7.1 0.0 copy-done.5
  7.1 0.0 copy-done.4
  7.1 0.8 pad_maximum_fusion.shard_ref
  7.9 0.0 copy-done.7
  8.0 0.6 broadcast_in_dim.39.bias_ref
  8.6 0.0 copy-done.8
  8.6 0.0 copy-done.9
  8.7 0.0 copy-done.10
  8.7 0.0 copy-done.11
  8.7 0.0 copy-done.12
  8.7 0.0 copy-done.13
  8.8 0.6 stack.68.vec_ref
  9.4 117.7 %gather_all.1 = (bf16[2,4,2,2,48,1536]{5,4,3,2,1,0:T(8,128)(2,1)}, bf16[2,2,4,2,2,48,1536]{6,5,4,3,2,1,0:T(8,128)(2,1)}, bf16[2,512,768]{2,1,0:T(8,128)(2,1)}, b...) custom-call(bf16[3,48,1536]{2,1,0:T(8,128)(2,1)} %pad_maximum_fusion, ...), custom_call_target="tpu_custom_call" | custom-call | tf_op jit(solution)/shard_map/gather_all/pallas_call | solution.py:1016
  127.1 33.1 %rows_pass.1 = (bf16[1024,768]{1,0:T(8,128)(2,1)}, bf16[1024,768]{1,0:T(8,128)(2,1)}, bf16[1024,768]{1,0:T(8,128)(2,1)}, bf16[1024,768]{1,0:T(8,128)(2,1)}, f32[...) custom-call(f32[1024,768]{1,0:T(8,128)} %get-tuple-element.38.normed, ...), custom_call_target="tpu_custom_call" | custom-call | tf_op jit(solution)/shard_map/rows_pass/pallas_call | solution.py:426
  160.2 0.7 reshape.104
  161.0 1.3 maximum_bitcast_fusion.1.small_ref
  162.3 9.0 %outer.3 = bf16[2,768,1536]{2,1,0:T(8,128)(2,1)} custom-call(bf16[1024,768]{1,0:T(8,128)(2,1)} %get-tuple-element.47.rows_ref, bf16[2,1024,1536]{2,1,0:T(8,128)(2,1)} %get-tuple-element.40.act_ref.cols_ref), custom_call_target="tpu_custom_call" | custom-call | tf_op jit(solution)/shard_map/outer/pallas_call | solution.py:482
  171.4 9.1 %outer.2 = bf16[2,768,1536]{2,1,0:T(8,128)(2,1)} custom-call(bf16[1024,768]{1,0:T(8,128)(2,1)} %get-tuple-element.45.rows_ref, bf16[2,1024,1536]{2,1,0:T(8,128)(2,1)} %get-tuple-element.46.cols_ref), custom_call_target="tpu_custom_call" | custom-call | tf_op jit(solution)/shard_map/outer/pallas_call | solution.py:482
  180.5 125.4 %back_all.1 = (f32[3,48,1536]{2,1,0:T(8,128)}, bf16[2,512,768]{2,1,0:T(8,128)(2,1)}, bf16[2,512,768]{2,1,0:T(8,128)(2,1)}, f32[72,128]{1,0:T(8,128)}) custom-call(bf16[2,4,2,2,48,1536]{5,4,3,2,1,0:T(8,128)(2,1)} %bitcast.73, bf16[2,4,2,2,48,1536]{5,4,3,2,1,0:T(8,128)(2,1)} %bitcast.72, bf16[1024,768]{1,0:T(8,128)(2,1)} %bitcast.74, ...), custom_call_target="tpu_custom_call" | custom-call | tf_op jit(solution)/shard_map/back_all/pallas_call | solution.py:1461
  305.9 0.0 copy-start.3
  305.9 0.9 fusion.1
  306.8 0.6 pad_maximum_fusion.3
  307.4 2.0 slice_bitcast_fusion
  309.4 0.7 slice_bitcast_fusion.3
  310.1 0.7 pad_maximum_fusion.1
  310.8 1.9 bitcast_convert_fusion
  312.7 0.6 slice_bitcast_fusion.10
  313.3 0.7 dynamic_slice.23
  314.0 1.1 copy.33
  315.1 0.0 copy-done.1
  (24 shorter events, 0.1 us)
Async XLA Ops:
  0.6 0.7 copy-start
  0.7 6.4 %copy-start.5 = (bf16[48,1536]{1,0:T(8,128)(2,1)S(1)}, bf16[48,1536]{1,0:T(8,128)(2,1)}, u32[]{:S(2)}) copy-start(bf16[48,1536]{1,0:T(8,128)(2,1)} %param.25) | copy-start | bytes 442372
  0.7 6.4 %copy-start.4 = (bf16[1536,48]{0,1:T(8,128)(2,1)S(1)}, bf16[1536,48]{0,1:T(8,128)(2,1)}, u32[]{:S(2)}) copy-start(bf16[1536,48]{0,1:T(8,128)(2,1)} %param.27) | copy-start | bytes 442372
  0.7 7.2 %copy-start.7 = (f32[2,768]{1,0:T(2,128)S(1)}, f32[2,768]{1,0:T(2,128)}, u32[]{:S(2)}) copy-start(f32[2,768]{1,0:T(2,128)} %param.20) | copy-start | bytes 18436
  0.7 7.9 %copy-start.8 = (f32[768]{0:T(1024)S(1)}, f32[768]{0:T(1024)}, u32[]{:S(2)}) copy-start(f32[768]{0:T(1024)} %param.22) | copy-start | bytes 9220
  0.7 7.9 %copy-start.9 = (f32[768]{0:T(1024)S(1)}, f32[768]{0:T(1024)}, u32[]{:S(2)}) copy-start(f32[768]{0:T(1024)} %param.23) | copy-start | bytes 9220
  0.7 7.9 %copy-start.10 = (f32[768]{0:T(1024)S(1)}, f32[768]{0:T(1024)}, u32[]{:S(2)}) copy-start(f32[768]{0:T(1024)} %param.24) | copy-start | bytes 9220
  0.7 8.0 %copy-start.11 = (f32[768]{0:T(1024)S(1)}, f32[768]{0:T(1024)}, u32[]{:S(2)}) copy-start(f32[768]{0:T(1024)} %param.28) | copy-start | bytes 9220
  0.7 8.0 %copy-start.12 = (f32[768]{0:T(1024)S(1)}, f32[768]{0:T(1024)}, u32[]{:S(2)}) copy-start(f32[768]{0:T(1024)} %param.29) | copy-start | bytes 9220
  0.7 8.0 %copy-start.13 = (f32[768]{0:T(1024)S(1)}, f32[768]{0:T(1024)}, u32[]{:S(2)}) copy-start(f32[768]{0:T(1024)} %param.30) | copy-start | bytes 9220
  305.9 4.9 %copy-start.3 = (bf16[2,512,768]{2,1,0:T(8,128)(2,1)S(1)}, bf16[2,512,768]{2,1,0:T(8,128)(2,1)}, u32[]{:S(2)}) copy-start(bf16[2,512,768]{2,1,0:T(8,128)(2,1)} %get-tuple-element.59) | copy-start | bytes 4718596
  310.8 1.9 copy-start.6
  310.8 3.2 %copy-start.2 = (bf16[2,512,768]{2,1,0:T(8,128)(2,1)S(1)}, bf16[2,512,768]{2,1,0:T(8,128)(2,1)}, u32[]{:S(2)}) copy-start(bf16[2,512,768]{2,1,0:T(8,128)(2,1)} %get-tuple-element.58) | copy-start | bytes 4718596
  313.3 1.8 copy-start.1
